TPU v7x, 128 devices: a whole 4x4x4 slice. The times are simulated.
128 devices in a mesh: fsdp: 32 (over z, y, core), seq: 4 (over x).
Axes of the slice: x: 4, y: 4, z: 4, core: 2. Of those that a mesh axis runs over, the one named last changes fastest.
Arguments:
- tokens: bfloat16 [32, 512, 4096], P('fsdp'), may hold values from -7 to 7
- norm_gain: float32 [4096], replicated, may hold values from 0.1 to 1.9
- curvature: bfloat16 [32, 512, 4096], P('fsdp'), may hold values from 0.19921875 to 2
- weight_slots: bfloat16 [4, 384, 128, 128], P('seq', 'fsdp'), may hold values from -1 to 1
- probe_slots: bfloat16 [4, 384, 128, 128], P('seq', 'fsdp'), may hold values from -0.09375 to 0.09375
- block_counts: int32 [4, 32], P('seq'), may hold values from 1 to 12, 320 in all within a row
Outputs:
- hvp_slots: float32 [4, 384, 128, 128], P('seq', 'fsdp')
Inputs may be any that keep to these rules, and one draw needn't show every extreme that they name: `block_counts`: in each row, device d along fsdp owns the n_d blocks that follow the earlier devices' blocks, in its first n_d slots; a row sums to 320, and 12 is reached in every row.
All inputs are finite; a program needn't handle non-finite values.
Results may differ from a plain program's by a relative error of at most 0.018.
Values may be sent and summed in bfloat16 or wider, within the bound.
A program may use at most 128 MiB of HBM per device.

v0:
```python
import jax
import jax.numpy as jnp
from jax import lax
from jax.sharding import PartitionSpec as P

D = 4096
HQ = 16
HK = 4
HD = 128
BLK = 128


THETA = 500000.0
EPS = 1e-05
NEGATIVE = -1e30


def rotary(length, head_dim):
    half_dim = head_dim // 2
    frequency = jnp.exp(-jnp.log(THETA) * 2.0 * jnp.arange(half_dim, dtype=jnp.float32) / head_dim)
    angles = jnp.arange(length, dtype=jnp.float32)[:, None] * frequency[None, :]
    return (jnp.cos(angles)[:, None, :], jnp.sin(angles)[:, None, :])


def rotate(field_in, cosine, sine):
    half_dim = field_in.shape[-1] // 2
    first_half = field_in[..., :half_dim]
    second = field_in[..., half_dim:]
    return jnp.concatenate(
        [first_half * cosine - second * sine, second * cosine + first_half * sine], axis=-1
    )


def attention_branch(w_qkv, w_out, normed, cosine, sine, q_heads, kv_heads):
    length = normed.shape[0]
    head_dim = w_out.shape[0] // q_heads
    projected = jnp.dot(normed, w_qkv, preferred_element_type=jnp.float32)
    q_end = q_heads * head_dim
    k_end = q_end + kv_heads * head_dim
    queries = rotate(projected[:, :q_end].reshape(length, q_heads, head_dim), cosine, sine).astype(
        jnp.bfloat16
    )
    key_rows = rotate(
        projected[:, q_end:k_end].reshape(length, kv_heads, head_dim), cosine, sine
    ).astype(jnp.bfloat16)
    values = projected[:, k_end:].reshape(length, kv_heads, head_dim).astype(jnp.bfloat16)
    queries = queries.reshape(length, kv_heads, q_heads // kv_heads, head_dim)
    scores = jnp.einsum(
        "qkgd,skd->kgqs", queries, key_rows, preferred_element_type=jnp.float32
    ) * head_dim ** (-0.5)
    causal = jnp.arange(length)[:, None] >= jnp.arange(length)[None, :]
    scores = jnp.where(causal, scores, NEGATIVE)
    attn_probs = jax.nn.softmax(scores, axis=-1).astype(jnp.bfloat16)
    mixed_heads = jnp.einsum(
        "kgqs,skd->qkgd", attn_probs, values, preferred_element_type=jnp.float32
    )
    mixed_heads = mixed_heads.reshape(length, q_heads * head_dim).astype(jnp.bfloat16)
    return jnp.dot(mixed_heads, w_out, preferred_element_type=jnp.float32)


def to_matrix(blocks, row_blocks, col_blocks):
    blk_edge = blocks.shape[-1]
    return (
        blocks.reshape(row_blocks, col_blocks, blk_edge, blk_edge)
        .transpose(0, 2, 1, 3)
        .reshape(row_blocks * blk_edge, col_blocks * blk_edge)
    )


def to_blocks(matrix, blk_edge):
    row_blocks = matrix.shape[0] // blk_edge
    col_blocks = matrix.shape[1] // blk_edge
    return (
        matrix.reshape(row_blocks, blk_edge, col_blocks, blk_edge)
        .transpose(0, 2, 1, 3)
        .reshape(row_blocks * col_blocks, blk_edge, blk_edge)
    )


def local(tokens, norm_gain, curvature, weight_slots, probe_slots, block_counts):
    n_columns = lax.axis_size("seq")
    n_owners = lax.axis_size("fsdp")
    q_heads = HQ // n_columns
    kv_heads = HK // n_columns
    row_blocks = D // BLK
    qkv_cols = (q_heads + 2 * kv_heads) * HD // BLK
    out_rows = q_heads * HD // BLK
    qkv_split = row_blocks * qkv_cols
    total_blocks = qkv_split + out_rows * row_blocks
    slots = weight_slots.shape[1]
    length = tokens.shape[1]
    counts = block_counts[0]
    range_ends = jnp.cumsum(counts)
    starts = range_ends - counts
    owner_ids = jnp.arange(n_owners, dtype=jnp.int32)
    gathered_w, gathered_p = (
        lax.all_gather(weight_slots[0], "fsdp", axis=0, tiled=True),
        lax.all_gather(probe_slots[0], "fsdp", axis=0, tiled=True),
    )
    block_ids = jnp.arange(total_blocks, dtype=jnp.int32)
    owners = jnp.sum((range_ends[None, :] <= block_ids[:, None]).astype(jnp.int32), axis=1)
    first_block = jnp.sum(
        jnp.where(owners[:, None] == owner_ids[None, :], starts[None, :], 0), axis=1
    )
    slot_of = owners * slots + block_ids - first_block
    w_blocks = gathered_w[slot_of]
    p_blocks = gathered_p[slot_of]
    w_qkv = to_matrix(w_blocks[:qkv_split], row_blocks, qkv_cols)
    w_out = to_matrix(w_blocks[qkv_split:], out_rows, row_blocks)
    p_qkv = to_matrix(p_blocks[:qkv_split], row_blocks, qkv_cols)
    p_out = to_matrix(p_blocks[qkv_split:], out_rows, row_blocks)
    values = tokens[0].astype(jnp.float32)
    factor = lax.rsqrt(jnp.mean(values * values, axis=-1, keepdims=True) + EPS)
    normed = (values * factor * norm_gain).astype(jnp.bfloat16)
    cosine, sine = rotary(length, HD)

    def inner(first_w, second_w):
        return attention_branch(first_w, second_w, normed, cosine, sine, q_heads, kv_heads)

    _, tangent = jax.jvp(inner, (w_qkv, w_out), (p_qkv, p_out))
    summed = lax.psum(tangent.astype(jnp.bfloat16), "seq").astype(jnp.float32)
    weighted = (curvature[0].astype(jnp.float32) * summed).astype(jnp.bfloat16)
    _, pullback = jax.vjp(inner, w_qkv, w_out)
    g_qkv, g_out = pullback(weighted.astype(jnp.float32))
    grad_blocks = jnp.concatenate([to_blocks(g_qkv, BLK), to_blocks(g_out, BLK)], axis=0)
    slot_index = jnp.arange(lax.axis_size("fsdp") * slots, dtype=jnp.int32)
    slot_owner = slot_index // slots
    slot_place = slot_index % slots
    owner_hot = slot_owner[:, None] == owner_ids[None, :]
    owner_first = jnp.sum(jnp.where(owner_hot, starts[None, :], 0), axis=1)
    own_count = jnp.sum(jnp.where(owner_hot, counts[None, :], 0), axis=1)
    is_live = slot_place < own_count
    picked = jnp.clip(owner_first + slot_place, 0, total_blocks - 1)
    summed_slots = lax.psum_scatter(
        jnp.where(is_live[:, None, None], grad_blocks[picked].astype(jnp.float32), 0.0).astype(
            jnp.bfloat16
        ),
        "fsdp",
        scatter_dimension=0,
        tiled=True,
    ).astype(jnp.float32)
    scaled = summed_slots * (1.0 / jnp.sqrt(jnp.float32(length * n_owners)))
    return scaled.reshape(1, slots, BLK, BLK)


def solution(mesh):
    in_specs = (
        P("fsdp", None, None),
        P(),
        P("fsdp", None, None),
        P("seq", "fsdp", None, None),
        P("seq", "fsdp", None, None),
        P("seq", None),
    )
    out_specs = P("seq", "fsdp", None, None)
    return jax.shard_map(local, mesh=mesh, in_specs=in_specs, out_specs=out_specs, check_vma=False)
```

profile of v0, /device:TPU:1, one launch (start us, length us, event | category | flops | bytes accessed | tf_op | source)
XLA Modules:
  0.0 534.9 jit_solution(1952781171609489015)
XLA Ops:
  10.5 3.1 fusion.2
  15.4 60.8 %all-gather.5.cloned.1.call-done = bf16[1,384,128,128]{3,2,0,1:T(8,128)(2,1)} async-done(((bf16[1,12,128,128]{3,2,0,1:T(8,128)(2,1)}), bf16[1,384,128,128]{3,2,0,1:T(8,128)(2,1)}) %all-gather.5.cloned.1.call-update) | async-done | bytes 12582928 | tf_op jit(solution)/shard_map/all_gather | solution.py:98
  76.2 15.2 %gather_fusion = bf16[320,128,128]{2,1,0:T(8,128)(2,1)} fusion(bf16[384,128,128]{2,1,0:T(8,128)(2,1)} %bitcast.283, s32[1024]{0:T(1024)S(1)} %pad_clamp_fusion.1), kind=kCustom, calls=%fused_computation | custom fusion | bytes 20972800 | tf_op jit(solution)/shard_map/gather | solution.py:107
  91.4 8.1 %slice.87 = bf16[192,128,128]{2,1,0:T(8,128)(2,1)} slice(bf16[320,128,128]{2,1,0:T(8,128)(2,1)} %gather_fusion), slice={[0:192], [0:128], [0:128]} | slice | bytes 12582912 | tf_op jit(solution)/shard_map/slice | solution.py:110
  99.5 41.4 %all-gather.7.cloned.1.call-done = bf16[1,384,128,128]{3,2,0,1:T(8,128)(2,1)} async-done(((bf16[1,12,128,128]{3,2,0,1:T(8,128)(2,1)}), bf16[1,384,128,128]{3,2,0,1:T(8,128)(2,1)}) %all-gather.7.cloned.1.call-update) | async-done | bytes 12582928 | tf_op jit(solution)/shard_map/all_gather | solution.py:97
  140.9 15.3 %gather_fusion.1 = bf16[320,128,128]{2,1,0:T(8,128)(2,1)} fusion(bf16[384,128,128]{2,1,0:T(8,128)(2,1)} %bitcast.284, s32[1024]{0:T(1024)S(1)} %pad_clamp_fusion.1), kind=kCustom, calls=%fused_computation.1 | custom fusion | bytes 20972800 | tf_op jit(solution)/shard_map/gather | solution.py:106
  156.1 8.1 %slice.89 = bf16[192,128,128]{2,1,0:T(8,128)(2,1)} slice(bf16[320,128,128]{2,1,0:T(8,128)(2,1)} %gather_fusion.1), slice={[0:192], [0:128], [0:128]} | slice | bytes 12582912 | tf_op jit(solution)/shard_map/slice | solution.py:108
  164.2 9.1 %copy.79 = bf16[32,6,128,128]{2,0,3,1:T(8,128)(2,1)} copy(bf16[32,6,128,128]{3,2,1,0:T(8,128)(2,1)} %bitcast.273) | data formatting | bytes 12582912 | tf_op jit(solution)/shard_map/reshape | solution.py:64
  173.3 8.4 %fusion.11 = f32[512,768]{1,0:T(8,128)S(1)} fusion(bf16[96,8,32,128]{3,2,1,0:T(8,128)(2,1)} %bitcast.287, bf16[1,512,4096]{2,1,0:T(8,128)(2,1)} %param.6, f32[4096]{0:T(1024)S(1)} %copy-done.25, f32[512]{0:T(512)S(1)} %add_rsqrt_fusion), kind=kOutput, calls=%fused_computation.21 | convolution fusion | flops 3229614080 | bytes 12077056 | tf_op jit(solution)/shard_map/jvp()/dot_general | solution.py:37
  183.0 8.9 %copy.81 = bf16[32,6,128,128]{2,0,3,1:T(8,128)(2,1)} copy(bf16[32,6,128,128]{3,2,1,0:T(8,128)(2,1)} %bitcast.274) | data formatting | bytes 12582912 | tf_op jit(solution)/shard_map/reshape | solution.py:64
  191.9 8.3 %fusion.8 = f32[512,768]{1,0:T(8,128)S(1)} fusion(bf16[96,8,32,128]{3,2,1,0:T(8,128)(2,1)} %bitcast.288, bf16[1,512,4096]{2,1,0:T(8,128)(2,1)} %param.6, f32[4096]{0:T(1024)S(1)} %copy-done.25, f32[512]{0:T(512)S(1)} %add_rsqrt_fusion), kind=kOutput, calls=%fused_computation.18 | convolution fusion | flops 3229614080 | bytes 12077056 | tf_op jit(solution)/shard_map/jvp()/dot_general | solution.py:37
  203.1 2.7 fusion.110
  212.5 2.7 copy.93
  215.2 2.7 copy.90
  218.8 2.3 fusion.137
  222.6 2.9 fusion.38
  226.9 2.5 fusion.29
  229.4 4.6 add_convert_fusion
  236.2 89.6 %all-reduce.9.cloned.1.call-done = bf16[512,4096]{1,0:T(8,128)(2,1)} async-done(((bf16[512,4096]{1,0:T(8,128)(2,1)}), bf16[512,4096]{1,0:T(8,128)(2,1)}) %all-reduce.9.cloned.1.call-update) | async-done | bytes 4194320 | tf_op jit(solution)/shard_map/psum | solution.py:121
  325.8 8.1 %fusion.59 = bf16[512,512]{0,1:T(8,128)(2,1)S(1)} fusion(bf16[64,8,32,128]{3,2,1,0:T(8,128)(2,1)} %bitcast.279, bf16[512,4096]{1,0:T(8,128)(2,1)} %all-reduce.9.cloned.1.call-done, bf16[1,512,4096]{2,1,0:T(8,128)(2,1)} %param.8), kind=kOutput, calls=%fused_computation.71 | convolution fusion | flops 2156134400 | bytes 13107200 | tf_op jit(solution)/shard_map/transpose(jvp())/dot_general | solution.py:58
  334.6 2.7 fusion.22
  337.3 2.1 fusion.91
  342.9 2.5 fusion.37
  347.0 3.6 copy.103
  353.9 5.6 %convolution_convert_fusion = bf16[4096,768]{1,0:T(8,128)(2,1)} fusion(bf16[1,512,4096]{2,1,0:T(8,128)(2,1)S(1)} %copy-done.7, f32[4096]{0:T(1024)S(1)} %copy-done.26, f32[512]{0:T(512)S(1)} %copy-done.24, f32[512,512]{1,0:T(8,128)S(1)} %copy_bitcast_fusion, f32[512,128]{1,0:T(8,128)S(1)} %add_bitcast_fusion.1, bf16[512,128]{1,0:T(8,128)(2,1)S(1)} %fusion.85), kind=kOutput, calls=%fused_computation.17 | convolution fusion | flops 3233939456 | bytes 11945984 | tf_op jit(solution)/shard_map/transpose(jvp())/dot_general | solution.py:37
  359.6 8.7 %copy.101 = bf16[4096,768]{0,1:T(8,128)(2,1)} copy(bf16[4096,768]{1,0:T(8,128)(2,1)} %convolution_convert_fusion) | data formatting | bytes 12582912 | tf_op jit(solution)/shard_map/transpose(jvp())/convert_element_type | solution.py:37
  368.3 7.5 %copy.131 = bf16[96,8,32,128]{3,2,1,0:T(8,128)(2,1)} copy(bf16[96,8,32,128]{3,1,2,0:T(8,128)(2,1)} %bitcast.275) | data formatting | bytes 12582912
  375.7 9.1 %copy.102 = bf16[32,6,128,128]{3,2,1,0:T(8,128)(2,1)} copy(bf16[32,6,128,128]{2,0,3,1:T(8,128)(2,1)} %bitcast.276) | data formatting | bytes 12582912 | tf_op jit(solution)/shard_map/transpose | solution.py:75
  384.8 11.5 %pad_maximum_fusion = bf16[320,128,128]{2,1,0:T(8,128)(2,1)} fusion(bf16[128,128,128]{2,1,0:T(8,128)(2,1)} %bitcast.280, bf16[192,128,128]{2,1,0:T(8,128)(2,1)} %bitcast.277), kind=kLoop, calls=%fused_computation.8 | loop fusion | flops 5242880 | bytes 20971520 | tf_op jit(solution)/shard_map/concatenate | solution.py:125
  396.3 15.3 %gather_fusion.2 = bf16[384,128,128]{2,1,0:T(8,128)(2,1)} fusion(bf16[320,128,128]{2,1,0:T(8,128)(2,1)} %pad_maximum_fusion, s32[1024]{0:T(1024)S(1)} %copy-done.16), kind=kCustom, calls=%fused_computation.2 | custom fusion | bytes 25167360 | tf_op jit(solution)/shard_map/gather | solution.py:135
  411.6 11.5 %select_convert_fusion = bf16[384,128,128]{2,1,0:T(8,128)(2,1)} fusion(bf16[384,128,128]{2,1,0:T(8,128)(2,1)} %gather_fusion.2, pred[384]{0:T(512)(128)(4,1)S(1)} %copy-done.21), kind=kLoop, calls=%fused_computation.3 | loop fusion | flops 18874368 | bytes 25166208 | tf_op jit(solution)/shard_map/convert_element_type | solution.py:135
  423.1 102.8 %reduce-scatter.2.cloned.1.call-done = bf16[12,128,128]{2,1,0:T(8,128)(2,1)} async-done(((bf16[384,128,128]{2,1,0:T(8,128)(2,1)}), bf16[12,128,128]{2,1,0:T(8,128)(2,1)}) %reduce-scatter.2.cloned.1.call-update) | async-done | bytes 393232 | tf_op jit(solution)/shard_map/reduce_scatter | solution.py:134
  (108 shorter events, 33.0 us)
Async XLA Ops:
  6.5 69.6 %all-gather.5.cloned.1.call-start = ((), (), s32[]{:S(2)}) async-start(), calls=%async_computation.3 | async-start | bytes 12976128 | tf_op jit(solution)/shard_map/all_gather | solution.py:98
  7.3 133.6 %all-gather.7.cloned.1.call-start = ((), (), s32[]{:S(2)}) async-start(), calls=%async_computation.4 | async-start | bytes 12976128 | tf_op jit(solution)/shard_map/all_gather | solution.py:97
  8.0 317.8 %all-reduce.9.cloned.1.call-start = ((), (), s32[]{:S(2)}) async-start(), calls=%async_computation.1 | async-start | bytes 8388608 | tf_op jit(solution)/shard_map/psum | solution.py:121
  10.4 192.7 %copy-start.19 = (f32[64]{0:T(128)}, f32[64]{0:T(128)S(1)}, u32[]{:S(2)}) copy-start(f32[64]{0:T(128)S(1)} %multiply_exponential_fusion) | copy-start | bytes 772
  13.6 178.3 %copy-start.23 = (f32[512]{0:T(512)}, f32[512]{0:T(512)S(1)}, u32[]{:S(2)}) copy-start(f32[512]{0:T(512)S(1)} %add_rsqrt_fusion) | copy-start | bytes 6148
  164.2 9.1 %copy-start.25 = (f32[4096]{0:T(1024)S(1)}, f32[4096]{0:T(1024)}, u32[]{:S(2)}) copy-start(f32[4096]{0:T(1024)} %param.7) | copy-start | bytes 49156
  181.7 1.2 copy-start.13
  200.2 2.0 copy-start.12
  205.8 12.9 %copy-start.14 = (bf16[512,64]{1,0:T(8,128)(2,1)}, bf16[512,64]{1,0:T(8,128)(2,1)S(1)}, u32[]{:S(2)}) copy-start(bf16[512,64]{1,0:T(8,128)(2,1)S(1)} %get-tuple-element.26) | copy-start | bytes 196612
  205.8 1.2 copy-start.8
  205.8 1.2 copy-start.10
  207.6 10.3 %copy-start.3 = (bf16[512,4,64]{2,0,1:T(8,128)(2,1)}, bf16[512,4,64]{2,0,1:T(8,128)(2,1)S(1)}, u32[]{:S(2)}) copy-start(bf16[512,4,64]{2,0,1:T(8,128)(2,1)S(1)} %get-tuple-element.18) | copy-start | bytes 786436
  208.8 13.7 %copy-start = (f32[512,512,4]{1,0,2:T(8,128)}, f32[512,512,4]{1,0,2:T(8,128)S(1)}, u32[]{:S(2)}) copy-start(f32[512,512,4]{1,0,2:T(8,128)S(1)} %get-tuple-element.30) | copy-start | bytes 12582916
  209.8 2.7 slice-start.1
  209.8 12.7 %copy-start.17 = (f32[4,512]{1,0:T(4,128)}, f32[4,512]{1,0:T(4,128)S(1)}, u32[]{:S(2)}) copy-start(f32[4,512]{1,0:T(4,128)S(1)} %multiply_divide_fusion) | copy-start | bytes 24580
  212.5 2.7 slice-start
  217.9 8.9 %copy-start.2 = (bf16[4,32,128,128]{3,1,2,0:T(8,128)(2,1)}, bf16[4,32,128,128]{3,1,2,0:T(8,128)(2,1)S(1)}, u32[]{:S(2)}) copy-start(bf16[4,32,128,128]{3,1,2,0:T(8,128)(2,1)S(1)} %copy.90) | copy-start | bytes 12582916
  234.0 291.9 %reduce-scatter.2.cloned.1.call-start = ((), (), s32[]{:S(2)}) async-start(), calls=%async_computation.2 | async-start | bytes 12976128 | tf_op jit(solution)/shard_map/reduce_scatter | solution.py:134
  325.8 8.8 %copy-start.1 = (f32[512,512,4]{1,0,2:T(8,128)S(1)}, f32[512,512,4]{1,0,2:T(8,128)}, u32[]{:S(2)}) copy-start(f32[512,512,4]{1,0,2:T(8,128)} %copy-done) | copy-start | bytes 12582916
  325.8 8.8 %copy-start.18 = (f32[4,512]{1,0:T(4,128)S(1)}, f32[4,512]{1,0:T(4,128)}, u32[]{:S(2)}) copy-start(f32[4,512]{1,0:T(4,128)} %copy-done.17) | copy-start | bytes 24580
  334.6 2.7 copy-start.4
  337.3 2.2 copy-start.15
  339.4 2.2 copy-start.5
  339.5 3.5 copy-start.6
  346.9 3.7 copy-start.20
  346.9 4.8 copy-start.9
  347.0 4.8 copy-start.11
  351.7 2.2 copy-start.7
  351.7 2.2 copy-start.24
  351.8 2.2 copy-start.26
  384.8 11.5 %copy-start.16 = (s32[1024]{0:T(1024)S(1)}, s32[1024]{0:T(1024)}, u32[]{:S(2)}) copy-start(s32[1024]{0:T(1024)} %pad_clamp_fusion) | copy-start | bytes 12292
  396.3 15.3 %copy-start.21 = (pred[384]{0:T(512)(128)(4,1)S(1)}, pred[384]{0:T(512)(128)(4,1)}, u32[]{:S(2)}) copy-start(pred[384]{0:T(512)(128)(4,1)} %fusion.112) | copy-start | bytes 1156
  (1 other events, 0.5 us)
Sparse Core Ops, SparseCore 0:
  9.6 66.5 all-gather.4
  78.4 62.3 all-gather.6
  234.2 91.5 all-reduce.8
  423.3 102.6 reduce-scatter.1
where the time goes:
time: 545 us; the launch traced here: 535 us
  waiting for transfers between devices  296 us (54%)
  local copies, waits for them, and re-layouts  127 us (23%)
  matrix products  57.7 us (11%)
  other arithmetic  40 us (7%)
  between operations  14.1 us (3%)
    reduce_scatter x1, waiting for transfers between devices, local(): lax.psum_scatter(jnp.where(is_live[:, None, None], grad_blocks[picked].as...  103 us
    psum x1, waiting for transfers between devices, local(): summed = lax.psum(tangent.astype(jnp.bfloat16), 'seq').astype(jnp.float32)  89.6 us
    all_gather x1, waiting for transfers between devices, local(): lax.all_gather(probe_slots[0], 'fsdp', axis=0, tiled=True)  60.8 us
    all_gather x1, waiting for transfers between devices, local(): lax.all_gather(weight_slots[0], 'fsdp', axis=0, tiled=True)  41.4 us
    reshape x4, local copies, waits for them, and re-layouts, to_matrix(): blocks.reshape(row_blocks, col_blocks, blk_edge, blk_edge)  23.4 us
    dot_general x3, matrix products, attention_branch(): projected = jnp.dot(normed, w_qkv, preferred_element_type=jnp.float32)  22.3 us
    dot_general x4, matrix products, attention_branch(): return jnp.dot(mixed_heads, w_out, preferred_element_type=jnp.float32)  17.7 us
    gather x1, local copies, waits for them, and re-layouts, local(): grad_blocks[picked].astype(jnp.float32)  15.3 us
  transfers between devices with their start and end apart: 4, of which 4 were waited for; matrix products, arithmetic and copies ran while one was open for 6% of the time, Pallas kernels for 0%

commit v1 on v0

v1 whole, which is shorter than its diff:
```python
import functools

import jax
import jax.numpy as jnp
import numpy as np
from jax import lax
from jax.experimental import pallas as pl
from jax.experimental.pallas import tpu as pltpu
from jax.sharding import PartitionSpec as P

D = 4096
HD = 128
BLK = 128
LEN = 512
QH = 4
QKV = 768
OUT = 512
NQKV = 192
NB = 320
SLOTS = 12
HALF = 6
THETA = 500000.0
EPS = 1e-05
NEGATIVE = -1e30
VMEM_LIMIT = 66_000_000
MESH = pl.DeviceIdType.MESH
F32 = jnp.float32
BF16 = jnp.bfloat16


def tables():
    half = HD // 2
    frequency = np.exp(-np.log(THETA) * 2.0 * np.arange(half) / HD)
    angles = np.arange(LEN)[:, None] * frequency[None, :]
    c, s = np.cos(angles), np.sin(angles)
    return (
        np.concatenate([c, c], axis=1).astype(np.float32),
        np.concatenate([-s, s], axis=1).astype(np.float32),
    )


def place():
    me = lax.axis_index("fsdp")
    core = lax.rem(me, 2)
    y = lax.rem(me // 2, 4)
    z = me // 8
    return me, core, y, z


def index_of(z, y, core):
    return (z * 4 + y) * 2 + core


def wrap(a):
    return lax.rem(a + 4, 4)


def greet(targets):
    barrier = pltpu.get_barrier_semaphore()
    for t in targets:
        pl.semaphore_signal(barrier, inc=1, device_id=t, device_id_type=MESH)
    pl.semaphore_wait(barrier, len(targets))


def gather_kernel(w_ref, p_ref, out_ref, send_sem, recv_sem, local_sem):
    me, core, y, z = place()
    sib = index_of(z, y, 1 - core)

    def at(axis, step):
        if axis == "y":
            return {"fsdp": index_of(z, wrap(y + step), core)}
        return {"fsdp": index_of(wrap(z + step), y, core)}

    greet([at("y", 1), at("y", -1), at("z", 1), at("z", -1), {"fsdp": sib}])

    own = [
        pltpu.make_async_copy(w_ref, out_ref.at[me, 0], local_sem.at[0]),
        pltpu.make_async_copy(p_ref, out_ref.at[me, 1], local_sem.at[1]),
    ]
    for c in own:
        c.start()

    counter = [0]
    sends = []

    def sem():
        counter[0] += 1
        return counter[0] - 1

    def send(src, dst, number, target):
        copy = pltpu.make_async_remote_copy(
            src_ref=src,
            dst_ref=dst,
            send_sem=send_sem.at[number],
            recv_sem=recv_sem.at[number],
            device_id=target,
            device_id_type=MESH,
        )
        copy.start()
        sends.append(copy)
        return copy

    def piece(tensor, origin, part=None):
        if part is None:
            return out_ref.at[origin, tensor]
        return out_ref.at[origin, tensor, pl.ds(part * HALF, HALF)]

    first = ("y", "z")
    second = ("z", "y")

    def origin_of(tensor, f, s):
        if tensor == 0:
            return index_of(wrap(z + s), wrap(y + f), core)
        return index_of(wrap(z + f), wrap(y + s), core)

    number = {}
    for tensor in (0, 1):
        for role in ("f+", "f-", "fa", "fb"):
            number[tensor, role] = sem()
        for f in (0, 1, -1, 2):
            for role in ("s+", "s-", "sa", "sb"):
                number[tensor, role, f] = sem()
        for f in (0, 1, -1, 2):
            for s in (0, 1, -1, 2):
                number[tensor, "sib", f, s] = sem()

    arrivals = {}

    def go(tensor, role, src_origin, axis, step, part=None, src=None):
        ref = piece(tensor, src_origin, part)
        copy = send(ref if src is None else src, ref, number[(tensor,) + role], at(axis, step))
        arrivals[(tensor,) + role] = copy

    def to_sib(tensor, f, s, src=None):
        origin = origin_of(tensor, f, s)
        ref = piece(tensor, origin)
        copy = send(ref if src is None else src, ref, number[tensor, "sib", f, s], {"fsdp": sib})
        arrivals[tensor, "sib", f, s] = copy

    mine = (w_ref, p_ref)
    for tensor in (0, 1):
        go(tensor, ("f+",), me, first[tensor], 1, src=mine[tensor])
        go(tensor, ("f-",), me, first[tensor], -1, src=mine[tensor])
    for tensor in (0, 1):
        go(tensor, ("s+", 0), me, second[tensor], 1, src=mine[tensor])
        go(tensor, ("s-", 0), me, second[tensor], -1, src=mine[tensor])
    for tensor in (0, 1):
        to_sib(tensor, 0, 0, src=mine[tensor])

    for tensor in (0, 1):
        arrivals[tensor, "f+"].wait_recv()
        lower = origin_of(tensor, -1, 0)
        go(tensor, ("fa",), lower, first[tensor], 1, part=0)
        go(tensor, ("s+", -1), lower, second[tensor], 1)
        go(tensor, ("s-", -1), lower, second[tensor], -1)
        arrivals[tensor, "f-"].wait_recv()
        upper = origin_of(tensor, 1, 0)
        go(tensor, ("fb",), upper, first[tensor], -1, part=1)
        go(tensor, ("s+", 1), upper, second[tensor], 1)
        go(tensor, ("s-", 1), upper, second[tensor], -1)
        to_sib(tensor, -1, 0)
        to_sib(tensor, 1, 0)

    def pass_on(tensor, f):
        arrivals[tensor, "s+", f].wait_recv()
        go(tensor, ("sa", f), origin_of(tensor, f, -1), second[tensor], 1, part=0)
        to_sib(tensor, f, -1)
        arrivals[tensor, "s-", f].wait_recv()
        go(tensor, ("sb", f), origin_of(tensor, f, 1), second[tensor], -1, part=1)
        to_sib(tensor, f, 1)

    for tensor in (0, 1):
        pass_on(tensor, 0)
    for tensor in (0, 1):
        arrivals[tensor, "fa"].wait_recv()
        arrivals[tensor, "fb"].wait_recv()
        far = origin_of(tensor, 2, 0)
        go(tensor, ("s+", 2), far, second[tensor], 1)
        go(tensor, ("s-", 2), far, second[tensor], -1)
        to_sib(tensor, 2, 0)
    for f in (-1, 1, 2):
        for tensor in (0, 1):
            pass_on(tensor, f)
            if f == -1:
                g = 0
            elif f == 1:
                g = -1
            else:
                g = 1
            arrivals[tensor, "sa", g].wait_recv()
            arrivals[tensor, "sb", g].wait_recv()
            to_sib(tensor, g, 2)
    for tensor in (0, 1):
        arrivals[tensor, "sa", 2].wait_recv()
        arrivals[tensor, "sb", 2].wait_recv()
        to_sib(tensor, 2, 2)
    for key, copy in arrivals.items():
        if key[1] == "sib":
            copy.wait_recv()
    for c in own:
        c.wait()
    for copy in sends:
        copy.wait_send()


def gather(w, p):
    vmem = pl.BlockSpec(memory_space=pltpu.VMEM)
    return pl.pallas_call(
        gather_kernel,
        out_shape=jax.ShapeDtypeStruct((32, 2, SLOTS, BLK, BLK), BF16),
        in_specs=[vmem, vmem],
        out_specs=pl.BlockSpec(memory_space=pl.ANY),
        scratch_shapes=[
            pltpu.SemaphoreType.DMA((72,)),
            pltpu.SemaphoreType.DMA((72,)),
            pltpu.SemaphoreType.DMA((2,)),
        ],
        compiler_params=pltpu.CompilerParams(collective_id=0, has_side_effects=True),
        name="gather",
    )(w, p)


def nt(a, b):
    return lax.dot_general(a, b, (((1,), (1,)), ((), ())), preferred_element_type=F32)


def nn(a, b):
    return jnp.dot(a, b, preferred_element_type=F32)


def causal_mask():
    row = lax.broadcasted_iota(jnp.int32, (LEN, LEN), 0)
    col = lax.broadcasted_iota(jnp.int32, (LEN, LEN), 1)
    return row >= col


def forward_kernel(
    counts,
    tokens,
    gain,
    cos,
    sin,
    slots,
    tan_out,
    normed_out,
    qkv_out,
    mixed_out,
    probs_out,
    wo_out,
    normed,
    wqkv,
    wout,
    proj,
    sides,
    probs,
    qkv,
    sem,
):
    def device(d, start):
        n = counts[d]

        def one(t, carry):
            b = start + t

            @pl.when(b < NQKV)
            def _():
                r = pl.multiple_of((b // 6) * BLK, BLK)
                c = pl.multiple_of((b % 6) * BLK, BLK)
                pltpu.make_async_copy(
                    slots.at[d, :, t], wqkv.at[:, pl.ds(r, BLK), pl.ds(c, BLK)], sem.at[0]
                ).start()

            @pl.when(b >= NQKV)
            def _():
                e = b - NQKV
                r = pl.multiple_of((e // 32) * BLK, BLK)
                c = pl.multiple_of((e % 32) * BLK, BLK)
                pltpu.make_async_copy(
                    slots.at[d, :, t], wout.at[:, pl.ds(r, BLK), pl.ds(c, BLK)], sem.at[1]
                ).start()

            return carry

        lax.fori_loop(0, n, one, 0)
        return start + n

    lax.fori_loop(0, 32, device, 0)

    def norm(i, carry):
        rows = pl.ds(pl.multiple_of(i * 32, 32), 32)
        x = tokens[rows, :].astype(F32)
        factor = lax.rsqrt(jnp.mean(x * x, axis=-1, keepdims=True) + EPS)
        normed[rows, :] = (x * factor * gain[...]).astype(BF16)
        return carry

    lax.fori_loop(0, LEN // 32, norm, 0)
    save_normed = pltpu.make_async_copy(normed, normed_out, sem.at[2])
    save_normed.start()
    pltpu.make_async_copy(wqkv, wqkv, sem.at[0]).wait()

    for tensor in (0, 1):
        for n in range(3):
            cols = slice(n * 256, (n + 1) * 256)
            proj[tensor, :, cols] = nn(normed[...], wqkv[tensor, :, cols])

    c2, s2 = cos[...], sin[...]

    def rot(x):
        return x * c2 + pltpu.roll(x, 64, 1) * s2

    def head(tensor, h):
        x = proj[tensor, :, h * HD : (h + 1) * HD]
        if h < QH + 1:
            x = rot(x)
        return x.astype(BF16)

    for h in range(QH + 2):
        qkv[:, h * HD : (h + 1) * HD] = head(0, h)
    save_qkv = pltpu.make_async_copy(qkv, qkv_out, sem.at[3])
    save_qkv.start()
    k = qkv[:, QH * HD : (QH + 1) * HD]
    v = qkv[:, (QH + 1) * HD :]
    keys = jnp.concatenate([k, head(1, QH)], axis=1)
    values = jnp.concatenate([v, head(1, QH + 1)], axis=1)
    causal = causal_mask()
    scale = HD**-0.5
    for h in range(QH):
        q = qkv[:, h * HD : (h + 1) * HD]
        tq = head(1, h)
        s = jnp.where(causal, nt(q, k) * scale, NEGATIVE)
        m = jnp.max(s, axis=-1, keepdims=True)
        e = jnp.exp(s - m)
        p = e * (1.0 / jnp.sum(e, axis=-1, keepdims=True))
        ts = nt(jnp.concatenate([tq, q], axis=1), keys) * scale
        pt = p * ts
        tp = pt - p * jnp.sum(pt, axis=-1, keepdims=True)
        pb = p.astype(BF16)
        probs[h] = pb
        both = nn(pb, values)
        mixed_t = nn(tp.astype(BF16), v) + both[:, HD:]
        sides[0, :, h * HD : (h + 1) * HD] = mixed_t.astype(BF16)
        sides[1, :, h * HD : (h + 1) * HD] = both[:, :HD].astype(BF16)
    save_probs = pltpu.make_async_copy(probs, probs_out, sem.at[4])
    save_probs.start()
    save_mixed = pltpu.make_async_copy(sides.at[1], mixed_out, sem.at[5])
    save_mixed.start()
    pltpu.make_async_copy(wout, wout, sem.at[1]).wait()
    save_wo = pltpu.make_async_copy(wout.at[0], wo_out, sem.at[6])
    save_wo.start()
    for n in range(8):
        cols = slice(n * 512, (n + 1) * 512)
        tan_out[:, cols] = (
            nn(sides[0], wout[0, :, cols]) + nn(sides[1], wout[1, :, cols])
        ).astype(BF16)
    for c in (save_normed, save_qkv, save_probs, save_mixed, save_wo):
        c.wait()


def forward(counts, tokens, gain, cos, sin, slots):
    vmem = pl.BlockSpec(memory_space=pltpu.VMEM)
    hbm = pl.BlockSpec(memory_space=pl.ANY)
    smem = pl.BlockSpec(memory_space=pltpu.SMEM)
    shape = jax.ShapeDtypeStruct
    return pl.pallas_call(
        forward_kernel,
        out_shape=[
            shape((LEN, D), BF16),
            shape((LEN, D), BF16),
            shape((LEN, QKV), BF16),
            shape((LEN, OUT), BF16),
            shape((QH, LEN, LEN), BF16),
            shape((OUT, D), BF16),
        ],
        in_specs=[smem, vmem, vmem, vmem, vmem, hbm],
        out_specs=[vmem, hbm, hbm, hbm, hbm, hbm],
        scratch_shapes=[
            pltpu.VMEM((LEN, D), BF16),
            pltpu.VMEM((2, D, QKV), BF16),
            pltpu.VMEM((2, OUT, D), BF16),
            pltpu.VMEM((2, LEN, QKV), F32),
            pltpu.VMEM((2, LEN, OUT), BF16),
            pltpu.VMEM((QH, LEN, LEN), BF16),
            pltpu.VMEM((LEN, QKV), BF16),
            pltpu.SemaphoreType.DMA((7,)),
        ],
        compiler_params=pltpu.CompilerParams(vmem_limit_bytes=VMEM_LIMIT),
        name="forward",
    )(counts, tokens, gain, cos, sin, slots)


def exchange_kernel(tan, curv, out, cbuf, opp_a, opp_b, low, high, send_sem, recv_sem, sem):
    me = lax.axis_index("seq")
    rows = LEN // 4
    half = rows // 2
    up, down = {"seq": wrap(me + 1)}, {"seq": wrap(me - 1)}
    greet([up, down])
    get = pltpu.make_async_copy(
        curv.at[pl.ds(pl.multiple_of(me * rows, rows), rows)], cbuf, sem.at[0]
    )
    get.start()

    def span(chunk, part=None):
        if part is None:
            return pl.ds(pl.multiple_of(chunk * rows, rows), rows)
        return pl.ds(pl.multiple_of(chunk * rows + part * half, half), half)

    sends = []

    def send(src, dst, number, target):
        copy = pltpu.make_async_remote_copy(
            src_ref=src,
            dst_ref=dst,
            send_sem=send_sem.at[number],
            recv_sem=recv_sem.at[number],
            device_id=target,
            device_id_type=MESH,
        )
        copy.start()
        sends.append(copy)
        return copy

    far = wrap(me + 2)
    nxt, prv = wrap(me + 1), wrap(me - 1)
    a0 = send(tan.at[span(far, 0)], opp_a, 0, up)
    b0 = send(tan.at[span(far, 1)], opp_b, 1, down)
    a1 = send(tan.at[span(nxt, 1)], low.at[1], 2, up)
    b1 = send(tan.at[span(prv, 0)], high.at[0], 3, down)
    a0.wait_recv()
    opp_a[...] = (opp_a[...].astype(F32) + tan[span(nxt, 0), :].astype(F32)).astype(BF16)
    a2 = send(opp_a, low.at[0], 4, up)
    b0.wait_recv()
    opp_b[...] = (opp_b[...].astype(F32) + tan[span(prv, 1), :].astype(F32)).astype(BF16)
    b2 = send(opp_b, high.at[1], 5, down)
    get.wait()

    def finish(part):
        total = (
            tan[span(me, part), :].astype(F32)
            + low[part].astype(F32)
            + high[part].astype(F32)
        )
        c = cbuf[pl.ds(part * half, half), :].astype(F32)
        out[span(me, part), :] = (total * c).astype(BF16)

    a1.wait_recv()
    b2.wait_recv()
    finish(1)
    c1 = send(out.at[span(me, 1)], out.at[span(me, 1)], 6, up)
    d1 = send(out.at[span(me, 1)], out.at[span(me, 1)], 7, down)
    a2.wait_recv()
    b1.wait_recv()
    finish(0)
    c0 = send(out.at[span(me, 0)], out.at[span(me, 0)], 8, up)
    d0 = send(out.at[span(me, 0)], out.at[span(me, 0)], 9, down)
    c1.wait_recv()
    e1 = send(out.at[span(prv, 1)], out.at[span(prv, 1)], 10, up)
    d1.wait_recv()
    d0.wait_recv()
    e0 = send(out.at[span(nxt, 0)], out.at[span(nxt, 0)], 11, down)
    c0.wait_recv()
    e1.wait_recv()
    e0.wait_recv()
    for copy in sends:
        copy.wait_send()


def exchange(tan, curv):
    vmem = pl.BlockSpec(memory_space=pltpu.VMEM)
    hbm = pl.BlockSpec(memory_space=pl.ANY)
    rows = LEN // 4
    half = rows // 2
    return pl.pallas_call(
        exchange_kernel,
        out_shape=jax.ShapeDtypeStruct((LEN, D), BF16),
        in_specs=[vmem, hbm],
        out_specs=vmem,
        scratch_shapes=[
            pltpu.VMEM((rows, D), BF16),
            pltpu.VMEM((half, D), BF16),
            pltpu.VMEM((half, D), BF16),
            pltpu.VMEM((2, half, D), BF16),
            pltpu.VMEM((2, half, D), BF16),
            pltpu.SemaphoreType.DMA((12,)),
            pltpu.SemaphoreType.DMA((12,)),
            pltpu.SemaphoreType.DMA((1,)),
        ],
        compiler_params=pltpu.CompilerParams(
            collective_id=1, has_side_effects=True, vmem_limit_bytes=40_000_000
        ),
        name="exchange",
    )(tan, curv)


def backward_kernel(
    counts,
    weighted,
    cos,
    sin,
    normed_in,
    qkv_in,
    mixed_in,
    probs_in,
    wo_in,
    out,
    normed,
    qkv,
    mixed,
    probs,
    wo,
    gout,
    gqkv,
    dprojt,
    sem,
):
    loads = [
        pltpu.make_async_copy(a, b, sem.at[i])
        for i, (a, b) in enumerate(
            ((wo_in, wo), (mixed_in, mixed), (probs_in, probs), (qkv_in, qkv), (normed_in, normed))
        )
    ]
    for c in loads:
        c.start()
    loads[0].wait()
    dmixed = nt(weighted[...], wo[...]).astype(BF16)
    loads[1].wait()
    mixedt = mixed[...].T
    for n in range(8):
        cols = slice(n * 512, (n + 1) * 512)
        gout[:, cols] = nn(mixedt, weighted[:, cols]).astype(BF16)
    loads[2].wait()
    loads[3].wait()
    c2, s2 = cos[...], sin[...]

    def unrot(x):
        return x * c2 - pltpu.roll(x, 64, 1) * s2

    k = qkv[:, QH * HD : (QH + 1) * HD]
    v = qkv[:, (QH + 1) * HD :]
    scale = HD**-0.5
    dkt = jnp.zeros((HD, LEN), F32)
    dvt = jnp.zeros((HD, LEN), F32)
    for h in range(QH):
        dm = dmixed[:, h * HD : (h + 1) * HD]
        q = qkv[:, h * HD : (h + 1) * HD]
        pb = probs[h]
        dp = nt(dm, v).astype(BF16).astype(F32)
        dvt = dvt + nn(dm.T, pb)
        pf = pb.astype(F32)
        pd = pf * dp
        ds = ((pd - pf * jnp.sum(pd, axis=-1, keepdims=True)) * scale).astype(BF16)
        dkt = dkt + nn(q.T, ds)
        dq = unrot(nn(ds, k).astype(BF16).astype(F32)).astype(BF16)
        dprojt[h * HD : (h + 1) * HD, :] = dq.T
    dk = unrot(dkt.astype(BF16).astype(F32).T).astype(BF16)
    dprojt[QH * HD : (QH + 1) * HD, :] = dk.T
    dprojt[(QH + 1) * HD :, :] = dvt.astype(BF16)
    loads[4].wait()
    for n in range(8):
        cols = slice(n * 512, (n + 1) * 512)
        gqkv[:, cols] = nn(dprojt[...], normed[:, cols]).astype(BF16)

    def device(d, start):
        n = counts[d]

        def one(t, carry):
            b = start + t

            @pl.when(b < NQKV)
            def _():
                r = pl.multiple_of((b // 6) * BLK, BLK)
                c = pl.multiple_of((b % 6) * BLK, BLK)
                pltpu.make_async_copy(
                    gqkv.at[pl.ds(c, BLK), pl.ds(r, BLK)], out.at[d, t], sem.at[5]
                ).start()

            @pl.when(b >= NQKV)
            def _():
                e = b - NQKV
                r = pl.multiple_of((e // 32) * BLK, BLK)
                c = pl.multiple_of((e % 32) * BLK, BLK)
                pltpu.make_async_copy(
                    gout.at[pl.ds(r, BLK), pl.ds(c, BLK)], out.at[d, t], sem.at[6]
                ).start()

            return carry

        lax.fori_loop(0, n, one, 0)
        return start + n

    lax.fori_loop(0, 32, device, 0)
    pltpu.make_async_copy(gqkv, gqkv, sem.at[5]).wait()
    pltpu.make_async_copy(gout, gout, sem.at[6]).wait()


def backward(counts, weighted, cos, sin, normed, qkv, mixed, probs, wo):
    vmem = pl.BlockSpec(memory_space=pltpu.VMEM)
    hbm = pl.BlockSpec(memory_space=pl.ANY)
    smem = pl.BlockSpec(memory_space=pltpu.SMEM)
    return pl.pallas_call(
        backward_kernel,
        out_shape=jax.ShapeDtypeStruct((32, SLOTS, BLK, BLK), BF16),
        in_specs=[smem, vmem, vmem, vmem] + [hbm] * 5,
        out_specs=hbm,
        scratch_shapes=[
            pltpu.VMEM((LEN, D), BF16),
            pltpu.VMEM((LEN, QKV), BF16),
            pltpu.VMEM((LEN, OUT), BF16),
            pltpu.VMEM((QH, LEN, LEN), BF16),
            pltpu.VMEM((OUT, D), BF16),
            pltpu.VMEM((OUT, D), BF16),
            pltpu.VMEM((QKV, D), BF16),
            pltpu.VMEM((QKV, LEN), BF16),
            pltpu.SemaphoreType.DMA((7,)),
        ],
        compiler_params=pltpu.CompilerParams(vmem_limit_bytes=VMEM_LIMIT),
        name="backward",
    )(counts, weighted, cos, sin, normed, qkv, mixed, probs, wo)


def scatter_kernel(
    grads, out, acc, sibling, r_far, r_low, r_high, red, t_far, t_low, t_high,
    send_sem, recv_sem, local_sem,
):
    me, core, y, z = place()
    sib = {"fsdp": index_of(z, y, 1 - core)}

    def at(axis, step):
        if axis == "y":
            return {"fsdp": index_of(z, wrap(y + step), core)}
        return {"fsdp": index_of(wrap(z + step), y, core)}

    greet([at("y", 1), at("y", -1), at("z", 1), at("z", -1), sib])
    first = ("z", "y")
    second = ("y", "z")
    here = {"y": y, "z": z}
    sends = []
    counter = [0]

    def send(src, dst, target):
        number = counter[0]
        counter[0] += 1
        copy = pltpu.make_async_remote_copy(
            src_ref=src,
            dst_ref=dst,
            send_sem=send_sem.at[number],
            recv_sem=recv_sem.at[number],
            device_id=target,
            device_id_type=MESH,
        )
        copy.start()
        sends.append(copy)
        return copy

    def source(part, f, lane):
        index = wrap(here[first[part]] + f)
        slots = pl.ds(part * HALF, HALF)
        if part == 0:
            return grads.at[index, :, lane, slots]
        return grads.at[:, index, lane, slots]

    order = (2, 1, -1, 0)
    local, cross = {}, {}
    for i, f in enumerate(order):
        for part in (0, 1):
            cross[part, f] = send(source(part, f, 1 - core), sibling.at[part, i], sib)
            local[part, f] = pltpu.make_async_copy(
                source(part, f, core), acc.at[part, i], local_sem.at[part * 4 + i]
            )
            local[part, f].start()

    def add_sibling(part, f):
        i = order.index(f)
        local[part, f].wait()
        cross[part, f].wait_recv()

        def step(s, carry):
            acc[part, i, s] = (
                acc[part, i, s].astype(F32) + sibling[part, i, s].astype(F32)
            ).astype(BF16)
            return carry

        lax.fori_loop(0, 4, step, 0)

    lo, hi = pl.ds(0, 3), pl.ds(3, 3)
    a = {}
    for part in (0, 1):
        add_sibling(part, 2)
        a[part, "fu"] = send(acc.at[part, 0, :, lo], r_far.at[part, 0], at(first[part], 1))
        a[part, "fd"] = send(acc.at[part, 0, :, hi], r_far.at[part, 1], at(first[part], -1))
    for part in (0, 1):
        add_sibling(part, 1)
        a[part, "lo1"] = send(acc.at[part, 1, :, hi], r_low.at[part, 1], at(first[part], 1))
    for part in (0, 1):
        add_sibling(part, -1)
        a[part, "hi0"] = send(acc.at[part, 2, :, lo], r_high.at[part, 0], at(first[part], -1))
    for part in (0, 1):
        a[part, "fu"].wait_recv()

        def step(s, carry, part=part):
            r_far[part, 0, s] = (
                r_far[part, 0, s].astype(F32) + acc[part, 1, s, lo].astype(F32)
            ).astype(BF16)
            return carry

        lax.fori_loop(0, 4, step, 0)
        a[part, "lo0"] = send(r_far.at[part, 0], r_low.at[part, 0], at(first[part], 1))
        a[part, "fd"].wait_recv()

        def step2(s, carry, part=part):
            r_far[part, 1, s] = (
                r_far[part, 1, s].astype(F32) + acc[part, 2, s, hi].astype(F32)
            ).astype(BF16)
            return carry

        lax.fori_loop(0, 4, step2, 0)
        a[part, "hi1"] = send(r_far.at[part, 1], r_high.at[part, 1], at(first[part], -1))
    for part in (0, 1):
        add_sibling(part, 0)
    for part in (0, 1):
        for name in ("lo1", "hi0", "lo0", "hi1"):
            a[part, name].wait_recv()
        for h in (0, 1):

            def step3(s, carry, part=part, h=h):
                red[part, s, pl.ds(3 * h, 3)] = (
                    acc[part, 3, s, pl.ds(3 * h, 3)].astype(F32)
                    + r_low[part, h, s].astype(F32)
                    + r_high[part, h, s].astype(F32)
                ).astype(BF16)
                return carry

            lax.fori_loop(0, 4, step3, 0)
        s_here = here[second[part]]
        far, nxt, prv = wrap(s_here + 2), wrap(s_here + 1), wrap(s_here - 1)
        up, down = at(second[part], 1), at(second[part], -1)
        a[part, "tu"] = send(red.at[part, far, lo], t_far.at[part, 0], up)
        a[part, "td"] = send(red.at[part, far, hi], t_far.at[part, 1], down)
        a[part, "tl1"] = send(red.at[part, nxt, hi], t_low.at[part, 1], up)
        a[part, "th0"] = send(red.at[part, prv, lo], t_high.at[part, 0], down)
    for part in (0, 1):
        s_here = here[second[part]]
        nxt, prv = wrap(s_here + 1), wrap(s_here - 1)
        up, down = at(second[part], 1), at(second[part], -1)
        a[part, "tu"].wait_recv()
        t_far[part, 0] = (t_far[part, 0].astype(F32) + red[part, nxt, lo].astype(F32)).astype(BF16)
        a[part, "tl0"] = send(t_far.at[part, 0], t_low.at[part, 0], up)
        a[part, "td"].wait_recv()
        t_far[part, 1] = (t_far[part, 1].astype(F32) + red[part, prv, hi].astype(F32)).astype(BF16)
        a[part, "th1"] = send(t_far.at[part, 1], t_high.at[part, 1], down)
    for part in (0, 1):
        s_here = here[second[part]]
        for name in ("tl1", "th0", "tl0", "th1"):
            a[part, name].wait_recv()
        for h in (0, 1):
            out[pl.ds(part * HALF + 3 * h, 3)] = (
                red[part, s_here, pl.ds(3 * h, 3)].astype(F32)
                + t_low[part, h].astype(F32)
                + t_high[part, h].astype(F32)
            )
    for copy in sends:
        copy.wait_send()


def scatter(grads):
    vmem = pl.BlockSpec(memory_space=pltpu.VMEM)
    hbm = pl.BlockSpec(memory_space=pl.ANY)
    block = (BLK, BLK)
    return pl.pallas_call(
        scatter_kernel,
        out_shape=jax.ShapeDtypeStruct((SLOTS,) + block, F32),
        in_specs=[hbm],
        out_specs=vmem,
        scratch_shapes=[
            pltpu.VMEM((2, 4, 4, HALF) + block, BF16),
            pltpu.VMEM((2, 4, 4, HALF) + block, BF16),
            pltpu.VMEM((2, 2, 4, 3) + block, BF16),
            pltpu.VMEM((2, 2, 4, 3) + block, BF16),
            pltpu.VMEM((2, 2, 4, 3) + block, BF16),
            pltpu.VMEM((2, 4, HALF) + block, BF16),
            pltpu.VMEM((2, 2, 3) + block, BF16),
            pltpu.VMEM((2, 2, 3) + block, BF16),
            pltpu.VMEM((2, 2, 3) + block, BF16),
            pltpu.SemaphoreType.DMA((32,)),
            pltpu.SemaphoreType.DMA((32,)),
            pltpu.SemaphoreType.DMA((8,)),
        ],
        compiler_params=pltpu.CompilerParams(
            collective_id=2, has_side_effects=True, vmem_limit_bytes=48_000_000
        ),
        name="scatter",
    )(grads.reshape(4, 4, 2, SLOTS, BLK, BLK))


def finish_kernel(counts, total, out):
    me = lax.axis_index("fsdp")
    start = lax.fori_loop(0, me, lambda d, s: s + counts[d], 0)
    n = counts[me]
    factor = 1.0 / np.sqrt(np.float32(LEN * 32))

    def one(t, carry):
        x = total[t] * factor
        x = jnp.where(start + t < NQKV, x.T, x)
        out[t] = jnp.where(t < n, x, 0.0)
        return carry

    lax.fori_loop(0, SLOTS, one, 0)


def finish(counts, total):
    vmem = pl.BlockSpec(memory_space=pltpu.VMEM)
    smem = pl.BlockSpec(memory_space=pltpu.SMEM)
    return pl.pallas_call(
        finish_kernel,
        out_shape=jax.ShapeDtypeStruct((SLOTS, BLK, BLK), F32),
        in_specs=[smem, vmem],
        out_specs=vmem,
        name="finish",
    )(counts, total)


def local(tokens, norm_gain, curvature, weight_slots, probe_slots, block_counts):
    counts = block_counts[0]
    cos, sin = tables()
    slots = gather(weight_slots[0], probe_slots[0])
    tan, normed, qkv, mixed, probs, wo = forward(
        counts, tokens[0], norm_gain.reshape(1, D), cos, sin, slots
    )
    weighted = exchange(tan, curvature[0])
    grads = backward(counts, weighted, cos, sin, normed, qkv, mixed, probs, wo)
    total = scatter(grads)
    return finish(counts, total)[None]


def solution(mesh):
    in_specs = (
        P("fsdp", None, None),
        P(),
        P("fsdp", None, None),
        P("seq", "fsdp", None, None),
        P("seq", "fsdp", None, None),
        P("seq", None),
    )
    out_specs = P("seq", "fsdp", None, None)
    return jax.shard_map(local, mesh=mesh, in_specs=in_specs, out_specs=out_specs, check_vma=False)
```

time: 545 us -> 262 us (0.48); the launches traced: 535 us -> 262 us
  waiting for transfers between devices: 296 us -> 0 us
  Pallas kernels: 0 us -> 255 us
  local copies, waits for them, and re-layouts: 127 us -> 7.18 us
  matrix products: 57.7 us -> 0 us
  other arithmetic: 40 us -> 0 us
  between operations: 14.1 us -> 0.07 us
    pallas_call x0 -> x6, Pallas kernels: none -> 255 us  [the longest x1 78 us: gather(): pl.pallas_call(gather_kernel, out_shape=jax.ShapeDtypeStruct((32, 2, SLOT...]
    reduce_scatter x1 -> x0, waiting for transfers between devices: 103 us -> none  [local(): lax.psum_scatter(jnp.where(is_live[:, None, None], grad_blocks[picked].as...]
    all_gather x2 -> x0, waiting for transfers between devices: 102 us -> none  [the longest x1 60.8 us: local(): lax.all_gather(probe_slots[0], 'fsdp', axis=0, tiled=True)]
    psum x1 -> x0, waiting for transfers between devices: 89.6 us -> none  [local(): summed = lax.psum(tangent.astype(jnp.bfloat16), 'seq').astype(jnp.float32)]
    dot_general x17 -> x0, matrix products: 57.7 us -> none  [the longest x3 22.3 us: attention_branch(): projected = jnp.dot(normed, w_qkv, preferred_element_type=jnp.float32)]
    gather x3 -> x0, local copies, waits for them, and re-layouts: 45.8 us -> none  [the longest x1 15.3 us: local(): grad_blocks[picked].astype(jnp.float32)]
    reshape x9 -> x0, local copies, waits for them, and re-layouts: 30.5 us -> none  [the longest x4 23.4 us: to_matrix(): blocks.reshape(row_blocks, col_blocks, blk_edge, blk_edge)]
    slice x9 -> x0, local copies, waits for them, and re-layouts: 19.3 us -> none  [the longest x1 8.09 us: local(): w_qkv = to_matrix(w_blocks[:qkv_split], row_blocks, qkv_cols)]
  transfers between devices with their start and end apart: 4 -> 0, of which waited for: 4 -> 0; matrix products, arithmetic and copies ran while one was open for 6% -> 0% of each run, Pallas kernels for 0% -> 0%
where the time goes in v1:
time: 262 us
  Pallas kernels  255 us (97%)
  local copies, waits for them, and re-layouts  7.18 us (3%)
    pallas_call x1, Pallas kernels, gather(): pl.pallas_call(gather_kernel, out_shape=jax.ShapeDtypeStruct((32, 2, SLOT...  78 us
    pallas_call x1, Pallas kernels, exchange(): pl.pallas_call(exchange_kernel, out_shape=jax.ShapeDtypeStruct((LEN, D),...  74.3 us
    pallas_call x1, Pallas kernels, scatter(): pl.pallas_call(scatter_kernel, out_shape=jax.ShapeDtypeStruct((SLOTS,) +...  42.8 us
    pallas_call x1, Pallas kernels, forward(): pl.pallas_call(forward_kernel, out_shape=[shape((LEN, D), BF16), shape((L...  32.8 us
    pallas_call x1, Pallas kernels, backward(): pl.pallas_call(backward_kernel, out_shape=jax.ShapeDtypeStruct((32, SLOTS...  23.8 us
    unnamed x8, local copies, waits for them, and re-layouts  7.18 us

profile of v1, /device:TPU:1, one launch (start us, length us, event | category | flops | bytes accessed | tf_op | source)
XLA Modules:
  0.0 262.2 jit_solution(13203586919461595614)
XLA Ops:
  0.0 78.0 %gather.1.slots = bf16[32,2,12,128,128]{4,3,2,1,0:T(8,128)(2,1)} custom-call(bf16[12,128,128]{2,1,0:T(8,128)(2,1)} %bitcast.11, bf16[12,128,128]{2,1,0:T(8,128)(2,1)} %bitcast.12), custom_call_target="tpu_custom_call" | custom-call | tf_op jit(solution)/shard_map/gather/pallas_call | solution.py:208
  78.0 32.8 %forward.1 = (bf16[512,4096]{1,0:T(8,128)(2,1)}, bf16[512,4096]{1,0:T(8,128)(2,1)}, bf16[512,768]{1,0:T(8,128)(2,1)}, bf16[512,512]{1,0:T(8,128)(2,1)}, bf16[4,5...) custom-call(s32[32]{0:T(128)} %bitcast.14, bf16[512,4096]{1,0:T(8,128)(2,1)} %bitcast.10, f32[1,4096]{1,0:T(1,128)} %bitcast.13, ...), custom_call_target="tpu_custom_call" | custom-call | tf_op jit(solution)/shard_map/forward/pallas_call | solution.py:364
  110.8 0.0 copy-start.1
  110.8 2.2 copy-done.1
  113.0 0.0 copy-start.2
  113.0 2.2 copy-done.2
  115.2 74.3 %exchange.1.weighted = bf16[512,4096]{1,0:T(8,128)(2,1)S(1)} custom-call(bf16[512,4096]{1,0:T(8,128)(2,1)S(1)} %copy-done.2, bf16[512,4096]{1,0:T(8,128)(2,1)S(1)} %bitcast.8), custom_call_target="tpu_custom_call" | custom-call | tf_op jit(solution)/shard_map/exchange/pallas_call | solution.py:472
  189.4 0.0 copy-start
  189.5 1.9 copy-done
  191.4 23.8 %backward.1 = bf16[32,12,128,128]{3,2,1,0:T(8,128)(2,1)} custom-call(s32[32]{0:T(128)} %bitcast.15, bf16[512,4096]{1,0:T(8,128)(2,1)} %copy-done, f32[512,128]{1,0:T(8,128)} %constant.4.clone.cos, f32[512,128]{1,0:T(8,128)} %constant.5.clone.sin, bf16[512,4096]{1,0:T(8,128)(2,1)} %get-tuple-element.12.normed_in, bf16[512,768]{1,0:T(8,128)(2,1)} %get-tuple-element.13.qkv_in, ...), custom_call_target="tpu_custom_call" | custom-call | tf_op jit(solution)/shard_map/backward/pallas_call | solution.py:599
  215.2 42.8 %scatter.1.total = f32[12,128,128]{2,1,0:T(8,128)S(1)} custom-call(bf16[4,4,2,12,128,128]{5,4,3,2,1,0:T(8,128)(2,1)} %bitcast.9), custom_call_target="tpu_custom_call" | custom-call | tf_op jit(solution)/shard_map/scatter/pallas_call | solution.py:768
  258.0 0.0 copy-start.3
  258.0 0.9 copy-done.3
  258.9 3.3 %finish.1 = f32[12,128,128]{2,1,0:T(8,128)} custom-call(s32[32]{0:T(128)} %bitcast.16, f32[12,128,128]{2,1,0:T(8,128)} %copy-done.3), custom_call_target="tpu_custom_call" | custom-call | tf_op jit(solution)/shard_map/finish/pallas_call | solution.py:812
Async XLA Ops:
  110.8 2.2 copy-start.1
  113.0 2.2 copy-start.2
  189.4 1.9 copy-start
  258.0 0.9 copy-start.3

commit v2 on v1

v2 whole, which is shorter than its diff:
```python
import functools

import jax
import jax.numpy as jnp
import numpy as np
from jax import lax
from jax.experimental import pallas as pl
from jax.experimental.pallas import tpu as pltpu
from jax.sharding import PartitionSpec as P

D = 4096
HD = 128
BLK = 128
LEN = 512
QH = 4
QKV = 768
OUT = 512
NQKV = 192
NB = 320
SLOTS = 12
HALF = 6
CHUNK = 1024
THETA = 500000.0
EPS = 1e-05
NEGATIVE = -1e30
VMEM_LIMIT = 66_000_000
MESH = pl.DeviceIdType.MESH
F32 = jnp.float32
BF16 = jnp.bfloat16


def tables():
    half = HD // 2
    frequency = np.exp(-np.log(THETA) * 2.0 * np.arange(half) / HD)
    angles = np.arange(LEN)[:, None] * frequency[None, :]
    c, s = np.cos(angles), np.sin(angles)
    return (
        np.concatenate([c, c], axis=1).astype(np.float32),
        np.concatenate([-s, s], axis=1).astype(np.float32),
    )


def place():
    me = lax.axis_index("fsdp")
    core = lax.rem(me, 2)
    y = lax.rem(me // 2, 4)
    z = me // 8
    return me, core, y, z


def index_of(z, y, core):
    return (z * 4 + y) * 2 + core


def wrap(a):
    return lax.rem(a + 4, 4)


def greet(targets):
    barrier = pltpu.get_barrier_semaphore()
    for t in targets:
        pl.semaphore_signal(barrier, inc=1, device_id=t, device_id_type=MESH)
    pl.semaphore_wait(barrier, len(targets))


def gather_kernel(
    w_ref, p_ref, tokens_in, gain, out_ref, normed_out, tokens, normed, send_sem, recv_sem, local_sem
):
    me, core, y, z = place()
    get_tokens = pltpu.make_async_copy(tokens_in, tokens, local_sem.at[2])
    get_tokens.start()
    sib = index_of(z, y, 1 - core)

    def at(axis, step):
        if axis == "y":
            return {"fsdp": index_of(z, wrap(y + step), core)}
        return {"fsdp": index_of(wrap(z + step), y, core)}

    greet([at("y", 1), at("y", -1), at("z", 1), at("z", -1), {"fsdp": sib}])

    own = [
        pltpu.make_async_copy(w_ref, out_ref.at[me, 0], local_sem.at[0]),
        pltpu.make_async_copy(p_ref, out_ref.at[me, 1], local_sem.at[1]),
    ]
    for c in own:
        c.start()

    counter = [0]
    sends = []

    def sem():
        counter[0] += 1
        return counter[0] - 1

    def send(src, dst, number, target):
        copy = pltpu.make_async_remote_copy(
            src_ref=src,
            dst_ref=dst,
            send_sem=send_sem.at[number],
            recv_sem=recv_sem.at[number],
            device_id=target,
            device_id_type=MESH,
        )
        copy.start()
        sends.append(copy)
        return copy

    def piece(tensor, origin, part=None):
        if part is None:
            return out_ref.at[origin, tensor]
        return out_ref.at[origin, tensor, pl.ds(part * HALF, HALF)]

    first = ("y", "z")
    second = ("z", "y")

    def origin_of(tensor, f, s):
        if tensor == 0:
            return index_of(wrap(z + s), wrap(y + f), core)
        return index_of(wrap(z + f), wrap(y + s), core)

    number = {}
    for tensor in (0, 1):
        for role in ("f+", "f-", "fa", "fb"):
            number[tensor, role] = sem()
        for f in (0, 1, -1, 2):
            for role in ("s+", "s-", "sa", "sb"):
                number[tensor, role, f] = sem()
        for f in (0, 1, -1, 2):
            for s in (0, 1, -1, 2):
                number[tensor, "sib", f, s] = sem()

    arrivals = {}

    def go(tensor, role, src_origin, axis, step, part=None, src=None):
        ref = piece(tensor, src_origin, part)
        copy = send(ref if src is None else src, ref, number[(tensor,) + role], at(axis, step))
        arrivals[(tensor,) + role] = copy

    def to_sib(tensor, f, s, src=None):
        origin = origin_of(tensor, f, s)
        ref = piece(tensor, origin)
        copy = send(ref if src is None else src, ref, number[tensor, "sib", f, s], {"fsdp": sib})
        arrivals[tensor, "sib", f, s] = copy

    mine = (w_ref, p_ref)
    for tensor in (0, 1):
        go(tensor, ("f+",), me, first[tensor], 1, src=mine[tensor])
        go(tensor, ("f-",), me, first[tensor], -1, src=mine[tensor])
    for tensor in (0, 1):
        go(tensor, ("s+", 0), me, second[tensor], 1, src=mine[tensor])
        go(tensor, ("s-", 0), me, second[tensor], -1, src=mine[tensor])
    for tensor in (0, 1):
        to_sib(tensor, 0, 0, src=mine[tensor])

    get_tokens.wait()

    def norm(i, carry):
        rows = pl.ds(pl.multiple_of(i * 32, 32), 32)
        x = tokens[rows, :].astype(F32)
        factor = lax.rsqrt(jnp.mean(x * x, axis=-1, keepdims=True) + EPS)
        normed[rows, :] = (x * factor * gain[...]).astype(BF16)
        return carry

    lax.fori_loop(0, LEN // 32, norm, 0)
    own.append(pltpu.make_async_copy(normed, normed_out, local_sem.at[3]))
    own[-1].start()

    for tensor in (0, 1):
        arrivals[tensor, "f+"].wait_recv()
        lower = origin_of(tensor, -1, 0)
        go(tensor, ("fa",), lower, first[tensor], 1, part=0)
        go(tensor, ("s+", -1), lower, second[tensor], 1)
        go(tensor, ("s-", -1), lower, second[tensor], -1)
        arrivals[tensor, "f-"].wait_recv()
        upper = origin_of(tensor, 1, 0)
        go(tensor, ("fb",), upper, first[tensor], -1, part=1)
        go(tensor, ("s+", 1), upper, second[tensor], 1)
        go(tensor, ("s-", 1), upper, second[tensor], -1)
        to_sib(tensor, -1, 0)
        to_sib(tensor, 1, 0)

    def pass_on(tensor, f):
        arrivals[tensor, "s+", f].wait_recv()
        go(tensor, ("sa", f), origin_of(tensor, f, -1), second[tensor], 1, part=0)
        to_sib(tensor, f, -1)
        arrivals[tensor, "s-", f].wait_recv()
        go(tensor, ("sb", f), origin_of(tensor, f, 1), second[tensor], -1, part=1)
        to_sib(tensor, f, 1)

    for tensor in (0, 1):
        pass_on(tensor, 0)
    for tensor in (0, 1):
        arrivals[tensor, "fa"].wait_recv()
        arrivals[tensor, "fb"].wait_recv()
        far = origin_of(tensor, 2, 0)
        go(tensor, ("s+", 2), far, second[tensor], 1)
        go(tensor, ("s-", 2), far, second[tensor], -1)
        to_sib(tensor, 2, 0)
    for f in (-1, 1, 2):
        for tensor in (0, 1):
            pass_on(tensor, f)
            if f == -1:
                g = 0
            elif f == 1:
                g = -1
            else:
                g = 1
            arrivals[tensor, "sa", g].wait_recv()
            arrivals[tensor, "sb", g].wait_recv()
            to_sib(tensor, g, 2)
    for tensor in (0, 1):
        arrivals[tensor, "sa", 2].wait_recv()
        arrivals[tensor, "sb", 2].wait_recv()
        to_sib(tensor, 2, 2)
    for key, copy in arrivals.items():
        if key[1] == "sib":
            copy.wait_recv()
    for c in own:
        c.wait()
    for copy in sends:
        copy.wait_send()


def gather(w, p, tokens, gain):
    vmem = pl.BlockSpec(memory_space=pltpu.VMEM)
    hbm = pl.BlockSpec(memory_space=pl.ANY)
    return pl.pallas_call(
        gather_kernel,
        out_shape=[
            jax.ShapeDtypeStruct((32, 2, SLOTS, BLK, BLK), BF16),
            jax.ShapeDtypeStruct((LEN, D), BF16),
        ],
        in_specs=[vmem, vmem, hbm, vmem],
        out_specs=[hbm, hbm],
        scratch_shapes=[
            pltpu.VMEM((LEN, D), BF16),
            pltpu.VMEM((LEN, D), BF16),
            pltpu.SemaphoreType.DMA((72,)),
            pltpu.SemaphoreType.DMA((72,)),
            pltpu.SemaphoreType.DMA((4,)),
        ],
        compiler_params=pltpu.CompilerParams(
            collective_id=0, has_side_effects=True, vmem_limit_bytes=VMEM_LIMIT
        ),
        name="gather",
    )(w, p, tokens, gain)


def nt(a, b):
    return lax.dot_general(a, b, (((1,), (1,)), ((), ())), preferred_element_type=F32)


def nn(a, b):
    return jnp.dot(a, b, preferred_element_type=F32)


def causal_mask():
    row = lax.broadcasted_iota(jnp.int32, (LEN, LEN), 0)
    col = lax.broadcasted_iota(jnp.int32, (LEN, LEN), 1)
    return row >= col


def forward_kernel(
    counts,
    cos,
    sin,
    normed_in,
    slots,
    qkv_out,
    sides_out,
    probs_out,
    wo_out,
    normed,
    wqkv,
    wout,
    proj,
    sides,
    probs,
    qkv,
    sem,
):
    get_normed = pltpu.make_async_copy(normed_in, normed, sem.at[2])
    get_normed.start()

    def device(d, start):
        n = counts[d]

        def one(t, carry):
            b = start + t

            @pl.when(b < NQKV)
            def _():
                r = pl.multiple_of((b // 6) * BLK, BLK)
                c = pl.multiple_of((b % 6) * BLK, BLK)
                pltpu.make_async_copy(
                    slots.at[d, :, t], wqkv.at[:, pl.ds(r, BLK), pl.ds(c, BLK)], sem.at[0]
                ).start()

            @pl.when(b >= NQKV)
            def _():
                e = b - NQKV
                j = e % 32
                r = pl.multiple_of((e // 32) * BLK, BLK)
                c = pl.multiple_of((j % 8) * BLK, BLK)
                pltpu.make_async_copy(
                    slots.at[d, :, t],
                    wout.at[j // 8, :, pl.ds(r, BLK), pl.ds(c, BLK)],
                    sem.at[1],
                ).start()

            return carry

        lax.fori_loop(0, n, one, 0)
        return start + n

    lax.fori_loop(0, 32, device, 0)
    get_normed.wait()
    pltpu.make_async_copy(wqkv, wqkv, sem.at[0]).wait()

    for tensor in (0, 1):
        for n in range(3):
            cols = slice(n * 256, (n + 1) * 256)
            proj[tensor, :, cols] = nn(normed[...], wqkv[tensor, :, cols])
    pltpu.make_async_copy(wout, wout, sem.at[1]).wait()
    save_wo = pltpu.make_async_copy(wout, wo_out, sem.at[6])
    save_wo.start()

    c2, s2 = cos[...], sin[...]

    def rot(x):
        return x * c2 + pltpu.roll(x, 64, 1) * s2

    def head(tensor, h):
        x = proj[tensor, :, h * HD : (h + 1) * HD]
        if h < QH + 1:
            x = rot(x)
        return x.astype(BF16)

    for h in range(QH + 2):
        qkv[:, h * HD : (h + 1) * HD] = head(0, h)
    save_qkv = pltpu.make_async_copy(qkv, qkv_out, sem.at[3])
    save_qkv.start()
    k = qkv[:, QH * HD : (QH + 1) * HD]
    v = qkv[:, (QH + 1) * HD :]
    keys = jnp.concatenate([k, head(1, QH)], axis=1)
    values = jnp.concatenate([v, head(1, QH + 1)], axis=1)
    causal = causal_mask()
    scale = HD**-0.5
    for h in range(QH):
        q = qkv[:, h * HD : (h + 1) * HD]
        tq = head(1, h)
        s = jnp.where(causal, nt(q, k) * scale, NEGATIVE)
        m = jnp.max(s, axis=-1, keepdims=True)
        e = jnp.exp(s - m)
        p = e * (1.0 / jnp.sum(e, axis=-1, keepdims=True))
        ts = nt(jnp.concatenate([tq, q], axis=1), keys) * scale
        pt = p * ts
        tp = pt - p * jnp.sum(pt, axis=-1, keepdims=True)
        pb = p.astype(BF16)
        probs[h] = pb
        both = nn(pb, values)
        mixed_t = nn(tp.astype(BF16), v) + both[:, HD:]
        sides[0, :, h * HD : (h + 1) * HD] = mixed_t.astype(BF16)
        sides[1, :, h * HD : (h + 1) * HD] = both[:, :HD].astype(BF16)
    save_probs = pltpu.make_async_copy(probs, probs_out, sem.at[4])
    save_probs.start()
    save_sides = pltpu.make_async_copy(sides, sides_out, sem.at[5])
    save_sides.start()
    for c in (save_wo, save_qkv, save_probs, save_sides):
        c.wait()


def forward(counts, cos, sin, normed, slots):
    vmem = pl.BlockSpec(memory_space=pltpu.VMEM)
    hbm = pl.BlockSpec(memory_space=pl.ANY)
    smem = pl.BlockSpec(memory_space=pltpu.SMEM)
    shape = jax.ShapeDtypeStruct
    return pl.pallas_call(
        forward_kernel,
        out_shape=[
            shape((LEN, QKV), BF16),
            shape((2, LEN, OUT), BF16),
            shape((QH, LEN, LEN), BF16),
            shape((4, 2, OUT, CHUNK), BF16),
        ],
        in_specs=[smem, vmem, vmem, hbm, hbm],
        out_specs=[hbm, hbm, hbm, hbm],
        scratch_shapes=[
            pltpu.VMEM((LEN, D), BF16),
            pltpu.VMEM((2, D, QKV), BF16),
            pltpu.VMEM((4, 2, OUT, CHUNK), BF16),
            pltpu.VMEM((2, LEN, QKV), F32),
            pltpu.VMEM((2, LEN, OUT), BF16),
            pltpu.VMEM((QH, LEN, LEN), BF16),
            pltpu.VMEM((LEN, QKV), BF16),
            pltpu.SemaphoreType.DMA((7,)),
        ],
        compiler_params=pltpu.CompilerParams(vmem_limit_bytes=VMEM_LIMIT),
        name="forward",
    )(counts, cos, sin, normed, slots)


FAR, NXT, PRV, OWN = 0, 1, 2, 3


def main_kernel(
    counts, cos, sin, sides_in, wo_in, curv_in, probs_in, qkv_in, normed_in,
    out,
    starts, sides, wo, curv, probs, qkv, normed,
    tan, opp, low, high, wt, dmix, dprojt, gb, sb,
    acc, r_far, r_low, r_high, red, t_far, t_low, t_high, fin,
    send_sem, recv_sem, local_sem,
):
    me, core, y, z = place()
    x = lax.axis_index("seq")
    sib = {"fsdp": index_of(z, y, 1 - core)}
    up, down = {"seq": wrap(x + 1)}, {"seq": wrap(x - 1)}

    def at(axis, step):
        if axis == "y":
            return {"fsdp": index_of(z, wrap(y + step), core)}
        return {"fsdp": index_of(wrap(z + step), y, core)}

    chunk = (wrap(x + 2), wrap(x + 1), wrap(x - 1), x)
    curv_cols = pl.ds(pl.multiple_of(x * CHUNK, CHUNK), CHUNK)
    loads = [
        pltpu.make_async_copy(a, b, local_sem.at[i])
        for i, (a, b) in enumerate(
            [(wo_in.at[chunk[rel]], wo.at[rel]) for rel in range(4)]
            + [
                (sides_in, sides),
                (curv_in.at[:, curv_cols], curv),
                (probs_in, probs),
                (qkv_in, qkv),
                (normed_in, normed),
            ]
        )
    ]
    for i in (4, 0, 1, 2, 3, 5, 6, 7, 8):
        loads[i].start()
    greet([up, down, at("y", 1), at("y", -1), at("z", 1), at("z", -1), sib])

    sends = []
    counter = [0]

    def send(src, dst, target):
        number = counter[0]
        counter[0] += 1
        copy = pltpu.make_async_remote_copy(
            src_ref=src,
            dst_ref=dst,
            send_sem=send_sem.at[number],
            recv_sem=recv_sem.at[number],
            device_id=target,
            device_id_type=MESH,
        )
        copy.start()
        sends.append(copy)
        return copy

    half = LEN // 2
    rows = (pl.ds(0, half), pl.ds(half, half))

    def term(rel, part):
        r = rows[part]
        tan[rel, r] = (nn(sides[0, r], wo[rel, 0]) + nn(sides[1, r], wo[rel, 1])).astype(BF16)

    loads[4].wait()
    loads[FAR].wait()
    term(FAR, 0)
    a0 = send(tan.at[FAR, rows[0]], opp.at[0], up)
    term(FAR, 1)
    b0 = send(tan.at[FAR, rows[1]], opp.at[1], down)
    loads[NXT].wait()
    term(NXT, 1)
    a1 = send(tan.at[NXT, rows[1]], low.at[1], up)
    loads[PRV].wait()
    term(PRV, 0)
    b1 = send(tan.at[PRV, rows[0]], high.at[0], down)
    term(NXT, 0)
    term(PRV, 1)
    loads[OWN].wait()
    term(OWN, 0)
    term(OWN, 1)
    a0.wait_recv()
    opp[0] = (opp[0].astype(F32) + tan[NXT, rows[0]].astype(F32)).astype(BF16)
    a2 = send(opp.at[0], low.at[0], up)
    b0.wait_recv()
    opp[1] = (opp[1].astype(F32) + tan[PRV, rows[1]].astype(F32)).astype(BF16)
    b2 = send(opp.at[1], high.at[1], down)
    loads[5].wait()

    def prefix(d, s):
        starts[d] = s
        return s + counts[d]

    lax.fori_loop(0, 32, prefix, 0)

    def weigh(part):
        r = rows[part]
        total = tan[OWN, r].astype(F32) + low[part].astype(F32) + high[part].astype(F32)
        wt[OWN, r] = (total * curv[r].astype(F32)).astype(BF16)

    def hand_on(src, dst, part, target):
        return send(wt.at[src, rows[part]], wt.at[dst, rows[part]], target)

    a1.wait_recv()
    b2.wait_recv()
    weigh(1)
    c1 = hand_on(OWN, PRV, 1, up)
    d1 = hand_on(OWN, NXT, 1, down)
    b1.wait_recv()
    a2.wait_recv()
    weigh(0)
    d0 = hand_on(OWN, NXT, 0, down)
    c0 = hand_on(OWN, PRV, 0, up)

    mixedt = sides[1].T

    def consume(rel):
        part = nt(wt[rel], wo[rel, 0])
        if rel == OWN:
            dmix[...] = part
        else:
            dmix[...] += part
        g = nn(mixedt, wt[rel]).astype(BF16)
        for i in range(4):
            for j in range(8):
                gb[j % 2, NQKV // 2 + 16 * i + 4 * chunk[rel] + j // 2] = g[
                    i * BLK : (i + 1) * BLK, j * BLK : (j + 1) * BLK
                ]

    consume(OWN)
    c1.wait_recv()
    e1 = hand_on(PRV, FAR, 1, up)
    d1.wait_recv()
    d0.wait_recv()
    e0 = hand_on(NXT, FAR, 0, down)
    consume(NXT)
    c0.wait_recv()
    consume(PRV)
    e1.wait_recv()
    e0.wait_recv()
    consume(FAR)
    n_out = NB // 2 - NQKV // 2
    out_part = pl.ds(NQKV // 2, n_out)
    swap_out = send(gb.at[1 - core, out_part], sb.at[out_part], sib)

    for i in (6, 7, 8):
        loads[i].wait()
    c2, s2 = cos[...], sin[...]

    def unrot(x):
        return x * c2 - pltpu.roll(x, 64, 1) * s2

    k = qkv[:, QH * HD : (QH + 1) * HD]
    v = qkv[:, (QH + 1) * HD :]
    scale = HD**-0.5
    dkt = jnp.zeros((HD, LEN), F32)
    dvt = jnp.zeros((HD, LEN), F32)
    for h in range(QH):
        dm = dmix[:, h * HD : (h + 1) * HD].astype(BF16)
        q = qkv[:, h * HD : (h + 1) * HD]
        pb = probs[h]
        dp = nt(dm, v).astype(BF16).astype(F32)
        dvt = dvt + nn(dm.T, pb)
        pf = pb.astype(F32)
        pd = pf * dp
        ds = ((pd - pf * jnp.sum(pd, axis=-1, keepdims=True)) * scale).astype(BF16)
        dkt = dkt + nn(q.T, ds)
        dq = unrot(nn(ds, k).astype(BF16).astype(F32)).astype(BF16)
        dprojt[h * HD : (h + 1) * HD, :] = dq.T
    dk = unrot(dkt.astype(BF16).astype(F32).T).astype(BF16)
    dprojt[QH * HD : (QH + 1) * HD, :] = dk.T
    dprojt[(QH + 1) * HD :, :] = dvt.astype(BF16)

    def add_sibling(base, count):
        def step(i, carry):
            b = base + i * 4
            gb[core, pl.ds(b, 4)] = (
                gb[core, pl.ds(b, 4)].astype(F32) + sb[pl.ds(b, 4)].astype(F32)
            ).astype(BF16)
            return carry

        lax.fori_loop(0, count // 4, step, 0)

    swaps = []
    for n in range(8):
        cols = slice(n * 512, (n + 1) * 512)
        g = nn(dprojt[...], normed[:, cols]).astype(BF16)
        for r in range(4):
            for c in range(6):
                gb[c % 2, 3 * (4 * n + r) + c // 2] = g[
                    c * BLK : (c + 1) * BLK, r * BLK : (r + 1) * BLK
                ]
        piece = pl.ds(12 * n, 12)
        swaps.append(send(gb.at[1 - core, piece], sb.at[piece], sib))
    swap_out.wait_recv()
    add_sibling(NQKV // 2, n_out)
    for n in range(8):
        swaps[n].wait_recv()
        add_sibling(12 * n, 12)

    first = ("z", "y")
    second = ("y", "z")
    here = {"y": y, "z": z}
    steps = (2, 1, -1, 0)

    def fill(part, rel):
        f = wrap(here[first[part]] + steps[rel])

        def step(s, carry):
            if part == 0:
                d = index_of(f, s, part)
            else:
                d = index_of(s, f, part)
            base = (starts[d] + 1 - core) // 2
            for i in range(HALF):
                acc[part, rel, s, i] = gb[core, jnp.minimum(base + i, NB // 2 - 1)]
            return carry

        lax.fori_loop(0, 4, step, 0)

    lo, hi = pl.ds(0, 3), pl.ds(3, 3)
    a = {}
    for part in (0, 1):
        fill(part, FAR)
        a[part, "fu"] = send(acc.at[part, FAR, :, lo], r_far.at[part, 0], at(first[part], 1))
        a[part, "fd"] = send(acc.at[part, FAR, :, hi], r_far.at[part, 1], at(first[part], -1))
    for part in (0, 1):
        fill(part, NXT)
        a[part, "lo1"] = send(acc.at[part, NXT, :, hi], r_low.at[part, 1], at(first[part], 1))
    for part in (0, 1):
        fill(part, PRV)
        a[part, "hi0"] = send(acc.at[part, PRV, :, lo], r_high.at[part, 0], at(first[part], -1))
    for part in (0, 1):
        fill(part, OWN)
    for part in (0, 1):
        for p, name, rel, span, name2, dst, step_to in (
            (0, "fu", NXT, lo, "lo0", r_low, 1),
            (1, "fd", PRV, hi, "hi1", r_high, -1),
        ):
            a[part, name].wait_recv()

            def step(s, carry, part=part, p=p, rel=rel, span=span):
                r_far[part, p, s] = (
                    r_far[part, p, s].astype(F32) + acc[part, rel, s, span].astype(F32)
                ).astype(BF16)
                return carry

            lax.fori_loop(0, 4, step, 0)
            a[part, name2] = send(r_far.at[part, p], dst.at[part, p], at(first[part], step_to))
    for part in (0, 1):
        for name in ("lo1", "hi0", "lo0", "hi1"):
            a[part, name].wait_recv()
        for h in (0, 1):

            def step3(s, carry, part=part, h=h):
                red[part, s, pl.ds(3 * h, 3)] = (
                    acc[part, OWN, s, pl.ds(3 * h, 3)].astype(F32)
                    + r_low[part, h, s].astype(F32)
                    + r_high[part, h, s].astype(F32)
                ).astype(BF16)
                return carry

            lax.fori_loop(0, 4, step3, 0)
        s_here = here[second[part]]
        far, nxt, prv = wrap(s_here + 2), wrap(s_here + 1), wrap(s_here - 1)
        to_up, to_down = at(second[part], 1), at(second[part], -1)
        a[part, "tu"] = send(red.at[part, far, lo], t_far.at[part, 0], to_up)
        a[part, "td"] = send(red.at[part, far, hi], t_far.at[part, 1], to_down)
        a[part, "tl1"] = send(red.at[part, nxt, hi], t_low.at[part, 1], to_up)
        a[part, "th0"] = send(red.at[part, prv, lo], t_high.at[part, 0], to_down)
    for part in (0, 1):
        s_here = here[second[part]]
        nxt, prv = wrap(s_here + 1), wrap(s_here - 1)
        to_up, to_down = at(second[part], 1), at(second[part], -1)
        a[part, "tu"].wait_recv()
        t_far[part, 0] = (t_far[part, 0].astype(F32) + red[part, nxt, lo].astype(F32)).astype(BF16)
        a[part, "tl0"] = send(t_far.at[part, 0], t_low.at[part, 0], to_up)
        a[part, "td"].wait_recv()
        t_far[part, 1] = (t_far[part, 1].astype(F32) + red[part, prv, hi].astype(F32)).astype(BF16)
        a[part, "th1"] = send(t_far.at[part, 1], t_high.at[part, 1], to_down)
    for part in (0, 1):
        s_here = here[second[part]]
        for name in ("tl1", "th0", "tl0", "th1"):
            a[part, name].wait_recv()
        for h in (0, 1):
            fin[part, pl.ds(3 * h, 3)] = (
                red[part, s_here, pl.ds(3 * h, 3)].astype(F32)
                + t_low[part, h].astype(F32)
                + t_high[part, h].astype(F32)
            )
    last = send(fin.at[1 - core], out.at[core], sib)
    out[core] = fin[core]
    last.wait_recv()
    for copy in sends:
        copy.wait_send()


def main(counts, cos, sin, sides, wo, curv, probs, qkv, normed):
    vmem = pl.BlockSpec(memory_space=pltpu.VMEM)
    hbm = pl.BlockSpec(memory_space=pl.ANY)
    smem = pl.BlockSpec(memory_space=pltpu.SMEM)
    block = (BLK, BLK)
    half = LEN // 2
    v = pltpu.VMEM
    return pl.pallas_call(
        main_kernel,
        out_shape=jax.ShapeDtypeStruct((2, HALF) + block, F32),
        in_specs=[smem, vmem, vmem] + [hbm] * 6,
        out_specs=vmem,
        scratch_shapes=[
            pltpu.SMEM((32,), jnp.int32),
            v((2, LEN, OUT), BF16),
            v((4, 2, OUT, CHUNK), BF16),
            v((LEN, CHUNK), BF16),
            v((QH, LEN, LEN), BF16),
            v((LEN, QKV), BF16),
            v((LEN, D), BF16),
            v((4, LEN, CHUNK), BF16),
            v((2, half, CHUNK), BF16),
            v((2, half, CHUNK), BF16),
            v((2, half, CHUNK), BF16),
            v((4, LEN, CHUNK), BF16),
            v((LEN, OUT), F32),
            v((QKV, LEN), BF16),
            v((2, NB // 2) + block, BF16),
            v((NB // 2,) + block, BF16),
            v((2, 4, 4, HALF) + block, BF16),
            v((2, 2, 4, 3) + block, BF16),
            v((2, 2, 4, 3) + block, BF16),
            v((2, 2, 4, 3) + block, BF16),
            v((2, 4, HALF) + block, BF16),
            v((2, 2, 3) + block, BF16),
            v((2, 2, 3) + block, BF16),
            v((2, 2, 3) + block, BF16),
            v((2, HALF) + block, F32),
            pltpu.SemaphoreType.DMA((64,)),
            pltpu.SemaphoreType.DMA((64,)),
            pltpu.SemaphoreType.DMA((9,)),
        ],
        compiler_params=pltpu.CompilerParams(
            collective_id=1, has_side_effects=True, vmem_limit_bytes=67_000_000
        ),
        name="main",
    )(counts, cos, sin, sides, wo, curv, probs, qkv, normed)


def finish_kernel(counts, total, out):
    me = lax.axis_index("fsdp")
    start = lax.fori_loop(0, me, lambda d, s: s + counts[d], 0)
    n = counts[me]
    factor = 1.0 / np.sqrt(np.float32(LEN * 32))

    def one(t, carry):
        b = start + t
        parity = b % 2
        x = total[parity, b // 2 - (start + 1 - parity) // 2] * factor
        x = jnp.where(b < NQKV, x.T, x)
        out[t] = jnp.where(t < n, x, 0.0)
        return carry

    lax.fori_loop(0, SLOTS, one, 0)


def finish(counts, total):
    vmem = pl.BlockSpec(memory_space=pltpu.VMEM)
    smem = pl.BlockSpec(memory_space=pltpu.SMEM)
    return pl.pallas_call(
        finish_kernel,
        out_shape=jax.ShapeDtypeStruct((SLOTS, BLK, BLK), F32),
        in_specs=[smem, vmem],
        out_specs=vmem,
        name="finish",
    )(counts, total)


def local(tokens, norm_gain, curvature, weight_slots, probe_slots, block_counts):
    counts = block_counts[0]
    cos, sin = tables()
    slots, normed = gather(weight_slots[0], probe_slots[0], tokens[0], norm_gain.reshape(1, D))
    qkv, sides, probs, wo = forward(counts, cos, sin, normed, slots)
    total = main(counts, cos, sin, sides, wo, curvature[0], probs, qkv, normed)
    return finish(counts, total)[None]


def solution(mesh):
    in_specs = (
        P("fsdp", None, None),
        P(),
        P("fsdp", None, None),
        P("seq", "fsdp", None, None),
        P("seq", "fsdp", None, None),
        P("seq", None),
    )
    out_specs = P("seq", "fsdp", None, None)
    return jax.shard_map(local, mesh=mesh, in_specs=in_specs, out_specs=out_specs, check_vma=False)
```

time: 262 us -> 239 us (0.912)
  Pallas kernels: 255 us -> 239 us
  local copies, waits for them, and re-layouts: 7.18 us -> 0 us
    pallas_call x5 -> x3, Pallas kernels: 252 us -> 236 us  [the longest x1 131 us: main(): pl.pallas_call(main_kernel, out_shape=jax.ShapeDtypeStruct((2, HALF) + bl...]
    unnamed x8 -> x0, local copies, waits for them, and re-layouts: 7.18 us -> none
where the time goes in v2:
time: 239 us
  Pallas kernels  239 us (100%)
    pallas_call x1, Pallas kernels, main(): pl.pallas_call(main_kernel, out_shape=jax.ShapeDtypeStruct((2, HALF) + bl...  131 us
    pallas_call x1, Pallas kernels, gather(): pl.pallas_call(gather_kernel, out_shape=[jax.ShapeDtypeStruct((32, 2, SLO...  78 us
    pallas_call x1, Pallas kernels, forward(): pl.pallas_call(forward_kernel, out_shape=[shape((LEN, QKV), BF16), shape(...  26.9 us

profile of v2, /device:TPU:1, one launch (start us, length us, event | category | flops | bytes accessed | tf_op | source)
XLA Modules:
  0.0 239.3 jit_solution(2663653712575315315)
XLA Ops:
  0.0 78.0 %gather.1 = (bf16[32,2,12,128,128]{4,3,2,1,0:T(8,128)(2,1)}, bf16[512,4096]{1,0:T(8,128)(2,1)}) custom-call(bf16[12,128,128]{2,1,0:T(8,128)(2,1)} %bitcast.9, bf16[12,128,128]{2,1,0:T(8,128)(2,1)} %bitcast.10, bf16[512,4096]{1,0:T(8,128)(2,1)} %bitcast.7, f32[1,4096]{1,0:T(1,128)} %bitcast.11), custom_call_target="tpu_custom_call" | custom-call | tf_op jit(solution)/shard_map/gather/pallas_call | solution.py:227
  78.0 26.9 %forward.1 = (bf16[512,768]{1,0:T(8,128)(2,1)}, bf16[2,512,512]{2,1,0:T(8,128)(2,1)}, bf16[4,512,512]{2,1,0:T(8,128)(2,1)}, bf16[4,2,512,1024]{3,2,1,0:T(8,128)(2,1)}) custom-call(s32[32]{0:T(128)} %bitcast.12, f32[512,128]{1,0:T(8,128)} %constant.4.clone.cos, f32[512,128]{1,0:T(8,128)} %constant.5.clone.sin, bf16[512,4096]{1,0:T(8,128)(2,1)} %get-tuple-element.11.normed_in, ...), custom_call_target="tpu_custom_call" | custom-call | tf_op jit(solution)/shard_map/forward/pallas_call | solution.py:378
  104.9 130.9 %main.1.total = f32[2,6,128,128]{3,2,1,0:T(8,128)} custom-call(s32[32]{0:T(128)} %bitcast.13, f32[512,128]{1,0:T(8,128)} %constant.4.clone.cos, f32[512,128]{1,0:T(8,128)} %constant.5.clone.sin, bf16[2,512,512]{2,1,0:T(8,128)(2,1)} %get-tuple-element.13.sides_in, bf16[4,2,512,1024]{3,2,1,0:T(8,128)(2,1)} %get-tuple-element.14.wo_in, ...), custom_call_target="tpu_custom_call" | custom-call | tf_op jit(solution)/shard_map/main/pallas_call | solution.py:708
  235.9 3.4 %finish.1 = f32[12,128,128]{2,1,0:T(8,128)} custom-call(s32[32]{0:T(128)} %bitcast.14, f32[2,6,128,128]{3,2,1,0:T(8,128)} %main.1.total), custom_call_target="tpu_custom_call" | custom-call | tf_op jit(solution)/shard_map/finish/pallas_call | solution.py:770

commit v3 on v2

--- a/solution.py
+++ b/solution.py
@@ -20,6 +20,7 @@
 SLOTS = 12
 HALF = 6
 CHUNK = 1024
+SUB = 512
 THETA = 500000.0
 EPS = 1e-05
 NEGATIVE = -1e30
@@ -64,7 +65,8 @@
 
 
 def gather_kernel(
-    w_ref, p_ref, tokens_in, gain, out_ref, normed_out, tokens, normed, send_sem, recv_sem, local_sem
+    counts, w_ref, p_ref, tokens_in, gain, out_ref, normed_out, table,
+    tokens, normed, send_sem, recv_sem, local_sem,
 ):
     me, core, y, z = place()
     get_tokens = pltpu.make_async_copy(tokens_in, tokens, local_sem.at[2])
@@ -79,8 +81,8 @@
     greet([at("y", 1), at("y", -1), at("z", 1), at("z", -1), {"fsdp": sib}])
 
     own = [
-        pltpu.make_async_copy(w_ref, out_ref.at[me, 0], local_sem.at[0]),
-        pltpu.make_async_copy(p_ref, out_ref.at[me, 1], local_sem.at[1]),
+        pltpu.make_async_copy(w_ref, out_ref.at[0, pl.ds(me * SLOTS, SLOTS)], local_sem.at[0]),
+        pltpu.make_async_copy(p_ref, out_ref.at[1, pl.ds(me * SLOTS, SLOTS)], local_sem.at[1]),
     ]
     for c in own:
         c.start()
@@ -107,8 +109,8 @@
 
     def piece(tensor, origin, part=None):
         if part is None:
-            return out_ref.at[origin, tensor]
-        return out_ref.at[origin, tensor, pl.ds(part * HALF, HALF)]
+            return out_ref.at[tensor, pl.ds(origin * SLOTS, SLOTS)]
+        return out_ref.at[tensor, pl.ds(origin * SLOTS + part * HALF, HALF)]
 
     first = ("y", "z")
     second = ("z", "y")
@@ -152,6 +154,14 @@
     for tensor in (0, 1):
         to_sib(tensor, 0, 0, src=mine[tensor])
 
+    b = lax.broadcasted_iota(jnp.int32, (8, 128), 0) * 128 + lax.broadcasted_iota(
+        jnp.int32, (8, 128), 1
+    )
+    slot, end = b, 0
+    for d in range(32):
+        end = end + counts[d]
+        slot = slot + jnp.where(b >= end, SLOTS - counts[d], 0)
+    table[...] = slot
     get_tokens.wait()
 
     def norm(i, carry):
@@ -221,17 +231,19 @@
         copy.wait_send()
 
 
-def gather(w, p, tokens, gain):
+def gather(counts, w, p, tokens, gain):
     vmem = pl.BlockSpec(memory_space=pltpu.VMEM)
     hbm = pl.BlockSpec(memory_space=pl.ANY)
+    smem = pl.BlockSpec(memory_space=pltpu.SMEM)
     return pl.pallas_call(
         gather_kernel,
         out_shape=[
-            jax.ShapeDtypeStruct((32, 2, SLOTS, BLK, BLK), BF16),
+            jax.ShapeDtypeStruct((2, 32 * SLOTS, BLK, BLK), BF16),
             jax.ShapeDtypeStruct((LEN, D), BF16),
+            jax.ShapeDtypeStruct((8, 128), jnp.int32),
         ],
-        in_specs=[vmem, vmem, hbm, vmem],
-        out_specs=[hbm, hbm],
+        in_specs=[smem, vmem, vmem, hbm, vmem],
+        out_specs=[hbm, hbm, vmem],
         scratch_shapes=[
             pltpu.VMEM((LEN, D), BF16),
             pltpu.VMEM((LEN, D), BF16),
@@ -243,7 +255,7 @@
             collective_id=0, has_side_effects=True, vmem_limit_bytes=VMEM_LIMIT
         ),
         name="gather",
-    )(w, p, tokens, gain)
+    )(counts, w, p, tokens, gain)
 
 
 def nt(a, b):
@@ -261,7 +273,7 @@
 
 
 def forward_kernel(
-    counts,
+    table,
     cos,
     sin,
     normed_in,
@@ -279,49 +291,50 @@
     qkv,
     sem,
 ):
-    get_normed = pltpu.make_async_copy(normed_in, normed, sem.at[2])
+    get_normed = pltpu.make_async_copy(normed_in, normed, sem.at[7])
     get_normed.start()
 
-    def device(d, start):
-        n = counts[d]
-
-        def one(t, carry):
-            b = start + t
-
-            @pl.when(b < NQKV)
-            def _():
-                r = pl.multiple_of((b // 6) * BLK, BLK)
-                c = pl.multiple_of((b % 6) * BLK, BLK)
+    for pair in range(3):
+
+        def rows(r, carry, pair=pair):
+            for c in range(2):
+                slot = table[r * 6 + 2 * pair + c]
                 pltpu.make_async_copy(
-                    slots.at[d, :, t], wqkv.at[:, pl.ds(r, BLK), pl.ds(c, BLK)], sem.at[0]
+                    slots.at[:, slot],
+                    wqkv.at[pair, :, pl.ds(pl.multiple_of(r * BLK, BLK), BLK), c * BLK : (c + 1) * BLK],
+                    sem.at[pair],
                 ).start()
-
-            @pl.when(b >= NQKV)
-            def _():
-                e = b - NQKV
-                j = e % 32
-                r = pl.multiple_of((e // 32) * BLK, BLK)
-                c = pl.multiple_of((j % 8) * BLK, BLK)
-                pltpu.make_async_copy(
-                    slots.at[d, :, t],
-                    wout.at[j // 8, :, pl.ds(r, BLK), pl.ds(c, BLK)],
-                    sem.at[1],
-                ).start()
-
             return carry
 
-        lax.fori_loop(0, n, one, 0)
-        return start + n
-
-    lax.fori_loop(0, 32, device, 0)
+        lax.fori_loop(0, 32, rows, 0, unroll=4)
+
+    def project(pair):
+        pltpu.make_async_copy(wqkv.at[pair], wqkv.at[pair], sem.at[pair]).wait()
+        for tensor in (0, 1):
+            proj[tensor, :, pair * 256 : (pair + 1) * 256] = nn(normed[...], wqkv[pair, tensor])
+
     get_normed.wait()
-    pltpu.make_async_copy(wqkv, wqkv, sem.at[0]).wait()
-
-    for tensor in (0, 1):
-        for n in range(3):
-            cols = slice(n * 256, (n + 1) * 256)
-            proj[tensor, :, cols] = nn(normed[...], wqkv[tensor, :, cols])
-    pltpu.make_async_copy(wout, wout, sem.at[1]).wait()
+    project(0)
+
+    def out_rows(i, carry):
+        for j in range(32):
+            slot = table[NQKV + i * 32 + j]
+            pltpu.make_async_copy(
+                slots.at[:, slot],
+                wout.at[
+                    j // 8,
+                    :,
+                    pl.ds(pl.multiple_of(i * BLK, BLK), BLK),
+                    (j % 8) * BLK : (j % 8 + 1) * BLK,
+                ],
+                sem.at[3],
+            ).start()
+        return carry
+
+    lax.fori_loop(0, 4, out_rows, 0)
+    project(1)
+    project(2)
+    pltpu.make_async_copy(wout, wout, sem.at[3]).wait()
     save_wo = pltpu.make_async_copy(wout, wo_out, sem.at[6])
     save_wo.start()
 
@@ -338,7 +351,7 @@
 
     for h in range(QH + 2):
         qkv[:, h * HD : (h + 1) * HD] = head(0, h)
-    save_qkv = pltpu.make_async_copy(qkv, qkv_out, sem.at[3])
+    save_qkv = pltpu.make_async_copy(qkv, qkv_out, sem.at[8])
     save_qkv.start()
     k = qkv[:, QH * HD : (QH + 1) * HD]
     v = qkv[:, (QH + 1) * HD :]
@@ -370,7 +383,7 @@
         c.wait()
 
 
-def forward(counts, cos, sin, normed, slots):
+def forward(table, cos, sin, normed, slots):
     vmem = pl.BlockSpec(memory_space=pltpu.VMEM)
     hbm = pl.BlockSpec(memory_space=pl.ANY)
     smem = pl.BlockSpec(memory_space=pltpu.SMEM)
@@ -387,17 +400,17 @@
         out_specs=[hbm, hbm, hbm, hbm],
         scratch_shapes=[
             pltpu.VMEM((LEN, D), BF16),
-            pltpu.VMEM((2, D, QKV), BF16),
+            pltpu.VMEM((3, 2, D, 256), BF16),
             pltpu.VMEM((4, 2, OUT, CHUNK), BF16),
             pltpu.VMEM((2, LEN, QKV), F32),
             pltpu.VMEM((2, LEN, OUT), BF16),
             pltpu.VMEM((QH, LEN, LEN), BF16),
             pltpu.VMEM((LEN, QKV), BF16),
-            pltpu.SemaphoreType.DMA((7,)),
+            pltpu.SemaphoreType.DMA((9,)),
         ],
         compiler_params=pltpu.CompilerParams(vmem_limit_bytes=VMEM_LIMIT),
         name="forward",
-    )(counts, cos, sin, normed, slots)
+    )(table, cos, sin, normed, slots)
 
 
 FAR, NXT, PRV, OWN = 0, 1, 2, 3
@@ -408,7 +421,7 @@
     out,
     starts, sides, wo, curv, probs, qkv, normed,
     tan, opp, low, high, wt, dmix, dprojt, gb, sb,
-    acc, r_far, r_low, r_high, red, t_far, t_low, t_high, fin,
+    acc, r_far, r_low, r_high, red, t_far, t_low, t_high, fin, tot,
     send_sem, recv_sem, local_sem,
 ):
     me, core, y, z = place()
@@ -458,90 +471,112 @@
         sends.append(copy)
         return copy
 
-    half = LEN // 2
-    rows = (pl.ds(0, half), pl.ds(half, half))
-
-    def term(rel, part):
-        r = rows[part]
-        tan[rel, r] = (nn(sides[0, r], wo[rel, 0]) + nn(sides[1, r], wo[rel, 1])).astype(BF16)
-
-    loads[4].wait()
-    loads[FAR].wait()
-    term(FAR, 0)
-    a0 = send(tan.at[FAR, rows[0]], opp.at[0], up)
-    term(FAR, 1)
-    b0 = send(tan.at[FAR, rows[1]], opp.at[1], down)
-    loads[NXT].wait()
-    term(NXT, 1)
-    a1 = send(tan.at[NXT, rows[1]], low.at[1], up)
-    loads[PRV].wait()
-    term(PRV, 0)
-    b1 = send(tan.at[PRV, rows[0]], high.at[0], down)
-    term(NXT, 0)
-    term(PRV, 1)
-    loads[OWN].wait()
-    term(OWN, 0)
-    term(OWN, 1)
-    a0.wait_recv()
-    opp[0] = (opp[0].astype(F32) + tan[NXT, rows[0]].astype(F32)).astype(BF16)
-    a2 = send(opp.at[0], low.at[0], up)
-    b0.wait_recv()
-    opp[1] = (opp[1].astype(F32) + tan[PRV, rows[1]].astype(F32)).astype(BF16)
-    b2 = send(opp.at[1], high.at[1], down)
-    loads[5].wait()
-
     def prefix(d, s):
         starts[d] = s
         return s + counts[d]
 
     lax.fori_loop(0, 32, prefix, 0)
 
-    def weigh(part):
+    half = LEN // 2
+    rows = (pl.ds(0, half), pl.ds(half, half))
+
+    def term(rel, part, s):
         r = rows[part]
-        total = tan[OWN, r].astype(F32) + low[part].astype(F32) + high[part].astype(F32)
-        wt[OWN, r] = (total * curv[r].astype(F32)).astype(BF16)
-
-    def hand_on(src, dst, part, target):
-        return send(wt.at[src, rows[part]], wt.at[dst, rows[part]], target)
-
-    a1.wait_recv()
-    b2.wait_recv()
-    weigh(1)
-    c1 = hand_on(OWN, PRV, 1, up)
-    d1 = hand_on(OWN, NXT, 1, down)
-    b1.wait_recv()
-    a2.wait_recv()
-    weigh(0)
-    d0 = hand_on(OWN, NXT, 0, down)
-    c0 = hand_on(OWN, PRV, 0, up)
+        cols = slice(s * SUB, (s + 1) * SUB)
+        tan[rel, s, r] = (
+            nn(sides[0, r], wo[rel, 0, :, cols]) + nn(sides[1, r], wo[rel, 1, :, cols])
+        ).astype(BF16)
+
+    a0, a1, a2, b0, b1, b2 = {}, {}, {}, {}, {}, {}
+    loads[4].wait()
+    loads[FAR].wait()
+    for s in (0, 1):
+        term(FAR, 0, s)
+        a0[s] = send(tan.at[FAR, s, rows[0]], opp.at[0, s], up)
+        term(FAR, 1, s)
+        b0[s] = send(tan.at[FAR, s, rows[1]], opp.at[1, s], down)
+        if s == 0:
+            loads[NXT].wait()
+            term(NXT, 1, s)
+            a1[s] = send(tan.at[NXT, s, rows[1]], low.at[1, s], up)
+            loads[PRV].wait()
+            term(PRV, 0, s)
+            b1[s] = send(tan.at[PRV, s, rows[0]], high.at[0, s], down)
+    term(NXT, 0, 0)
+    term(PRV, 1, 0)
+    term(NXT, 1, 1)
+    term(PRV, 0, 1)
+    term(NXT, 0, 1)
+    term(PRV, 1, 1)
+    loads[OWN].wait()
+    for s in (0, 1):
+        for part in (0, 1):
+            term(OWN, part, s)
+    for s in (0, 1):
+        a0[s].wait_recv()
+        opp[0, s] = (opp[0, s].astype(F32) + tan[NXT, s, rows[0]].astype(F32)).astype(BF16)
+        a2[s] = send(opp.at[0, s], low.at[0, s], up)
+        b0[s].wait_recv()
+        opp[1, s] = (opp[1, s].astype(F32) + tan[PRV, s, rows[1]].astype(F32)).astype(BF16)
+        b2[s] = send(opp.at[1, s], high.at[1, s], down)
+        if s == 0:
+            a1[1] = send(tan.at[NXT, 1, rows[1]], low.at[1, 1], up)
+            b1[1] = send(tan.at[PRV, 1, rows[0]], high.at[0, 1], down)
+    loads[5].wait()
+
+    def weigh(part, s):
+        r = rows[part]
+        total = tan[OWN, s, r].astype(F32) + low[part, s].astype(F32) + high[part, s].astype(F32)
+        c = curv[r, s * SUB : (s + 1) * SUB].astype(F32)
+        wt[OWN, s, r] = (total * c).astype(BF16)
+
+    def hand_on(src, dst, part, s, target):
+        return send(wt.at[src, s, rows[part]], wt.at[dst, s, rows[part]], target)
 
     mixedt = sides[1].T
 
-    def consume(rel):
-        part = nt(wt[rel], wo[rel, 0])
-        if rel == OWN:
+    def consume(rel, s):
+        part = nt(wt[rel, s], wo[rel, 0, :, s * SUB : (s + 1) * SUB])
+        if rel == OWN and s == 0:
             dmix[...] = part
         else:
             dmix[...] += part
-        g = nn(mixedt, wt[rel]).astype(BF16)
+        g = nn(mixedt, wt[rel, s]).astype(BF16)
         for i in range(4):
-            for j in range(8):
-                gb[j % 2, NQKV // 2 + 16 * i + 4 * chunk[rel] + j // 2] = g[
+            for j in range(4):
+                gb[j % 2, NQKV // 2 + 16 * i + 4 * chunk[rel] + 2 * s + j // 2] = g[
                     i * BLK : (i + 1) * BLK, j * BLK : (j + 1) * BLK
                 ]
 
-    consume(OWN)
-    c1.wait_recv()
-    e1 = hand_on(PRV, FAR, 1, up)
-    d1.wait_recv()
-    d0.wait_recv()
-    e0 = hand_on(NXT, FAR, 0, down)
-    consume(NXT)
-    c0.wait_recv()
-    consume(PRV)
-    e1.wait_recv()
-    e0.wait_recv()
-    consume(FAR)
+    c0, c1, d0, d1, e0, e1 = {}, {}, {}, {}, {}, {}
+    for s in (0, 1):
+        a1[s].wait_recv()
+        b2[s].wait_recv()
+        weigh(1, s)
+        c1[s] = hand_on(OWN, PRV, 1, s, up)
+        d1[s] = hand_on(OWN, NXT, 1, s, down)
+        b1[s].wait_recv()
+        a2[s].wait_recv()
+        weigh(0, s)
+        d0[s] = hand_on(OWN, NXT, 0, s, down)
+        c0[s] = hand_on(OWN, PRV, 0, s, up)
+        if s == 0:
+            consume(OWN, 0)
+    for s in (0, 1):
+        c1[s].wait_recv()
+        e1[s] = hand_on(PRV, FAR, 1, s, up)
+        d0[s].wait_recv()
+        e0[s] = hand_on(NXT, FAR, 0, s, down)
+        if s == 0:
+            consume(OWN, 1)
+        d1[s].wait_recv()
+        consume(NXT, s)
+        c0[s].wait_recv()
+        consume(PRV, s)
+    for s in (0, 1):
+        e1[s].wait_recv()
+        e0[s].wait_recv()
+        consume(FAR, s)
     n_out = NB // 2 - NQKV // 2
     out_part = pl.ds(NQKV // 2, n_out)
     swap_out = send(gb.at[1 - core, out_part], sb.at[out_part], sib)
@@ -574,17 +609,7 @@
     dprojt[QH * HD : (QH + 1) * HD, :] = dk.T
     dprojt[(QH + 1) * HD :, :] = dvt.astype(BF16)
 
-    def add_sibling(base, count):
-        def step(i, carry):
-            b = base + i * 4
-            gb[core, pl.ds(b, 4)] = (
-                gb[core, pl.ds(b, 4)].astype(F32) + sb[pl.ds(b, 4)].astype(F32)
-            ).astype(BF16)
-            return carry
-
-        lax.fori_loop(0, count // 4, step, 0)
-
-    swaps = []
+    swaps = [swap_out]
     for n in range(8):
         cols = slice(n * 512, (n + 1) * 512)
         g = nn(dprojt[...], normed[:, cols]).astype(BF16)
@@ -595,11 +620,8 @@
                 ]
         piece = pl.ds(12 * n, 12)
         swaps.append(send(gb.at[1 - core, piece], sb.at[piece], sib))
-    swap_out.wait_recv()
-    add_sibling(NQKV // 2, n_out)
-    for n in range(8):
-        swaps[n].wait_recv()
-        add_sibling(12 * n, 12)
+    for copy in swaps:
+        copy.wait_recv()
 
     first = ("z", "y")
     second = ("y", "z")
@@ -608,92 +630,122 @@
 
     def fill(part, rel):
         f = wrap(here[first[part]] + steps[rel])
-
-        def step(s, carry):
-            if part == 0:
-                d = index_of(f, s, part)
-            else:
-                d = index_of(s, f, part)
+        for srel in range(4):
+            s = wrap(here[second[part]] + steps[srel])
+            d = index_of(f, s, part) if part == 0 else index_of(s, f, part)
             base = (starts[d] + 1 - core) // 2
             for i in range(HALF):
-                acc[part, rel, s, i] = gb[core, jnp.minimum(base + i, NB // 2 - 1)]
-            return carry
-
-        lax.fori_loop(0, 4, step, 0)
+                j = jnp.minimum(base + i, NB // 2 - 1)
+                acc[part, rel, srel, i] = (
+                    gb[core, j].astype(F32) + sb[j].astype(F32)
+                ).astype(BF16)
 
     lo, hi = pl.ds(0, 3), pl.ds(3, 3)
+    subs = (pl.ds(0, 1), pl.ds(1, 2), pl.ds(3, 1))
     a = {}
-    for part in (0, 1):
+
+    def go(part, name, u, src, dst, axis, step):
+        a[part, name, u] = send(src, dst, at(axis[part], step))
+
+    def send_far(part, u):
+        sub = subs[u]
+        go(part, "fu", u, acc.at[part, FAR, sub, lo], r_far.at[part, 0, sub], first, 1)
+        go(part, "fd", u, acc.at[part, FAR, sub, hi], r_far.at[part, 1, sub], first, -1)
+
+    def send_near(part, u):
+        sub = subs[u]
+        go(part, "lo1", u, acc.at[part, NXT, sub, hi], r_low.at[part, 1, sub], first, 1)
+        go(part, "hi0", u, acc.at[part, PRV, sub, lo], r_high.at[part, 0, sub], first, -1)
+
+    def middle(part, u):
+        sub = subs[u]
+        a[part, "fu", u].wait_recv()
+        r_far[part, 0, sub] = (
+            r_far[part, 0, sub].astype(F32) + acc[part, NXT, sub, lo].astype(F32)
+        ).astype(BF16)
+        go(part, "lo0", u, r_far.at[part, 0, sub], r_low.at[part, 0, sub], first, 1)
+        a[part, "fd", u].wait_recv()
+        r_far[part, 1, sub] = (
+            r_far[part, 1, sub].astype(F32) + acc[part, PRV, sub, hi].astype(F32)
+        ).astype(BF16)
+        go(part, "hi1", u, r_far.at[part, 1, sub], r_high.at[part, 1, sub], first, -1)
+
+    def reduce(part, u):
+        sub = subs[u]
+        for name in ("lo1", "hi0", "lo0", "hi1"):
+            a[part, name, u].wait_recv()
+        for h in (lo, hi):
+            which = 0 if h is lo else 1
+            red[part, sub, h] = (
+                acc[part, OWN, sub, h].astype(F32)
+                + r_low[part, which, sub].astype(F32)
+                + r_high[part, which, sub].astype(F32)
+            ).astype(BF16)
+
+    both = (0, 1)
+    for part in both:
         fill(part, FAR)
-        a[part, "fu"] = send(acc.at[part, FAR, :, lo], r_far.at[part, 0], at(first[part], 1))
-        a[part, "fd"] = send(acc.at[part, FAR, :, hi], r_far.at[part, 1], at(first[part], -1))
-    for part in (0, 1):
+        send_far(part, 0)
+    for part in both:
         fill(part, NXT)
-        a[part, "lo1"] = send(acc.at[part, NXT, :, hi], r_low.at[part, 1], at(first[part], 1))
-    for part in (0, 1):
         fill(part, PRV)
-        a[part, "hi0"] = send(acc.at[part, PRV, :, lo], r_high.at[part, 0], at(first[part], -1))
-    for part in (0, 1):
+        send_near(part, 0)
+    for part in both:
+        send_far(part, 1)
+        send_near(part, 1)
+    for part in both:
         fill(part, OWN)
-    for part in (0, 1):
-        for p, name, rel, span, name2, dst, step_to in (
-            (0, "fu", NXT, lo, "lo0", r_low, 1),
-            (1, "fd", PRV, hi, "hi1", r_high, -1),
-        ):
-            a[part, name].wait_recv()
-
-            def step(s, carry, part=part, p=p, rel=rel, span=span):
-                r_far[part, p, s] = (
-                    r_far[part, p, s].astype(F32) + acc[part, rel, s, span].astype(F32)
-                ).astype(BF16)
-                return carry
-
-            lax.fori_loop(0, 4, step, 0)
-            a[part, name2] = send(r_far.at[part, p], dst.at[part, p], at(first[part], step_to))
-    for part in (0, 1):
-        for name in ("lo1", "hi0", "lo0", "hi1"):
-            a[part, name].wait_recv()
-        for h in (0, 1):
-
-            def step3(s, carry, part=part, h=h):
-                red[part, s, pl.ds(3 * h, 3)] = (
-                    acc[part, OWN, s, pl.ds(3 * h, 3)].astype(F32)
-                    + r_low[part, h, s].astype(F32)
-                    + r_high[part, h, s].astype(F32)
-                ).astype(BF16)
-                return carry
-
-            lax.fori_loop(0, 4, step3, 0)
-        s_here = here[second[part]]
-        far, nxt, prv = wrap(s_here + 2), wrap(s_here + 1), wrap(s_here - 1)
-        to_up, to_down = at(second[part], 1), at(second[part], -1)
-        a[part, "tu"] = send(red.at[part, far, lo], t_far.at[part, 0], to_up)
-        a[part, "td"] = send(red.at[part, far, hi], t_far.at[part, 1], to_down)
-        a[part, "tl1"] = send(red.at[part, nxt, hi], t_low.at[part, 1], to_up)
-        a[part, "th0"] = send(red.at[part, prv, lo], t_high.at[part, 0], to_down)
-    for part in (0, 1):
-        s_here = here[second[part]]
-        nxt, prv = wrap(s_here + 1), wrap(s_here - 1)
-        to_up, to_down = at(second[part], 1), at(second[part], -1)
-        a[part, "tu"].wait_recv()
-        t_far[part, 0] = (t_far[part, 0].astype(F32) + red[part, nxt, lo].astype(F32)).astype(BF16)
-        a[part, "tl0"] = send(t_far.at[part, 0], t_low.at[part, 0], to_up)
-        a[part, "td"].wait_recv()
-        t_far[part, 1] = (t_far[part, 1].astype(F32) + red[part, prv, hi].astype(F32)).astype(BF16)
-        a[part, "th1"] = send(t_far.at[part, 1], t_high.at[part, 1], to_down)
-    for part in (0, 1):
-        s_here = here[second[part]]
+    for part in both:
+        middle(part, 0)
+    for part in both:
+        send_far(part, 2)
+        send_near(part, 2)
+    for part in both:
+        middle(part, 1)
+    for part in both:
+        reduce(part, 0)
+        go(part, "tu", 0, red.at[part, FAR, lo], t_far.at[part, 0], second, 1)
+        go(part, "td", 0, red.at[part, FAR, hi], t_far.at[part, 1], second, -1)
+    for part in both:
+        middle(part, 2)
+    for part in both:
+        reduce(part, 1)
+        go(part, "tl1", 0, red.at[part, NXT, hi], t_low.at[part, 1], second, 1)
+        go(part, "th0", 0, red.at[part, PRV, lo], t_high.at[part, 0], second, -1)
+    for part in both:
+        a[part, "tu", 0].wait_recv()
+        t_far[part, 0] = (
+            t_far[part, 0].astype(F32) + red[part, NXT, lo].astype(F32)
+        ).astype(BF16)
+        go(part, "tl0", 0, t_far.at[part, 0], t_low.at[part, 0], second, 1)
+        a[part, "td", 0].wait_recv()
+        t_far[part, 1] = (
+            t_far[part, 1].astype(F32) + red[part, PRV, hi].astype(F32)
+        ).astype(BF16)
+        go(part, "th1", 0, t_far.at[part, 1], t_high.at[part, 1], second, -1)
+    for part in both:
+        reduce(part, 2)
+    for part in both:
         for name in ("tl1", "th0", "tl0", "th1"):
-            a[part, name].wait_recv()
+            a[part, name, 0].wait_recv()
         for h in (0, 1):
             fin[part, pl.ds(3 * h, 3)] = (
-                red[part, s_here, pl.ds(3 * h, 3)].astype(F32)
+                red[part, OWN, pl.ds(3 * h, 3)].astype(F32)
                 + t_low[part, h].astype(F32)
                 + t_high[part, h].astype(F32)
             )
-    last = send(fin.at[1 - core], out.at[core], sib)
-    out[core] = fin[core]
+    last = send(fin.at[1 - core], tot.at[core], sib)
+    tot[core] = fin[core]
     last.wait_recv()
+
+    start, n = starts[me], counts[me]
+    factor = 1.0 / np.sqrt(np.float32(LEN * 32))
+    for t in range(SLOTS):
+        b = start + t
+        parity = lax.rem(b, 2)
+        v = tot[parity, b // 2 - (start + 1 - parity) // 2] * factor
+        v = jnp.where(b < NQKV, v.T, v)
+        out[t] = jnp.where(t < n, v, 0.0)
     for copy in sends:
         copy.wait_send()
 
@@ -707,7 +759,7 @@
     v = pltpu.VMEM
     return pl.pallas_call(
         main_kernel,
-        out_shape=jax.ShapeDtypeStruct((2, HALF) + block, F32),
+        out_shape=jax.ShapeDtypeStruct((SLOTS,) + block, F32),
         in_specs=[smem, vmem, vmem] + [hbm] * 6,
         out_specs=vmem,
         scratch_shapes=[
@@ -718,11 +770,11 @@
             v((QH, LEN, LEN), BF16),
             v((LEN, QKV), BF16),
             v((LEN, D), BF16),
-            v((4, LEN, CHUNK), BF16),
-            v((2, half, CHUNK), BF16),
-            v((2, half, CHUNK), BF16),
-            v((2, half, CHUNK), BF16),
-            v((4, LEN, CHUNK), BF16),
+            v((4, 2, LEN, SUB), BF16),
+            v((2, 2, half, SUB), BF16),
+            v((2, 2, half, SUB), BF16),
+            v((2, 2, half, SUB), BF16),
+            v((4, 2, LEN, SUB), BF16),
             v((LEN, OUT), F32),
             v((QKV, LEN), BF16),
             v((2, NB // 2) + block, BF16),
@@ -736,8 +788,9 @@
             v((2, 2, 3) + block, BF16),
             v((2, 2, 3) + block, BF16),
             v((2, HALF) + block, F32),
-            pltpu.SemaphoreType.DMA((64,)),
-            pltpu.SemaphoreType.DMA((64,)),
+            v((2, HALF) + block, F32),
+            pltpu.SemaphoreType.DMA((82,)),
+            pltpu.SemaphoreType.DMA((82,)),
             pltpu.SemaphoreType.DMA((9,)),
         ],
         compiler_params=pltpu.CompilerParams(
@@ -747,42 +800,15 @@
     )(counts, cos, sin, sides, wo, curv, probs, qkv, normed)
 
 
-def finish_kernel(counts, total, out):
-    me = lax.axis_index("fsdp")
-    start = lax.fori_loop(0, me, lambda d, s: s + counts[d], 0)
-    n = counts[me]
-    factor = 1.0 / np.sqrt(np.float32(LEN * 32))
-
-    def one(t, carry):
-        b = start + t
-        parity = b % 2
-        x = total[parity, b // 2 - (start + 1 - parity) // 2] * factor
-        x = jnp.where(b < NQKV, x.T, x)
-        out[t] = jnp.where(t < n, x, 0.0)
-        return carry
-
-    lax.fori_loop(0, SLOTS, one, 0)
-
-
-def finish(counts, total):
-    vmem = pl.BlockSpec(memory_space=pltpu.VMEM)
-    smem = pl.BlockSpec(memory_space=pltpu.SMEM)
-    return pl.pallas_call(
-        finish_kernel,
-        out_shape=jax.ShapeDtypeStruct((SLOTS, BLK, BLK), F32),
-        in_specs=[smem, vmem],
-        out_specs=vmem,
-        name="finish",
-    )(counts, total)
-
-
 def local(tokens, norm_gain, curvature, weight_slots, probe_slots, block_counts):
     counts = block_counts[0]
     cos, sin = tables()
-    slots, normed = gather(weight_slots[0], probe_slots[0], tokens[0], norm_gain.reshape(1, D))
-    qkv, sides, probs, wo = forward(counts, cos, sin, normed, slots)
-    total = main(counts, cos, sin, sides, wo, curvature[0], probs, qkv, normed)
-    return finish(counts, total)[None]
+    slots, normed, table = gather(
+        counts, weight_slots[0], probe_slots[0], tokens[0], norm_gain.reshape(1, D)
+    )
+    qkv, sides, probs, wo = forward(table.reshape(1024), cos, sin, normed, slots)
+    out = main(counts, cos, sin, sides, wo, curvature[0], probs, qkv, normed)
+    return out[None]
 
 
 def solution(mesh):

time: 239 us -> 224 us (0.937)
  Pallas kernels: 239 us -> 221 us
    pallas_call x3 -> x2, Pallas kernels: 212 us -> 203 us  [the longest x1 124 us: main(): pl.pallas_call(main_kernel, out_shape=jax.ShapeDtypeStruct((SLOTS,) + blo...]
    pallas_call x1, Pallas kernels: 26.9 us -> 18.4 us  [forward(): pl.pallas_call(forward_kernel, out_shape=[shape((LEN, QKV), BF16), shape(...]
where the time goes in v3:
time: 224 us; the launch traced here: 223 us
  Pallas kernels  221 us (99%)
    pallas_call x1, Pallas kernels, main(): pl.pallas_call(main_kernel, out_shape=jax.ShapeDtypeStruct((SLOTS,) + blo...  124 us
    pallas_call x1, Pallas kernels, gather(): pl.pallas_call(gather_kernel, out_shape=[jax.ShapeDtypeStruct((2, 32 * SL...  78.6 us
    pallas_call x1, Pallas kernels, forward(): pl.pallas_call(forward_kernel, out_shape=[shape((LEN, QKV), BF16), shape(...  18.4 us

profile of v3, /device:TPU:1, one launch (start us, length us, event | category | flops | bytes accessed | tf_op | source)
XLA Modules:
  0.0 223.4 jit_solution(10069739600950888116)
XLA Ops:
  0.0 78.6 %gather.1 = (bf16[2,384,128,128]{3,2,1,0:T(8,128)(2,1)}, bf16[512,4096]{1,0:T(8,128)(2,1)}, s32[8,128]{1,0:T(8,128)}) custom-call(s32[32]{0:T(128)} %bitcast.15, bf16[12,128,128]{2,1,0:T(8,128)(2,1)} %bitcast.11, bf16[12,128,128]{2,1,0:T(8,128)(2,1)} %bitcast.12, bf16[512,4096]{1,0:T(8,128)(2,1)} %bitcast.8, f32[1,4096]{1,0:T(1,128)} %bitcast.13), custom_call_target="tpu_custom_call" | custom-call | tf_op jit(solution)/shard_map/gather/pallas_call | solution.py:238
  78.6 18.4 %forward.1 = (bf16[512,768]{1,0:T(8,128)(2,1)}, bf16[2,512,512]{2,1,0:T(8,128)(2,1)}, bf16[4,512,512]{2,1,0:T(8,128)(2,1)}, bf16[4,2,512,1024]{3,2,1,0:T(8,128)(2,1)}) custom-call(s32[1024]{0:T(1024)} %bitcast.14, f32[512,128]{1,0:T(8,128)} %constant.4.clone.cos, f32[512,128]{1,0:T(8,128)} %constant.5.clone.sin, ...), custom_call_target="tpu_custom_call" | custom-call | tf_op jit(solution)/shard_map/forward/pallas_call | solution.py:391
  97.1 124.3 %main.1 = f32[12,128,128]{2,1,0:T(8,128)} custom-call(s32[32]{0:T(128)} %bitcast.16, f32[512,128]{1,0:T(8,128)} %constant.4.clone.cos, f32[512,128]{1,0:T(8,128)} %constant.5.clone.sin, bf16[2,512,512]{2,1,0:T(8,128)(2,1)} %get-tuple-element.15.sides_in, bf16[4,2,512,1024]{3,2,1,0:T(8,128)(2,1)} %get-tuple-element.16.wo_in, bf16[512,4096]{1,0:T(8,128)(2,1)} %bitcast.9, ...), custom_call_target="tpu_custom_call" | custom-call | tf_op jit(solution)/shard_map/main/pallas_call | solution.py:760
  221.4 2.1 copy.10

commit v4 on v3

--- a/solution.py
+++ b/solution.py
@@ -64,37 +64,62 @@
     pl.semaphore_wait(barrier, len(targets))
 
 
-def gather_kernel(
-    counts, w_ref, p_ref, tokens_in, gain, out_ref, normed_out, table,
-    tokens, normed, send_sem, recv_sem, local_sem,
+def nt(a, b):
+    return lax.dot_general(a, b, (((1,), (1,)), ((), ())), preferred_element_type=F32)
+
+
+def nn(a, b):
+    return jnp.dot(a, b, preferred_element_type=F32)
+
+
+def causal_mask():
+    row = lax.broadcasted_iota(jnp.int32, (LEN, LEN), 0)
+    col = lax.broadcasted_iota(jnp.int32, (LEN, LEN), 1)
+    return row >= col
+
+
+def forward_kernel(
+    counts, w_ref, p_ref, gain, tokens_in, cos_in, sin_in,
+    normed_out, qkv_out, sides_out, probs_out, wo_out,
+    table, slots_w, slots_p, normed, cos, sin, wqkv, pqkv, wout, proj, sides, probs, qkv,
+    send_sem, recv_sem, local_sem,
 ):
     me, core, y, z = place()
-    get_tokens = pltpu.make_async_copy(tokens_in, tokens, local_sem.at[2])
-    get_tokens.start()
-    sib = index_of(z, y, 1 - core)
+    sib = {"fsdp": index_of(z, y, 1 - core)}
 
     def at(axis, step):
         if axis == "y":
             return {"fsdp": index_of(z, wrap(y + step), core)}
         return {"fsdp": index_of(wrap(z + step), y, core)}
 
-    greet([at("y", 1), at("y", -1), at("z", 1), at("z", -1), {"fsdp": sib}])
-
-    own = [
-        pltpu.make_async_copy(w_ref, out_ref.at[0, pl.ds(me * SLOTS, SLOTS)], local_sem.at[0]),
-        pltpu.make_async_copy(p_ref, out_ref.at[1, pl.ds(me * SLOTS, SLOTS)], local_sem.at[1]),
+    my_slots = pl.ds(me * SLOTS, SLOTS)
+    local = [
+        pltpu.make_async_copy(a, b, local_sem.at[i])
+        for i, (a, b) in enumerate(
+            (
+                (tokens_in, normed),
+                (cos_in, cos),
+                (sin_in, sin),
+                (w_ref, slots_w.at[my_slots]),
+                (p_ref, slots_p.at[my_slots]),
+            )
+        )
     ]
-    for c in own:
-        c.start()
-
+    for copy in local:
+        copy.start()
+    greet([at("y", 1), at("y", -1), at("z", 1), at("z", -1), sib])
+
+    first = ("y", "z", "y", "z")
+    second = ("z", "y", "z", "y")
+    mine = (w_ref, w_ref, p_ref, p_ref)
+    landed = (slots_w, slots_w, slots_p, slots_p)
     counter = [0]
     sends = []
-
-    def sem():
+    arrivals = {}
+
+    def send(key, src, dst, target):
+        number = counter[0]
         counter[0] += 1
-        return counter[0] - 1
-
-    def send(src, dst, number, target):
         copy = pltpu.make_async_remote_copy(
             src_ref=src,
             dst_ref=dst,
@@ -105,312 +130,280 @@
         )
         copy.start()
         sends.append(copy)
-        return copy
-
-    def piece(tensor, origin, part=None):
-        if part is None:
-            return out_ref.at[tensor, pl.ds(origin * SLOTS, SLOTS)]
-        return out_ref.at[tensor, pl.ds(origin * SLOTS + part * HALF, HALF)]
-
-    first = ("y", "z")
-    second = ("z", "y")
-
-    def origin_of(tensor, f, s):
-        if tensor == 0:
+        arrivals[key] = copy
+
+    def span(p, side):
+        start = (p % 2) * HALF
+        return (start, HALF) if side is None else (start + 3 * side, 3)
+
+    def piece(p, origin, side=None):
+        start, size = span(p, side)
+        return landed[p].at[pl.ds(origin * SLOTS + start, size)]
+
+    def origin_of(p, f, s):
+        if p % 2 == 0:
             return index_of(wrap(z + s), wrap(y + f), core)
         return index_of(wrap(z + f), wrap(y + s), core)
 
-    number = {}
-    for tensor in (0, 1):
-        for role in ("f+", "f-", "fa", "fb"):
-            number[tensor, role] = sem()
-        for f in (0, 1, -1, 2):
-            for role in ("s+", "s-", "sa", "sb"):
-                number[tensor, role, f] = sem()
-        for f in (0, 1, -1, 2):
-            for s in (0, 1, -1, 2):
-                number[tensor, "sib", f, s] = sem()
-
-    arrivals = {}
-
-    def go(tensor, role, src_origin, axis, step, part=None, src=None):
-        ref = piece(tensor, src_origin, part)
-        copy = send(ref if src is None else src, ref, number[(tensor,) + role], at(axis, step))
-        arrivals[(tensor,) + role] = copy
-
-    def to_sib(tensor, f, s, src=None):
-        origin = origin_of(tensor, f, s)
-        ref = piece(tensor, origin)
-        copy = send(ref if src is None else src, ref, number[tensor, "sib", f, s], {"fsdp": sib})
-        arrivals[tensor, "sib", f, s] = copy
-
-    mine = (w_ref, p_ref)
-    for tensor in (0, 1):
-        go(tensor, ("f+",), me, first[tensor], 1, src=mine[tensor])
-        go(tensor, ("f-",), me, first[tensor], -1, src=mine[tensor])
-    for tensor in (0, 1):
-        go(tensor, ("s+", 0), me, second[tensor], 1, src=mine[tensor])
-        go(tensor, ("s-", 0), me, second[tensor], -1, src=mine[tensor])
-    for tensor in (0, 1):
-        to_sib(tensor, 0, 0, src=mine[tensor])
-
-    b = lax.broadcasted_iota(jnp.int32, (8, 128), 0) * 128 + lax.broadcasted_iota(
-        jnp.int32, (8, 128), 1
-    )
-    slot, end = b, 0
-    for d in range(32):
-        end = end + counts[d]
-        slot = slot + jnp.where(b >= end, SLOTS - counts[d], 0)
-    table[...] = slot
-    get_tokens.wait()
+    def go(p, role, f, s, axis, step, side=None):
+        ref = piece(p, origin_of(p, f, s), side)
+        src = ref
+        if f == 0 and s == 0:
+            src = mine[p].at[pl.ds(*span(p, side))]
+        send((p,) + role, src, ref, at(axis[p], step))
+
+    def to_sib(p, f, s):
+        ref = piece(p, origin_of(p, f, s))
+        src = ref
+        if f == 0 and s == 0:
+            src = mine[p].at[pl.ds(*span(p, None))]
+        send((p, "sib", f, s), src, ref, sib)
+
+    def got(*key):
+        arrivals[key].wait_recv()
+
+    def begin(parts):
+        for p in parts:
+            go(p, ("f+",), 0, 0, first, 1)
+            go(p, ("f-",), 0, 0, first, -1)
+        for p in parts:
+            go(p, ("s+", 0), 0, 0, second, 1)
+            go(p, ("s-", 0), 0, 0, second, -1)
+        for p in parts:
+            to_sib(p, 0, 0)
+
+    def neighbours(p):
+        got(p, "f+")
+        go(p, ("fa",), -1, 0, first, 1, 0)
+        go(p, ("s+", -1), -1, 0, second, 1)
+        go(p, ("s-", -1), -1, 0, second, -1)
+        got(p, "f-")
+        go(p, ("fb",), 1, 0, first, -1, 1)
+        go(p, ("s+", 1), 1, 0, second, 1)
+        go(p, ("s-", 1), 1, 0, second, -1)
+        to_sib(p, -1, 0)
+        to_sib(p, 1, 0)
+
+    def pass_on(p, f):
+        got(p, "s+", f)
+        go(p, ("sa", f), f, -1, second, 1, 0)
+        to_sib(p, f, -1)
+        got(p, "s-", f)
+        go(p, ("sb", f), f, 1, second, -1, 1)
+        to_sib(p, f, 1)
+
+    def opposite(p):
+        got(p, "fa")
+        got(p, "fb")
+        go(p, ("s+", 2), 2, 0, second, 1)
+        go(p, ("s-", 2), 2, 0, second, -1)
+        to_sib(p, 2, 0)
+
+    def corner(p, f):
+        got(p, "sa", f)
+        got(p, "sb", f)
+        to_sib(p, f, 2)
+
+    def sibling_done(parts):
+        for p in parts:
+            for f in (0, -1, 1, 2):
+                for s in (0, -1, 1, 2):
+                    got(p, "sib", f, s)
+
+    w, pr = (0, 1), (2, 3)
+    begin(w)
+
+    def locate(b, carry):
+        d, t = carry
+        table[b] = d * SLOTS + t
+        more = t + 1 < counts[d]
+        return jnp.where(more, d, jnp.minimum(d + 1, 31)), jnp.where(more, t + 1, 0)
+
+    lax.fori_loop(0, NB, locate, (0, 0))
+    local[0].wait()
 
     def norm(i, carry):
         rows = pl.ds(pl.multiple_of(i * 32, 32), 32)
-        x = tokens[rows, :].astype(F32)
+        x = normed[rows, :].astype(F32)
         factor = lax.rsqrt(jnp.mean(x * x, axis=-1, keepdims=True) + EPS)
         normed[rows, :] = (x * factor * gain[...]).astype(BF16)
         return carry
 
     lax.fori_loop(0, LEN // 32, norm, 0)
-    own.append(pltpu.make_async_copy(normed, normed_out, local_sem.at[3]))
-    own[-1].start()
-
-    for tensor in (0, 1):
-        arrivals[tensor, "f+"].wait_recv()
-        lower = origin_of(tensor, -1, 0)
-        go(tensor, ("fa",), lower, first[tensor], 1, part=0)
-        go(tensor, ("s+", -1), lower, second[tensor], 1)
-        go(tensor, ("s-", -1), lower, second[tensor], -1)
-        arrivals[tensor, "f-"].wait_recv()
-        upper = origin_of(tensor, 1, 0)
-        go(tensor, ("fb",), upper, first[tensor], -1, part=1)
-        go(tensor, ("s+", 1), upper, second[tensor], 1)
-        go(tensor, ("s-", 1), upper, second[tensor], -1)
-        to_sib(tensor, -1, 0)
-        to_sib(tensor, 1, 0)
-
-    def pass_on(tensor, f):
-        arrivals[tensor, "s+", f].wait_recv()
-        go(tensor, ("sa", f), origin_of(tensor, f, -1), second[tensor], 1, part=0)
-        to_sib(tensor, f, -1)
-        arrivals[tensor, "s-", f].wait_recv()
-        go(tensor, ("sb", f), origin_of(tensor, f, 1), second[tensor], -1, part=1)
-        to_sib(tensor, f, 1)
-
-    for tensor in (0, 1):
-        pass_on(tensor, 0)
-    for tensor in (0, 1):
-        arrivals[tensor, "fa"].wait_recv()
-        arrivals[tensor, "fb"].wait_recv()
-        far = origin_of(tensor, 2, 0)
-        go(tensor, ("s+", 2), far, second[tensor], 1)
-        go(tensor, ("s-", 2), far, second[tensor], -1)
-        to_sib(tensor, 2, 0)
-    for f in (-1, 1, 2):
-        for tensor in (0, 1):
-            pass_on(tensor, f)
-            if f == -1:
-                g = 0
-            elif f == 1:
-                g = -1
-            else:
-                g = 1
-            arrivals[tensor, "sa", g].wait_recv()
-            arrivals[tensor, "sb", g].wait_recv()
-            to_sib(tensor, g, 2)
-    for tensor in (0, 1):
-        arrivals[tensor, "sa", 2].wait_recv()
-        arrivals[tensor, "sb", 2].wait_recv()
-        to_sib(tensor, 2, 2)
-    for key, copy in arrivals.items():
-        if key[1] == "sib":
-            copy.wait_recv()
-    for c in own:
-        c.wait()
+    saves = [pltpu.make_async_copy(normed, normed_out, local_sem.at[5])]
+    saves[-1].start()
+    for i in (1, 2, 3, 4):
+        local[i].wait()
+
+    def cols_of(h):
+        return pl.ds(h * HD if isinstance(h, int) else pl.multiple_of(h * HD, HD), HD)
+
+    def assemble_qkv(src, dst, start, stop):
+        def step(r, carry):
+            rows = pl.ds(pl.multiple_of(r * BLK, BLK), BLK)
+            for c in range(6):
+                dst[rows, c * BLK : (c + 1) * BLK] = src[table[r * 6 + c]]
+            return carry
+
+        lax.fori_loop(start, stop, step, 0)
+
+    def assemble_out(src, tensor):
+        def step(i, carry):
+            rows = pl.ds(pl.multiple_of(i * BLK, BLK), BLK)
+            for j in range(32):
+                wout[tensor, j // 8, rows, (j % 8) * BLK : (j % 8 + 1) * BLK] = src[
+                    table[NQKV + i * 32 + j]
+                ]
+            return carry
+
+        lax.fori_loop(0, 4, step, 0)
+        saves.append(
+            pltpu.make_async_copy(wout.at[tensor], wo_out.at[tensor], local_sem.at[6 + tensor])
+        )
+        saves[-1].start()
+
+    def project(matrix, n):
+        cols = slice(n * 256, (n + 1) * 256)
+        proj[:, cols] = nn(normed[...], matrix[:, cols])
+
+    def head(h, turn=True):
+        x = proj[:, cols_of(h)]
+        if turn:
+            x = x * cos[...] + pltpu.roll(x, 64, 1) * sin[...]
+        return x.astype(BF16)
+
+    def heads():
+        for h in range(QH + 2):
+            qkv[:, cols_of(h)] = head(h, h < QH + 1)
+        saves.append(pltpu.make_async_copy(qkv, qkv_out, local_sem.at[8]))
+        saves[-1].start()
+
+    scale = HD**-0.5
+
+    def primal(h, carry):
+        k = qkv[:, cols_of(QH)]
+        v = qkv[:, cols_of(QH + 1)]
+        s = jnp.where(causal_mask(), nt(qkv[:, cols_of(h)], k) * scale, NEGATIVE)
+        m = jnp.max(s, axis=-1, keepdims=True)
+        e = jnp.exp(s - m)
+        p = (e * (1.0 / jnp.sum(e, axis=-1, keepdims=True))).astype(BF16)
+        probs[h] = p
+        sides[1, :, cols_of(h)] = nn(p, v).astype(BF16)
+        return carry
+
+    neighbours(0)
+    neighbours(1)
+    pass_on(0, 0)
+    pass_on(1, 0)
+    opposite(0)
+    opposite(1)
+    begin(pr)
+    for f, g in ((-1, 0), (1, -1), (2, 1)):
+        for p in w:
+            pass_on(p, f)
+            corner(p, g)
+    neighbours(2)
+    neighbours(3)
+    corner(0, 2)
+    corner(1, 2)
+    pass_on(2, 0)
+    pass_on(3, 0)
+    sibling_done(w)
+    assemble_qkv(slots_w, wqkv, 0, 32)
+    opposite(2)
+    opposite(3)
+    project(wqkv, 0)
+    pass_on(2, -1)
+    pass_on(3, -1)
+    project(wqkv, 1)
+    corner(2, 0)
+    corner(3, 0)
+    project(wqkv, 2)
+    pass_on(2, 1)
+    pass_on(3, 1)
+    heads()
+    corner(2, -1)
+    corner(3, -1)
+    lax.fori_loop(0, 2, primal, 0)
+    pass_on(2, 2)
+    pass_on(3, 2)
+    lax.fori_loop(2, 4, primal, 0)
+    corner(2, 1)
+    corner(3, 1)
+    saves.append(pltpu.make_async_copy(probs, probs_out, local_sem.at[9]))
+    saves[-1].start()
+    assemble_out(slots_w, 0)
+    corner(2, 2)
+    corner(3, 2)
+    sibling_done(pr)
+
+    assemble_qkv(slots_p, pqkv, 0, 32)
+    for n in range(3):
+        project(pqkv, n)
+    assemble_out(slots_p, 1)
+    k = qkv[:, cols_of(QH)]
+    v = qkv[:, cols_of(QH + 1)]
+    keys = jnp.concatenate([k, head(QH)], axis=1)
+    values = head(QH + 1, False)
+
+    def tangent(h, carry):
+        pb = probs[h]
+        p = pb.astype(F32)
+        ts = nt(jnp.concatenate([head(h), qkv[:, cols_of(h)]], axis=1), keys) * scale
+        pt = p * ts
+        tp = pt - p * jnp.sum(pt, axis=-1, keepdims=True)
+        sides[0, :, cols_of(h)] = (nn(tp.astype(BF16), v) + nn(pb, values)).astype(BF16)
+        return carry
+
+    lax.fori_loop(0, QH, tangent, 0)
+    saves.append(pltpu.make_async_copy(sides, sides_out, local_sem.at[10]))
+    saves[-1].start()
+    for copy in saves:
+        copy.wait()
     for copy in sends:
         copy.wait_send()
 
 
-def gather(counts, w, p, tokens, gain):
-    vmem = pl.BlockSpec(memory_space=pltpu.VMEM)
-    hbm = pl.BlockSpec(memory_space=pl.ANY)
-    smem = pl.BlockSpec(memory_space=pltpu.SMEM)
-    return pl.pallas_call(
-        gather_kernel,
-        out_shape=[
-            jax.ShapeDtypeStruct((2, 32 * SLOTS, BLK, BLK), BF16),
-            jax.ShapeDtypeStruct((LEN, D), BF16),
-            jax.ShapeDtypeStruct((8, 128), jnp.int32),
-        ],
-        in_specs=[smem, vmem, vmem, hbm, vmem],
-        out_specs=[hbm, hbm, vmem],
-        scratch_shapes=[
-            pltpu.VMEM((LEN, D), BF16),
-            pltpu.VMEM((LEN, D), BF16),
-            pltpu.SemaphoreType.DMA((72,)),
-            pltpu.SemaphoreType.DMA((72,)),
-            pltpu.SemaphoreType.DMA((4,)),
-        ],
-        compiler_params=pltpu.CompilerParams(
-            collective_id=0, has_side_effects=True, vmem_limit_bytes=VMEM_LIMIT
-        ),
-        name="gather",
-    )(counts, w, p, tokens, gain)
-
-
-def nt(a, b):
-    return lax.dot_general(a, b, (((1,), (1,)), ((), ())), preferred_element_type=F32)
-
-
-def nn(a, b):
-    return jnp.dot(a, b, preferred_element_type=F32)
-
-
-def causal_mask():
-    row = lax.broadcasted_iota(jnp.int32, (LEN, LEN), 0)
-    col = lax.broadcasted_iota(jnp.int32, (LEN, LEN), 1)
-    return row >= col
-
-
-def forward_kernel(
-    table,
-    cos,
-    sin,
-    normed_in,
-    slots,
-    qkv_out,
-    sides_out,
-    probs_out,
-    wo_out,
-    normed,
-    wqkv,
-    wout,
-    proj,
-    sides,
-    probs,
-    qkv,
-    sem,
-):
-    get_normed = pltpu.make_async_copy(normed_in, normed, sem.at[7])
-    get_normed.start()
-
-    for pair in range(3):
-
-        def rows(r, carry, pair=pair):
-            for c in range(2):
-                slot = table[r * 6 + 2 * pair + c]
-                pltpu.make_async_copy(
-                    slots.at[:, slot],
-                    wqkv.at[pair, :, pl.ds(pl.multiple_of(r * BLK, BLK), BLK), c * BLK : (c + 1) * BLK],
-                    sem.at[pair],
-                ).start()
-            return carry
-
-        lax.fori_loop(0, 32, rows, 0, unroll=4)
-
-    def project(pair):
-        pltpu.make_async_copy(wqkv.at[pair], wqkv.at[pair], sem.at[pair]).wait()
-        for tensor in (0, 1):
-            proj[tensor, :, pair * 256 : (pair + 1) * 256] = nn(normed[...], wqkv[pair, tensor])
-
-    get_normed.wait()
-    project(0)
-
-    def out_rows(i, carry):
-        for j in range(32):
-            slot = table[NQKV + i * 32 + j]
-            pltpu.make_async_copy(
-                slots.at[:, slot],
-                wout.at[
-                    j // 8,
-                    :,
-                    pl.ds(pl.multiple_of(i * BLK, BLK), BLK),
-                    (j % 8) * BLK : (j % 8 + 1) * BLK,
-                ],
-                sem.at[3],
-            ).start()
-        return carry
-
-    lax.fori_loop(0, 4, out_rows, 0)
-    project(1)
-    project(2)
-    pltpu.make_async_copy(wout, wout, sem.at[3]).wait()
-    save_wo = pltpu.make_async_copy(wout, wo_out, sem.at[6])
-    save_wo.start()
-
-    c2, s2 = cos[...], sin[...]
-
-    def rot(x):
-        return x * c2 + pltpu.roll(x, 64, 1) * s2
-
-    def head(tensor, h):
-        x = proj[tensor, :, h * HD : (h + 1) * HD]
-        if h < QH + 1:
-            x = rot(x)
-        return x.astype(BF16)
-
-    for h in range(QH + 2):
-        qkv[:, h * HD : (h + 1) * HD] = head(0, h)
-    save_qkv = pltpu.make_async_copy(qkv, qkv_out, sem.at[8])
-    save_qkv.start()
-    k = qkv[:, QH * HD : (QH + 1) * HD]
-    v = qkv[:, (QH + 1) * HD :]
-    keys = jnp.concatenate([k, head(1, QH)], axis=1)
-    values = jnp.concatenate([v, head(1, QH + 1)], axis=1)
-    causal = causal_mask()
-    scale = HD**-0.5
-    for h in range(QH):
-        q = qkv[:, h * HD : (h + 1) * HD]
-        tq = head(1, h)
-        s = jnp.where(causal, nt(q, k) * scale, NEGATIVE)
-        m = jnp.max(s, axis=-1, keepdims=True)
-        e = jnp.exp(s - m)
-        p = e * (1.0 / jnp.sum(e, axis=-1, keepdims=True))
-        ts = nt(jnp.concatenate([tq, q], axis=1), keys) * scale
-        pt = p * ts
-        tp = pt - p * jnp.sum(pt, axis=-1, keepdims=True)
-        pb = p.astype(BF16)
-        probs[h] = pb
-        both = nn(pb, values)
-        mixed_t = nn(tp.astype(BF16), v) + both[:, HD:]
-        sides[0, :, h * HD : (h + 1) * HD] = mixed_t.astype(BF16)
-        sides[1, :, h * HD : (h + 1) * HD] = both[:, :HD].astype(BF16)
-    save_probs = pltpu.make_async_copy(probs, probs_out, sem.at[4])
-    save_probs.start()
-    save_sides = pltpu.make_async_copy(sides, sides_out, sem.at[5])
-    save_sides.start()
-    for c in (save_wo, save_qkv, save_probs, save_sides):
-        c.wait()
-
-
-def forward(table, cos, sin, normed, slots):
+def forward(counts, w, p, gain, tokens, cos, sin):
     vmem = pl.BlockSpec(memory_space=pltpu.VMEM)
     hbm = pl.BlockSpec(memory_space=pl.ANY)
     smem = pl.BlockSpec(memory_space=pltpu.SMEM)
     shape = jax.ShapeDtypeStruct
+    v = pltpu.VMEM
     return pl.pallas_call(
         forward_kernel,
         out_shape=[
+            shape((LEN, D), BF16),
             shape((LEN, QKV), BF16),
             shape((2, LEN, OUT), BF16),
             shape((QH, LEN, LEN), BF16),
-            shape((4, 2, OUT, CHUNK), BF16),
+            shape((2, 4, OUT, CHUNK), BF16),
         ],
-        in_specs=[smem, vmem, vmem, hbm, hbm],
-        out_specs=[hbm, hbm, hbm, hbm],
+        in_specs=[smem, vmem, vmem, vmem, hbm, hbm, hbm],
+        out_specs=[hbm] * 5,
         scratch_shapes=[
-            pltpu.VMEM((LEN, D), BF16),
-            pltpu.VMEM((3, 2, D, 256), BF16),
-            pltpu.VMEM((4, 2, OUT, CHUNK), BF16),
-            pltpu.VMEM((2, LEN, QKV), F32),
-            pltpu.VMEM((2, LEN, OUT), BF16),
-            pltpu.VMEM((QH, LEN, LEN), BF16),
-            pltpu.VMEM((LEN, QKV), BF16),
-            pltpu.SemaphoreType.DMA((9,)),
+            pltpu.SMEM((NB,), jnp.int32),
+            v((32 * SLOTS, BLK, BLK), BF16),
+            v((32 * SLOTS, BLK, BLK), BF16),
+            v((LEN, D), BF16),
+            v((LEN, HD), F32),
+            v((LEN, HD), F32),
+            v((D, QKV), BF16),
+            v((D, QKV), BF16),
+            v((2, 4, OUT, CHUNK), BF16),
+            v((LEN, QKV), F32),
+            v((2, LEN, OUT), BF16),
+            v((QH, LEN, LEN), BF16),
+            v((LEN, QKV), BF16),
+            pltpu.SemaphoreType.DMA((144,)),
+            pltpu.SemaphoreType.DMA((144,)),
+            pltpu.SemaphoreType.DMA((11,)),
         ],
-        compiler_params=pltpu.CompilerParams(vmem_limit_bytes=VMEM_LIMIT),
+        compiler_params=pltpu.CompilerParams(
+            collective_id=0, has_side_effects=True, vmem_limit_bytes=67_000_000
+        ),
         name="forward",
-    )(table, cos, sin, normed, slots)
+    )(counts, w, p, gain, tokens, cos, sin)
 
 
 FAR, NXT, PRV, OWN = 0, 1, 2, 3
@@ -439,7 +432,7 @@
     loads = [
         pltpu.make_async_copy(a, b, local_sem.at[i])
         for i, (a, b) in enumerate(
-            [(wo_in.at[chunk[rel]], wo.at[rel]) for rel in range(4)]
+            [(wo_in.at[:, chunk[rel]], wo.at[rel]) for rel in range(4)]
             + [
                 (sides_in, sides),
                 (curv_in.at[:, curv_cols], curv),
@@ -803,10 +796,9 @@
 def local(tokens, norm_gain, curvature, weight_slots, probe_slots, block_counts):
     counts = block_counts[0]
     cos, sin = tables()
-    slots, normed, table = gather(
-        counts, weight_slots[0], probe_slots[0], tokens[0], norm_gain.reshape(1, D)
+    normed, qkv, sides, probs, wo = forward(
+        counts, weight_slots[0], probe_slots[0], norm_gain.reshape(1, D), tokens[0], cos, sin
     )
-    qkv, sides, probs, wo = forward(table.reshape(1024), cos, sin, normed, slots)
     out = main(counts, cos, sin, sides, wo, curvature[0], probs, qkv, normed)
     return out[None]
 

time: 224 us -> 217 us (0.969)
  Pallas kernels: 221 us -> 215 us
    pallas_call x2 -> x1, Pallas kernels: 97 us -> 93.4 us  [forward(): pl.pallas_call(forward_kernel, out_shape=[shape((LEN, D), BF16), shape((L...]
    pallas_call x1, Pallas kernels: 124 us -> 122 us  [main(): pl.pallas_call(main_kernel, out_shape=jax.ShapeDtypeStruct((SLOTS,) + blo...]
where the time goes in v4:
time: 217 us
  Pallas kernels  215 us (99%)
    pallas_call x1, Pallas kernels, main(): pl.pallas_call(main_kernel, out_shape=jax.ShapeDtypeStruct((SLOTS,) + blo...  122 us
    pallas_call x1, Pallas kernels, forward(): pl.pallas_call(forward_kernel, out_shape=[shape((LEN, D), BF16), shape((L...  93.4 us

profile of v4, /device:TPU:1, one launch (start us, length us, event | category | flops | bytes accessed | tf_op | source)
XLA Modules:
  0.0 217.0 jit_solution(1125584651548222961)
XLA Ops:
  0.0 93.4 %forward.1 = (bf16[512,4096]{1,0:T(8,128)(2,1)}, bf16[512,768]{1,0:T(8,128)(2,1)}, bf16[2,512,512]{2,1,0:T(8,128)(2,1)}, bf16[4,512,512]{2,1,0:T(8,128)(2,1)}, bf16[2,4,512,1024]{3,2,1,0:T(8,128)(2,1)}) custom-call(s32[32]{0:T(128)} %bitcast.13, bf16[12,128,128]{2,1,0:T(8,128)(2,1)} %bitcast.10, bf16[12,128,128]{2,1,0:T(8,128)(2,1)} %bitcast.11, ...), custom_call_target="tpu_custom_call" | custom-call | tf_op jit(solution)/shard_map/forward/pallas_call | solution.py:373
  93.4 121.5 %main.1 = f32[12,128,128]{2,1,0:T(8,128)} custom-call(s32[32]{0:T(128)} %bitcast.14, f32[512,128]{1,0:T(8,128)} %constant.4.clone.cos_in.cos, f32[512,128]{1,0:T(8,128)} %constant.5.clone.sin_in.sin, bf16[2,512,512]{2,1,0:T(8,128)(2,1)} %get-tuple-element.10.sides_in, bf16[2,4,512,1024]{3,2,1,0:T(8,128)(2,1)} %get-tuple-element.11.wo_in, ...), custom_call_target="tpu_custom_call" | custom-call | tf_op jit(solution)/shard_map/main/pallas_call | solution.py:753
  214.9 2.1 copy.10

commit v5 on v4

--- a/solution.py
+++ b/solution.py
@@ -291,50 +291,51 @@
         sides[1, :, cols_of(h)] = nn(p, v).astype(BF16)
         return carry
 
-    neighbours(0)
-    neighbours(1)
-    pass_on(0, 0)
-    pass_on(1, 0)
-    opposite(0)
-    opposite(1)
+    for p in w:
+        neighbours(p)
+    for p in w:
+        pass_on(p, 0)
+    for p in w:
+        opposite(p)
     begin(pr)
-    for f, g in ((-1, 0), (1, -1), (2, 1)):
+    for f in (-1, 1):
         for p in w:
             pass_on(p, f)
-            corner(p, g)
-    neighbours(2)
-    neighbours(3)
-    corner(0, 2)
-    corner(1, 2)
-    pass_on(2, 0)
-    pass_on(3, 0)
+    for p in w:
+        corner(p, 0)
+    for p in w:
+        pass_on(p, 2)
+    for p in pr:
+        neighbours(p)
+    for p in pr:
+        pass_on(p, 0)
+    for f in (-1, 1, 2):
+        for p in w:
+            corner(p, f)
+    for p in pr:
+        opposite(p)
     sibling_done(w)
     assemble_qkv(slots_w, wqkv, 0, 32)
-    opposite(2)
-    opposite(3)
     project(wqkv, 0)
-    pass_on(2, -1)
-    pass_on(3, -1)
+    for p in pr:
+        pass_on(p, -1)
+    for p in pr:
+        corner(p, 0)
     project(wqkv, 1)
-    corner(2, 0)
-    corner(3, 0)
     project(wqkv, 2)
-    pass_on(2, 1)
-    pass_on(3, 1)
+    for p in pr:
+        pass_on(p, 1)
     heads()
-    corner(2, -1)
-    corner(3, -1)
     lax.fori_loop(0, 2, primal, 0)
-    pass_on(2, 2)
-    pass_on(3, 2)
+    for p in pr:
+        pass_on(p, 2)
     lax.fori_loop(2, 4, primal, 0)
-    corner(2, 1)
-    corner(3, 1)
     saves.append(pltpu.make_async_copy(probs, probs_out, local_sem.at[9]))
     saves[-1].start()
     assemble_out(slots_w, 0)
-    corner(2, 2)
-    corner(3, 2)
+    for f in (-1, 1, 2):
+        for p in pr:
+            corner(p, f)
     sibling_done(pr)
 
     assemble_qkv(slots_p, pqkv, 0, 32)

time: 217 us -> 212 us (0.977)
  Pallas kernels: 215 us -> 209 us
    pallas_call x1, Pallas kernels: 93.4 us -> 87.8 us  [forward(): pl.pallas_call(forward_kernel, out_shape=[shape((LEN, D), BF16), shape((L...]
where the time goes in v5:
time: 212 us
  Pallas kernels  209 us (99%)
    pallas_call x1, Pallas kernels, main(): pl.pallas_call(main_kernel, out_shape=jax.ShapeDtypeStruct((SLOTS,) + blo...  122 us
    pallas_call x1, Pallas kernels, forward(): pl.pallas_call(forward_kernel, out_shape=[shape((LEN, D), BF16), shape((L...  87.8 us

profile of v5, /device:TPU:1, one launch (start us, length us, event | category | flops | bytes accessed | tf_op | source)
XLA Modules:
  0.0 211.6 jit_solution(12143549861878106910)
XLA Ops:
  0.0 87.8 %forward.1 = (bf16[512,4096]{1,0:T(8,128)(2,1)}, bf16[512,768]{1,0:T(8,128)(2,1)}, bf16[2,512,512]{2,1,0:T(8,128)(2,1)}, bf16[4,512,512]{2,1,0:T(8,128)(2,1)}, bf16[2,4,512,1024]{3,2,1,0:T(8,128)(2,1)}) custom-call(s32[32]{0:T(128)} %bitcast.13, bf16[12,128,128]{2,1,0:T(8,128)(2,1)} %bitcast.10, bf16[12,128,128]{2,1,0:T(8,128)(2,1)} %bitcast.11, ...), custom_call_target="tpu_custom_call" | custom-call | tf_op jit(solution)/shard_map/forward/pallas_call | solution.py:374
  87.8 121.6 %main.1 = f32[12,128,128]{2,1,0:T(8,128)} custom-call(s32[32]{0:T(128)} %bitcast.14, f32[512,128]{1,0:T(8,128)} %constant.4.clone.cos_in.cos, f32[512,128]{1,0:T(8,128)} %constant.5.clone.sin_in.sin, bf16[2,512,512]{2,1,0:T(8,128)(2,1)} %get-tuple-element.10.sides_in, bf16[2,4,512,1024]{3,2,1,0:T(8,128)(2,1)} %get-tuple-element.11.wo_in, ...), custom_call_target="tpu_custom_call" | custom-call | tf_op jit(solution)/shard_map/main/pallas_call | solution.py:754
  209.5 2.1 copy.10

commit v6 on v5

v6 whole, which is shorter than its diff:
```python
import functools

import jax
import jax.numpy as jnp
import numpy as np
from jax import lax
from jax.experimental import pallas as pl
from jax.experimental.pallas import tpu as pltpu
from jax.sharding import PartitionSpec as P

D = 4096
HD = 128
BLK = 128
LEN = 512
QH = 4
QKV = 768
OUT = 512
NQKV = 192
NB = 320
SLOTS = 12
HALF = 6
CHUNK = 1024
FAR, NXT, PRV, OWN = 0, 1, 2, 3
THETA = 500000.0
EPS = 1e-05
NEGATIVE = -1e30
VMEM_LIMIT = 66_000_000
MESH = pl.DeviceIdType.MESH
F32 = jnp.float32
BF16 = jnp.bfloat16


def tables():
    half = HD // 2
    frequency = np.exp(-np.log(THETA) * 2.0 * np.arange(half) / HD)
    angles = np.arange(LEN)[:, None] * frequency[None, :]
    c, s = np.cos(angles), np.sin(angles)
    return (
        np.concatenate([c, c], axis=1).astype(np.float32),
        np.concatenate([-s, s], axis=1).astype(np.float32),
    )


def place():
    me = lax.axis_index("fsdp")
    core = lax.rem(me, 2)
    y = lax.rem(me // 2, 4)
    z = me // 8
    return me, core, y, z


def index_of(z, y, core):
    return (z * 4 + y) * 2 + core


def wrap(a):
    return lax.rem(a + 4, 4)


def greet(targets):
    barrier = pltpu.get_barrier_semaphore()
    for t in targets:
        pl.semaphore_signal(barrier, inc=1, device_id=t, device_id_type=MESH)
    pl.semaphore_wait(barrier, len(targets))


def nt(a, b):
    return lax.dot_general(a, b, (((1,), (1,)), ((), ())), preferred_element_type=F32)


def nn(a, b):
    return jnp.dot(a, b, preferred_element_type=F32)


def causal_mask():
    row = lax.broadcasted_iota(jnp.int32, (LEN, LEN), 0)
    col = lax.broadcasted_iota(jnp.int32, (LEN, LEN), 1)
    return row >= col


def kernel(
    counts, w_in, p_in, gain, tokens_in, cos_in, sin_in, curv_in,
    out,
    table, starts, slots_w, slots_p, normed, cos, sin, wqkv, wout, proj, sides, probs, qkv,
    opp, low, high, wt, r_far, r_low, r_high, t_far, t_low, t_high, tot,
    send_sem, recv_sem, local_sem, ready,
):
    me, core, y, z = place()
    x = lax.axis_index("seq")
    sib = {"fsdp": index_of(z, y, 1 - core)}
    up, down = {"seq": wrap(x + 1)}, {"seq": wrap(x - 1)}

    def at(axis, step):
        if axis == "y":
            return {"fsdp": index_of(z, wrap(y + step), core)}
        return {"fsdp": index_of(wrap(z + step), y, core)}

    my_slots = pl.ds(me * SLOTS, SLOTS)
    local = [
        pltpu.make_async_copy(a, b, local_sem.at[i])
        for i, (a, b) in enumerate(
            (
                (w_in, slots_w.at[my_slots]),
                (p_in, slots_p.at[my_slots]),
                (tokens_in, normed),
                (cos_in, cos),
                (sin_in, sin),
            )
        )
    ]
    for copy in local:
        copy.start()
    greet([up, down, at("y", 1), at("y", -1), at("z", 1), at("z", -1), sib])

    first = ("y", "z", "y", "z")
    second = ("z", "y", "z", "y")
    landed = (slots_w, slots_w, slots_p, slots_p)
    counter = [0]
    sends = []
    arrivals = {}

    def send(key, src, dst, target):
        number = counter[0]
        counter[0] += 1
        copy = pltpu.make_async_remote_copy(
            src_ref=src,
            dst_ref=dst,
            send_sem=send_sem.at[number],
            recv_sem=recv_sem.at[number],
            device_id=target,
            device_id_type=MESH,
        )
        copy.start()
        sends.append(copy)
        arrivals[key] = copy
        return copy

    def span(p, side):
        start = (p % 2) * HALF
        return (start, HALF) if side is None else (start + 3 * side, 3)

    def piece(p, origin, side=None):
        start, size = span(p, side)
        return landed[p].at[pl.ds(origin * SLOTS + start, size)]

    def origin_of(p, f, s):
        if p % 2 == 0:
            return index_of(wrap(z + s), wrap(y + f), core)
        return index_of(wrap(z + f), wrap(y + s), core)

    def go(p, role, f, s, axis, step, side=None):
        ref = piece(p, origin_of(p, f, s), side)
        send((p,) + role, ref, ref, at(axis[p], step))

    def to_sib(p, f, s):
        ref = piece(p, origin_of(p, f, s))
        send((p, "sib", f, s), ref, ref, sib)

    def got(*key):
        arrivals[key].wait_recv()

    def begin(parts):
        for p in parts:
            go(p, ("f+",), 0, 0, first, 1)
            go(p, ("f-",), 0, 0, first, -1)
        for p in parts:
            go(p, ("s+", 0), 0, 0, second, 1)
            go(p, ("s-", 0), 0, 0, second, -1)
        for p in parts:
            to_sib(p, 0, 0)

    def neighbours(p):
        got(p, "f+")
        go(p, ("fa",), -1, 0, first, 1, 0)
        go(p, ("s+", -1), -1, 0, second, 1)
        go(p, ("s-", -1), -1, 0, second, -1)
        got(p, "f-")
        go(p, ("fb",), 1, 0, first, -1, 1)
        go(p, ("s+", 1), 1, 0, second, 1)
        go(p, ("s-", 1), 1, 0, second, -1)
        to_sib(p, -1, 0)
        to_sib(p, 1, 0)

    def pass_on(p, f):
        got(p, "s+", f)
        go(p, ("sa", f), f, -1, second, 1, 0)
        to_sib(p, f, -1)
        got(p, "s-", f)
        go(p, ("sb", f), f, 1, second, -1, 1)
        to_sib(p, f, 1)

    def opposite(p):
        got(p, "fa")
        got(p, "fb")
        go(p, ("s+", 2), 2, 0, second, 1)
        go(p, ("s-", 2), 2, 0, second, -1)
        to_sib(p, 2, 0)

    def corner(p, f):
        got(p, "sa", f)
        got(p, "sb", f)
        to_sib(p, f, 2)

    def sibling_done(parts):
        for p in parts:
            for f in (0, -1, 1, 2):
                for s in (0, -1, 1, 2):
                    got(p, "sib", f, s)

    w, pr = (0, 1), (2, 3)
    local[0].wait()
    local[1].wait()
    begin(w)

    def locate(b, carry):
        d, t = carry
        table[b] = d * SLOTS + t
        more = t + 1 < counts[d]
        return jnp.where(more, d, jnp.minimum(d + 1, 31)), jnp.where(more, t + 1, 0)

    lax.fori_loop(0, NB, locate, (0, 0))

    def prefix(d, s):
        starts[d] = s
        return s + counts[d]

    lax.fori_loop(0, 32, prefix, 0)
    local[2].wait()

    def norm(i, carry):
        rows = pl.ds(pl.multiple_of(i * 32, 32), 32)
        x = normed[rows, :].astype(F32)
        factor = lax.rsqrt(jnp.mean(x * x, axis=-1, keepdims=True) + EPS)
        normed[rows, :] = (x * factor * gain[...]).astype(BF16)
        return carry

    lax.fori_loop(0, LEN // 32, norm, 0)
    local[3].wait()
    local[4].wait()

    def cols_of(h):
        return pl.ds(h * HD if isinstance(h, int) else pl.multiple_of(h * HD, HD), HD)

    def assemble_qkv(src):
        def step(r, carry):
            rows = pl.ds(pl.multiple_of(r * BLK, BLK), BLK)
            for c in range(6):
                wqkv[rows, c * BLK : (c + 1) * BLK] = src[table[r * 6 + c]]
            return carry

        lax.fori_loop(0, 32, step, 0)

    def assemble_out(src, tensor):
        def step(i, carry):
            rows = pl.ds(pl.multiple_of(i * BLK, BLK), BLK)
            for j in range(32):
                wout[tensor, j // 8, rows, (j % 8) * BLK : (j % 8 + 1) * BLK] = src[
                    table[NQKV + i * 32 + j]
                ]
            return carry

        lax.fori_loop(0, 4, step, 0)

    all_rows = slice(0, LEN)
    half = LEN // 2
    halves = (slice(0, half), slice(half, LEN))

    def project(n, rows=all_rows):
        cols = slice(n * 256, (n + 1) * 256)
        proj[rows, cols] = nn(normed[rows, :], wqkv[:, cols])

    def head(h, turn=True, rows=all_rows):
        v = proj[rows, cols_of(h)]
        if turn:
            v = v * cos[rows, :] + pltpu.roll(v, 64, 1) * sin[rows, :]
        return v.astype(BF16)

    def heads():
        for h in range(QH + 2):
            qkv[:, cols_of(h)] = head(h, h < QH + 1)

    scale = HD**-0.5

    def primal(h, carry):
        k = qkv[:, cols_of(QH)]
        v = qkv[:, cols_of(QH + 1)]
        s = jnp.where(causal_mask(), nt(qkv[:, cols_of(h)], k) * scale, NEGATIVE)
        m = jnp.max(s, axis=-1, keepdims=True)
        e = jnp.exp(s - m)
        p = (e * (1.0 / jnp.sum(e, axis=-1, keepdims=True))).astype(BF16)
        probs[h] = p
        sides[1, :, cols_of(h)] = nn(p, v).astype(BF16)
        return carry

    for p in w:
        neighbours(p)
    for p in w:
        pass_on(p, 0)
    for p in w:
        opposite(p)
    begin(pr)
    for f in (-1, 1):
        for p in w:
            pass_on(p, f)
    for p in w:
        corner(p, 0)
    for p in w:
        pass_on(p, 2)
    for p in pr:
        neighbours(p)
    for p in pr:
        pass_on(p, 0)
    for f in (-1, 1, 2):
        for p in w:
            corner(p, f)
    for p in pr:
        opposite(p)
    sibling_done(w)
    assemble_qkv(slots_w)
    project(0)
    for p in pr:
        pass_on(p, -1)
    for p in pr:
        corner(p, 0)
    project(1)
    project(2)
    for p in pr:
        pass_on(p, 1)
    heads()
    lax.fori_loop(0, 2, primal, 0)
    for p in pr:
        pass_on(p, 2)
    lax.fori_loop(2, 4, primal, 0)
    assemble_out(slots_w, 0)
    for f in (-1, 1, 2):
        for p in pr:
            corner(p, f)
    sibling_done(pr)

    chunk = (wrap(x + 2), wrap(x + 1), wrap(x - 1), x)
    key_tangent, value_tangent = cols_of(0), cols_of(1)

    def tangent(s):
        rows, seen = halves[s], slice(0, half * (s + 1))
        for n in range(3):
            project(n, rows)
        wt[OWN, rows, key_tangent] = head(QH, True, rows)
        wt[OWN, rows, value_tangent] = head(QH + 1, False, rows)
        keys = jnp.concatenate([qkv[seen, cols_of(QH)], wt[OWN, seen, key_tangent]], axis=1)

        def one(h, carry):
            pb = probs[h, rows, seen]
            pf = pb.astype(F32)
            side = jnp.concatenate([head(h, True, rows), qkv[rows, cols_of(h)]], axis=1)
            pt = pf * (nt(side, keys) * scale)
            tp = (pt - pf * jnp.sum(pt, axis=-1, keepdims=True)).astype(BF16)
            sides[0, rows, cols_of(h)] = (
                nn(tp, qkv[seen, cols_of(QH + 1)]) + nn(pb, wt[OWN, seen, value_tangent])
            ).astype(BF16)
            return carry

        lax.fori_loop(0, QH, one, 0)

    def term_at(rel, s, part):
        return ((rel * 2 + s) * 2 + part) * 8

    def term(rel, s):
        rows = halves[s]
        for n in range(2):
            cols = slice(n * 512, (n + 1) * 512)
            v = (
                nn(sides[0, rows, :], wout[0, chunk[rel], :, cols])
                + nn(sides[1, rows, :], wout[1, chunk[rel], :, cols])
            ).astype(BF16)
            for part in (0, 1):
                for j in range(4):
                    slots_p[term_at(rel, s, part) + 4 * n + j] = v[
                        part * BLK : (part + 1) * BLK, j * BLK : (j + 1) * BLK
                    ]

    def terms(rel, s, part):
        return slots_p.at[pl.ds(term_at(rel, s, part), 8)]

    def cast(name, src, dst, target):
        return send(name, src, dst, target)

    assemble_qkv(slots_p)
    assemble_out(slots_p, 1)
    tangent(0)
    for copy in sends:
        copy.wait_send()
    sends.clear()
    pl.semaphore_signal(ready, inc=1, device_id=sib, device_id_type=MESH)
    for s in (0, 1):
        if s == 1:
            tangent(1)
        term(FAR, s)
        cast(("a0", s), terms(FAR, s, 0), opp.at[0, s], up)
        cast(("b0", s), terms(FAR, s, 1), opp.at[1, s], down)
        term(NXT, s)
        term(PRV, s)
        if s == 0:
            cast(("a1", s), terms(NXT, s, 1), low.at[1, s], up)
            cast(("b1", s), terms(PRV, s, 0), high.at[0, s], down)
    curv_loads = []
    for n in range(2):
        curv_loads.append(
            pltpu.make_async_copy(
                curv_in.at[:, pl.ds(pl.multiple_of(x * CHUNK + n * 512, 512), 512)],
                wqkv.at[n * LEN : (n + 1) * LEN, 0:512],
                local_sem.at[5 + n],
            )
        )
        curv_loads[-1].start()
    for s in (0, 1):
        got("a0", s)
        mine = slots_p[pl.ds(term_at(NXT, s, 0), 8)].astype(F32)
        opp[0, s] = (opp[0, s].astype(F32) + mine).astype(BF16)
        cast(("a2", s), opp.at[0, s], low.at[0, s], up)
        got("b0", s)
        mine = slots_p[pl.ds(term_at(PRV, s, 1), 8)].astype(F32)
        opp[1, s] = (opp[1, s].astype(F32) + mine).astype(BF16)
        cast(("b2", s), opp.at[1, s], high.at[1, s], down)
        if s == 0:
            cast(("a1", 1), terms(NXT, 1, 1), low.at[1, 1], up)
            cast(("b1", 1), terms(PRV, 1, 0), high.at[0, 1], down)
            term(OWN, 0)
            term(OWN, 1)
            turned = slice(2 * LEN, 3 * LEN)
            wqkv[turned, 0:512] = sides[1].T
            for copy in curv_loads:
                copy.wait()

    def part_rows(s, part):
        return pl.ds(s * half + part * BLK, BLK)

    def weigh(part, s):
        rows = s * half + part * BLK
        for j in range(8):
            total = (
                slots_p[term_at(OWN, s, part) + j].astype(F32)
                + low[part, s, j].astype(F32)
                + high[part, s, j].astype(F32)
            )
            at_row = (j // 4) * LEN + rows
            c = wqkv[at_row : at_row + BLK, (j % 4) * BLK : (j % 4 + 1) * BLK].astype(F32)
            wt[OWN, rows : rows + BLK, j * BLK : (j + 1) * BLK] = (total * c).astype(BF16)

    def hand_on(name, src, dst, part, s, target):
        r = part_rows(s, part)
        cast((name, s), wt.at[src, r], wt.at[dst, r], target)

    def mixed_cotangent(rel, s):
        rows = halves[s]
        v = nt(wt[rel, rows, :], wout[0, chunk[rel]])
        if rel == OWN:
            proj[rows, 0:OUT] = v
        else:
            proj[rows, 0:OUT] += v

    per = NB // 2
    n_in = NQKV // 2

    def out_gradient(rel):
        for n in range(2):
            g = nn(wqkv[turned, 0:512], wt[rel, :, n * 512 : (n + 1) * 512]).astype(BF16)
            for i in range(4):
                for j in range(4):
                    slots_w[(j % 2) * per + n_in + 16 * i + 4 * chunk[rel] + 2 * n + j // 2] = g[
                        i * BLK : (i + 1) * BLK, j * BLK : (j + 1) * BLK
                    ]

    for s in (0, 1):
        got("a1", s)
        got("b2", s)
        weigh(1, s)
        hand_on("c1", OWN, PRV, 1, s, up)
        hand_on("d1", OWN, NXT, 1, s, down)
        got("b1", s)
        got("a2", s)
        weigh(0, s)
        hand_on("d0", OWN, NXT, 0, s, down)
        hand_on("c0", OWN, PRV, 0, s, up)
        mixed_cotangent(OWN, s)
    for s in (0, 1):
        got("c1", s)
        hand_on("e1", PRV, FAR, 1, s, up)
        got("d0", s)
        hand_on("e0", NXT, FAR, 0, s, down)
        if s == 0:
            out_gradient(OWN)
        got("d1", s)
        mixed_cotangent(NXT, s)
        got("c0", s)
        mixed_cotangent(PRV, s)
    got("e1", 0)
    got("e0", 0)
    mixed_cotangent(FAR, 0)

    def unrot(v, rows):
        return v * cos[rows, :] - pltpu.roll(v, 64, 1) * sin[rows, :]

    tail = slice(OUT, QKV)
    proj[:, tail] = jnp.zeros((LEN, QKV - OUT), F32)

    def attention_back(s):
        rows, seen = halves[s], slice(0, half * (s + 1))

        def one(h, carry):
            dm = proj[rows, cols_of(h)].astype(BF16)
            q = qkv[rows, cols_of(h)]
            pb = probs[h, rows, seen]
            dp = nt(dm, qkv[seen, cols_of(QH + 1)]).astype(BF16).astype(F32)
            pf = pb.astype(F32)
            pd = pf * dp
            ds = ((pd - pf * jnp.sum(pd, axis=-1, keepdims=True)) * scale).astype(BF16)
            dk = nn(q.T, ds)
            dv = nn(dm.T, pb)
            for u in range(s + 1):
                proj[u * BLK : (u + 1) * BLK, tail] += dk[:, u * half : (u + 1) * half]
                proj[half + u * BLK : half + (u + 1) * BLK, tail] += dv[
                    :, u * half : (u + 1) * half
                ]
            dq = unrot(nn(ds, qkv[seen, cols_of(QH)]).astype(BF16).astype(F32), rows).astype(BF16)
            sides[0, cols_of(h), rows] = dq.T
            return carry

        lax.fori_loop(0, QH, one, 0)

    attention_back(0)
    out_gradient(NXT)
    out_gradient(PRV)
    got("e1", 1)
    got("e0", 1)
    out_gradient(FAR)
    pl.semaphore_wait(ready, 1)
    sb = 192
    out_part = pl.ds((1 - core) * per + n_in, per - n_in)
    cast(("swap", 8), slots_w.at[out_part], slots_p.at[pl.ds(sb + n_in, per - n_in)], sib)
    mixed_cotangent(FAR, 1)
    attention_back(1)
    for u in range(2):
        dk = proj[u * BLK : (u + 1) * BLK, tail].astype(BF16).astype(F32).T
        sides[1, 0:BLK, halves[u]] = unrot(dk, halves[u]).astype(BF16).T
        sides[1, BLK : 2 * BLK, halves[u]] = proj[
            half + u * BLK : half + (u + 1) * BLK, tail
        ].astype(BF16)
    for n in range(8):
        cols = slice(n * 512, (n + 1) * 512)
        for c0, lhs in ((0, sides[0]), (4, sides[1, 0 : 2 * BLK, :])):
            g = nn(lhs, normed[:, cols]).astype(BF16)
            for r in range(4):
                for c in range(lhs.shape[0] // BLK):
                    slots_w[((c0 + c) % 2) * per + 3 * (4 * n + r) + (c0 + c) // 2] = g[
                        c * BLK : (c + 1) * BLK, r * BLK : (r + 1) * BLK
                    ]
        cast(
            ("swap", n),
            slots_w.at[pl.ds((1 - core) * per + 12 * n, 12)],
            slots_p.at[pl.ds(sb + 12 * n, 12)],
            sib,
        )
    for n in (8, 0, 1, 2, 3, 4, 5, 6, 7):
        got("swap", n)
    for copy in sends:
        copy.wait_send()
    sends.clear()

    chain = (("z", "y"), ("y", "z"))
    here = {"y": y, "z": z}
    steps = (2, 1, -1, 0)

    def acc_at(part, rel, h):
        return ((part * 4 + rel) * 2 + h) * 12

    def red_at(part, h, srel):
        return 2 * per + (part * 2 + h) * 12 + 3 * srel

    def fill(part, rel):
        f = wrap(here[chain[part][0]] + steps[rel])
        for srel in range(4):
            s = wrap(here[chain[part][1]] + steps[srel])
            d = index_of(f, s, part) if part == 0 else index_of(s, f, part)
            base = (starts[d] + 1 - core) // 2
            for i in range(HALF):
                j = jnp.minimum(base + i, per - 1)
                slots_p[acc_at(part, rel, i // 3) + 3 * srel + i % 3] = (
                    slots_w[core * per + j].astype(F32) + slots_p[sb + j].astype(F32)
                ).astype(BF16)

    subs = ((0, 3), (3, 6), (9, 3))

    def acc(part, rel, h, u):
        return pl.ds(acc_at(part, rel, h) + subs[u][0], subs[u][1])

    def ring(part, name, u, src, dst, leg, step):
        send((part, name, u), src, dst, at(chain[part][leg], step))

    def send_far(part, u):
        sub = pl.ds(*subs[u])
        ring(part, "fu", u, slots_p.at[acc(part, FAR, 0, u)], r_far.at[part, 0, sub], 0, 1)
        ring(part, "fd", u, slots_p.at[acc(part, FAR, 1, u)], r_far.at[part, 1, sub], 0, -1)

    def send_near(part, u):
        sub = pl.ds(*subs[u])
        ring(part, "lo1", u, slots_p.at[acc(part, NXT, 1, u)], r_low.at[part, 1, sub], 0, 1)
        ring(part, "hi0", u, slots_p.at[acc(part, PRV, 0, u)], r_high.at[part, 0, sub], 0, -1)

    def middle(part, u):
        sub = pl.ds(*subs[u])
        got(part, "fu", u)
        r_far[part, 0, sub] = (
            r_far[part, 0, sub].astype(F32) + slots_p[acc(part, NXT, 0, u)].astype(F32)
        ).astype(BF16)
        ring(part, "lo0", u, r_far.at[part, 0, sub], r_low.at[part, 0, sub], 0, 1)
        got(part, "fd", u)
        r_far[part, 1, sub] = (
            r_far[part, 1, sub].astype(F32) + slots_p[acc(part, PRV, 1, u)].astype(F32)
        ).astype(BF16)
        ring(part, "hi1", u, r_far.at[part, 1, sub], r_high.at[part, 1, sub], 0, -1)

    def reduce(part, u):
        sub = pl.ds(*subs[u])
        for name in ("lo1", "hi0", "lo0", "hi1"):
            got(part, name, u)
        for h in (0, 1):
            slots_w[pl.ds(red_at(part, h, 0) + subs[u][0], subs[u][1])] = (
                slots_p[acc(part, OWN, h, u)].astype(F32)
                + r_low[part, h, sub].astype(F32)
                + r_high[part, h, sub].astype(F32)
            ).astype(BF16)

    def red(part, h, srel):
        return pl.ds(red_at(part, h, srel), 3)

    both = (0, 1)
    for part in both:
        fill(part, FAR)
        send_far(part, 0)
    for part in both:
        fill(part, NXT)
        fill(part, PRV)
        send_near(part, 0)
    for part in both:
        send_far(part, 1)
        send_near(part, 1)
    for part in both:
        fill(part, OWN)
    for part in both:
        middle(part, 0)
    for part in both:
        send_far(part, 2)
        send_near(part, 2)
    for part in both:
        middle(part, 1)
    for part in both:
        reduce(part, 0)
        ring(part, "tu", 0, slots_w.at[red(part, 0, FAR)], t_far.at[part, 0], 1, 1)
        ring(part, "td", 0, slots_w.at[red(part, 1, FAR)], t_far.at[part, 1], 1, -1)
    for part in both:
        middle(part, 2)
    for part in both:
        reduce(part, 1)
        ring(part, "tl1", 0, slots_w.at[red(part, 1, NXT)], t_low.at[part, 1], 1, 1)
        ring(part, "th0", 0, slots_w.at[red(part, 0, PRV)], t_high.at[part, 0], 1, -1)
    for part in both:
        got(part, "tu", 0)
        t_far[part, 0] = (
            t_far[part, 0].astype(F32) + slots_w[red(part, 0, NXT)].astype(F32)
        ).astype(BF16)
        ring(part, "tl0", 0, t_far.at[part, 0], t_low.at[part, 0], 1, 1)
        got(part, "td", 0)
        t_far[part, 1] = (
            t_far[part, 1].astype(F32) + slots_w[red(part, 1, PRV)].astype(F32)
        ).astype(BF16)
        ring(part, "th1", 0, t_far.at[part, 1], t_high.at[part, 1], 1, -1)
    for part in both:
        reduce(part, 2)
    for part in both:
        for name in ("tl1", "th0", "tl0", "th1"):
            got(part, name, 0)

    def whole(part, h):
        return (
            slots_w[pl.ds(2 * per + (part * 2 + h) * 12 + 3 * OWN, 3)].astype(F32)
            + t_low[part, h].astype(F32)
            + t_high[part, h].astype(F32)
        )

    for h in (0, 1):
        out[pl.ds(3 * h, 3)] = whole(1 - core, h)
    last = cast(("last",), out.at[pl.ds(0, HALF)], tot.at[core], sib)
    for h in (0, 1):
        tot[core, pl.ds(3 * h, 3)] = whole(core, h)
    last.wait_recv()
    for copy in sends:
        copy.wait_send()

    start, n = starts[me], counts[me]
    factor = 1.0 / np.sqrt(np.float32(LEN * 32))
    for t in range(SLOTS):
        b = start + t
        parity = lax.rem(b, 2)
        v = tot[parity, b // 2 - (start + 1 - parity) // 2] * factor
        v = jnp.where(b < NQKV, v.T, v)
        out[t] = jnp.where(t < n, v, 0.0)


def product(counts, w, p, gain, tokens, cos, sin, curv):
    vmem = pl.BlockSpec(memory_space=pltpu.VMEM)
    hbm = pl.BlockSpec(memory_space=pl.ANY)
    smem = pl.BlockSpec(memory_space=pltpu.SMEM)
    v = pltpu.VMEM
    block = (BLK, BLK)
    return pl.pallas_call(
        kernel,
        out_shape=jax.ShapeDtypeStruct((SLOTS,) + block, F32),
        in_specs=[smem, hbm, hbm, vmem, hbm, hbm, hbm, hbm],
        out_specs=vmem,
        scratch_shapes=[
            pltpu.SMEM((NB,), jnp.int32),
            pltpu.SMEM((32,), jnp.int32),
            v((32 * SLOTS,) + block, BF16),
            v((32 * SLOTS,) + block, BF16),
            v((LEN, D), BF16),
            v((LEN, HD), F32),
            v((LEN, HD), F32),
            v((D, QKV), BF16),
            v((2, 4, OUT, CHUNK), BF16),
            v((LEN, QKV), F32),
            v((2, LEN, OUT), BF16),
            v((QH, LEN, LEN), BF16),
            v((LEN, QKV), BF16),
            v((2, 2, 8) + block, BF16),
            v((2, 2, 8) + block, BF16),
            v((2, 2, 8) + block, BF16),
            v((4, LEN, CHUNK), BF16),
            v((2, 2, 12) + block, BF16),
            v((2, 2, 12) + block, BF16),
            v((2, 2, 12) + block, BF16),
            v((2, 2, 3) + block, BF16),
            v((2, 2, 3) + block, BF16),
            v((2, 2, 3) + block, BF16),
            v((2, HALF) + block, F32),
            pltpu.SemaphoreType.DMA((226,)),
            pltpu.SemaphoreType.DMA((226,)),
            pltpu.SemaphoreType.DMA((7,)),
            pltpu.SemaphoreType.REGULAR,
        ],
        compiler_params=pltpu.CompilerParams(
            collective_id=0, has_side_effects=True, vmem_limit_bytes=67_000_000
        ),
        name="product",
    )(counts, w, p, gain, tokens, cos, sin, curv)


def local(tokens, norm_gain, curvature, weight_slots, probe_slots, block_counts):
    counts = block_counts[0]
    cos, sin = tables()
    out = product(
        counts,
        weight_slots[0],
        probe_slots[0],
        norm_gain.reshape(1, D),
        tokens[0],
        cos,
        sin,
        curvature[0],
    )
    return out[None]


def solution(mesh):
    in_specs = (
        P("fsdp", None, None),
        P(),
        P("fsdp", None, None),
        P("seq", "fsdp", None, None),
        P("seq", "fsdp", None, None),
        P("seq", None),
    )
    out_specs = P("seq", "fsdp", None, None)
    return jax.shard_map(local, mesh=mesh, in_specs=in_specs, out_specs=out_specs, check_vma=False)
```

time: 212 us -> 206 us (0.972)
  Pallas kernels: 209 us -> 204 us
    pallas_call x2 -> x1, Pallas kernels: 209 us -> 204 us  [product(): pl.pallas_call(kernel, out_shape=jax.ShapeDtypeStruct((SLOTS,) + block, F...]
where the time goes in v6:
time: 206 us
  Pallas kernels  204 us (99%)
  local copies, waits for them, and re-layouts  2.06 us (1%)
    pallas_call x1, Pallas kernels, product(): pl.pallas_call(kernel, out_shape=jax.ShapeDtypeStruct((SLOTS,) + block, F...  204 us

profile of v6, /device:TPU:1, one launch (start us, length us, event | category | flops | bytes accessed | tf_op | source)
XLA Modules:
  0.0 205.7 jit_solution(10517351995040826325)
XLA Ops:
  0.0 203.6 %product.1 = f32[12,128,128]{2,1,0:T(8,128)} custom-call(s32[32]{0:T(128)} %bitcast.13, bf16[12,128,128]{2,1,0:T(8,128)(2,1)} %bitcast.10, bf16[12,128,128]{2,1,0:T(8,128)(2,1)} %bitcast.11, f32[1,4096]{1,0:T(1,128)} %bitcast.12, bf16[512,4096]{1,0:T(8,128)(2,1)} %bitcast.7, f32[512,128]{1,0:T(8,128)} %constant.4.clone.cos_in, ...), custom_call_target="tpu_custom_call" | custom-call | tf_op jit(solution)/shard_map/product/pallas_call | solution.py:715
  203.6 2.1 %copy.10 = f32[1,12,128,128]{3,2,1,0:T(8,128)} copy(f32[1,12,128,128]{3,2,1,0:T(8,128)} %bitcast.9) | data formatting | bytes 1572864

commit v7 on v6

--- a/solution.py
+++ b/solution.py
@@ -248,7 +248,14 @@
                 wqkv[rows, c * BLK : (c + 1) * BLK] = src[table[r * 6 + c]]
             return carry
 
-        lax.fori_loop(0, 32, step, 0)
+        lax.fori_loop(0, 32, step, 0, unroll=2)
+
+    def assemble_out_chunk(src, tensor, q):
+        for i in range(4):
+            for j in range(8):
+                wout[tensor, q, i * BLK : (i + 1) * BLK, j * BLK : (j + 1) * BLK] = src[
+                    table[NQKV + i * 32 + q * 8 + j]
+                ]
 
     def assemble_out(src, tensor):
         def step(i, carry):
@@ -362,7 +369,7 @@
         lax.fori_loop(0, QH, one, 0)
 
     def term_at(rel, s, part):
-        return ((rel * 2 + s) * 2 + part) * 8
+        return (0, 32, 64, 160)[rel] + (s * 2 + part) * 8
 
     def term(rel, s):
         rows = halves[s]
@@ -374,34 +381,38 @@
             ).astype(BF16)
             for part in (0, 1):
                 for j in range(4):
-                    slots_p[term_at(rel, s, part) + 4 * n + j] = v[
+                    slots_w[term_at(rel, s, part) + 4 * n + j] = v[
                         part * BLK : (part + 1) * BLK, j * BLK : (j + 1) * BLK
                     ]
 
     def terms(rel, s, part):
-        return slots_p.at[pl.ds(term_at(rel, s, part), 8)]
+        return slots_w.at[pl.ds(term_at(rel, s, part), 8)]
 
     def cast(name, src, dst, target):
         return send(name, src, dst, target)
 
     assemble_qkv(slots_p)
-    assemble_out(slots_p, 1)
     tangent(0)
     for copy in sends:
         copy.wait_send()
     sends.clear()
-    pl.semaphore_signal(ready, inc=1, device_id=sib, device_id_type=MESH)
     for s in (0, 1):
         if s == 1:
             tangent(1)
-        term(FAR, s)
-        cast(("a0", s), terms(FAR, s, 0), opp.at[0, s], up)
-        cast(("b0", s), terms(FAR, s, 1), opp.at[1, s], down)
-        term(NXT, s)
-        term(PRV, s)
+        for rel in (FAR, NXT, PRV):
+            if s == 0:
+                assemble_out_chunk(slots_p, 1, chunk[rel])
+            term(rel, s)
+            if rel == FAR:
+                cast(("a0", s), terms(FAR, s, 0), opp.at[0, s], up)
+                cast(("b0", s), terms(FAR, s, 1), opp.at[1, s], down)
+            if rel == NXT and s == 0:
+                cast(("a1", s), terms(NXT, s, 1), low.at[1, s], up)
+            if rel == PRV and s == 0:
+                cast(("b1", s), terms(PRV, s, 0), high.at[0, s], down)
         if s == 0:
-            cast(("a1", s), terms(NXT, s, 1), low.at[1, s], up)
-            cast(("b1", s), terms(PRV, s, 0), high.at[0, s], down)
+            assemble_out_chunk(slots_p, 1, chunk[OWN])
+            pl.semaphore_signal(ready, inc=1, device_id=sib, device_id_type=MESH)
     curv_loads = []
     for n in range(2):
         curv_loads.append(
@@ -414,11 +425,11 @@
         curv_loads[-1].start()
     for s in (0, 1):
         got("a0", s)
-        mine = slots_p[pl.ds(term_at(NXT, s, 0), 8)].astype(F32)
+        mine = slots_w[pl.ds(term_at(NXT, s, 0), 8)].astype(F32)
         opp[0, s] = (opp[0, s].astype(F32) + mine).astype(BF16)
         cast(("a2", s), opp.at[0, s], low.at[0, s], up)
         got("b0", s)
-        mine = slots_p[pl.ds(term_at(PRV, s, 1), 8)].astype(F32)
+        mine = slots_w[pl.ds(term_at(PRV, s, 1), 8)].astype(F32)
         opp[1, s] = (opp[1, s].astype(F32) + mine).astype(BF16)
         cast(("b2", s), opp.at[1, s], high.at[1, s], down)
         if s == 0:
@@ -438,7 +449,7 @@
         rows = s * half + part * BLK
         for j in range(8):
             total = (
-                slots_p[term_at(OWN, s, part) + j].astype(F32)
+                slots_w[term_at(OWN, s, part) + j].astype(F32)
                 + low[part, s, j].astype(F32)
                 + high[part, s, j].astype(F32)
             )
@@ -460,6 +471,7 @@
 
     per = NB // 2
     n_in = NQKV // 2
+    sb = 192
 
     def out_gradient(rel):
         for n in range(2):
@@ -469,6 +481,16 @@
                     slots_w[(j % 2) * per + n_in + 16 * i + 4 * chunk[rel] + 2 * n + j // 2] = g[
                         i * BLK : (i + 1) * BLK, j * BLK : (j + 1) * BLK
                     ]
+        if rel == OWN:
+            pl.semaphore_wait(ready, 1)
+        for i in range(4):
+            b = n_in + 16 * i + 4 * chunk[rel]
+            cast(
+                ("swap", rel, i),
+                slots_w.at[pl.ds((1 - core) * per + b, 4)],
+                slots_p.at[pl.ds(sb + b, 4)],
+                sib,
+            )
 
     for s in (0, 1):
         got("a1", s)
@@ -533,10 +555,6 @@
     got("e1", 1)
     got("e0", 1)
     out_gradient(FAR)
-    pl.semaphore_wait(ready, 1)
-    sb = 192
-    out_part = pl.ds((1 - core) * per + n_in, per - n_in)
-    cast(("swap", 8), slots_w.at[out_part], slots_p.at[pl.ds(sb + n_in, per - n_in)], sib)
     mixed_cotangent(FAR, 1)
     attention_back(1)
     for u in range(2):
@@ -545,6 +563,11 @@
         sides[1, BLK : 2 * BLK, halves[u]] = proj[
             half + u * BLK : half + (u + 1) * BLK, tail
         ].astype(BF16)
+    for s in (0, 1):
+        for name in ("a0", "b0", "a1", "b1"):
+            done = arrivals[name, s]
+            done.wait_send()
+            sends[:] = [copy for copy in sends if copy is not done]
     for n in range(8):
         cols = slice(n * 512, (n + 1) * 512)
         for c0, lhs in ((0, sides[0]), (4, sides[1, 0 : 2 * BLK, :])):
@@ -560,7 +583,10 @@
             slots_p.at[pl.ds(sb + 12 * n, 12)],
             sib,
         )
-    for n in (8, 0, 1, 2, 3, 4, 5, 6, 7):
+    for rel in (OWN, NXT, PRV, FAR):
+        for i in range(4):
+            got("swap", rel, i)
+    for n in range(8):
         got("swap", n)
     for copy in sends:
         copy.wait_send()
@@ -697,11 +723,10 @@
         copy.wait_send()
 
     start, n = starts[me], counts[me]
-    factor = 1.0 / np.sqrt(np.float32(LEN * 32))
     for t in range(SLOTS):
         b = start + t
         parity = lax.rem(b, 2)
-        v = tot[parity, b // 2 - (start + 1 - parity) // 2] * factor
+        v = tot[parity, b // 2 - (start + 1 - parity) // 2]
         v = jnp.where(b < NQKV, v.T, v)
         out[t] = jnp.where(t < n, v, 0.0)
 
@@ -742,8 +767,8 @@
             v((2, 2, 3) + block, BF16),
             v((2, 2, 3) + block, BF16),
             v((2, HALF) + block, F32),
-            pltpu.SemaphoreType.DMA((226,)),
-            pltpu.SemaphoreType.DMA((226,)),
+            pltpu.SemaphoreType.DMA((241,)),
+            pltpu.SemaphoreType.DMA((241,)),
             pltpu.SemaphoreType.DMA((7,)),
             pltpu.SemaphoreType.REGULAR,
         ],
@@ -767,7 +792,7 @@
         sin,
         curvature[0],
     )
-    return out[None]
+    return (out * (1.0 / np.sqrt(np.float32(LEN * 32))))[None]
 
 
 def solution(mesh):

time: 206 us -> 205 us (level)
  other arithmetic: 0 us -> 2.08 us
  local copies, waits for them, and re-layouts: 2.06 us -> 0 us
    broadcast_in_dim x0 -> x1, other arithmetic: none -> 2.08 us  [local(): return (out * (1.0 / np.sqrt(np.float32(LEN * 32))))[None]]
    unnamed x1 -> x0, local copies, waits for them, and re-layouts: 2.06 us -> none
where the time goes in v7:
time: 205 us
  Pallas kernels  203 us (99%)
  other arithmetic  2.08 us (1%)
    pallas_call x1, Pallas kernels, product(): pl.pallas_call(kernel, out_shape=jax.ShapeDtypeStruct((SLOTS,) + block, F...  203 us

profile of v7, /device:TPU:1, one launch (start us, length us, event | category | flops | bytes accessed | tf_op | source)
XLA Modules:
  0.0 205.1 jit_solution(17034852169869464962)
XLA Ops:
  0.0 203.0 %product.1 = f32[12,128,128]{2,1,0:T(8,128)} custom-call(s32[32]{0:T(128)} %bitcast.13, bf16[12,128,128]{2,1,0:T(8,128)(2,1)} %bitcast.10, bf16[12,128,128]{2,1,0:T(8,128)(2,1)} %bitcast.11, f32[1,4096]{1,0:T(1,128)} %bitcast.12, bf16[512,4096]{1,0:T(8,128)(2,1)} %bitcast.8, f32[512,128]{1,0:T(8,128)} %constant.6.clone.cos_in, ...), custom_call_target="tpu_custom_call" | custom-call | tf_op jit(solution)/shard_map/product/pallas_call | solution.py:740
  203.0 2.1 %multiply_bitcast_fusion = f32[1,12,128,128]{3,2,1,0:T(8,128)} fusion(f32[12,128,128]{2,1,0:T(8,128)} %product.1), kind=kLoop, calls=%fused_computation | loop fusion | flops 196608 | bytes 1572864 | tf_op jit(solution)/shard_map/broadcast_in_dim | solution.py:795

commit v8 on v7

--- a/solution.py
+++ b/solution.py
@@ -525,7 +525,7 @@
     tail = slice(OUT, QKV)
     proj[:, tail] = jnp.zeros((LEN, QKV - OUT), F32)
 
-    def attention_back(s):
+    def attention_back(s, begin, end, unroll):
         rows, seen = halves[s], slice(0, half * (s + 1))
 
         def one(h, carry):
@@ -547,47 +547,54 @@
             sides[0, cols_of(h), rows] = dq.T
             return carry
 
-        lax.fori_loop(0, QH, one, 0)
-
-    attention_back(0)
+        lax.fori_loop(begin, end, one, 0, unroll=unroll)
+
+    attention_back(0, 0, QH, 1)
     out_gradient(NXT)
     out_gradient(PRV)
     got("e1", 1)
     got("e0", 1)
     out_gradient(FAR)
     mixed_cotangent(FAR, 1)
-    attention_back(1)
+    for s in (0, 1):
+        for name in ("a0", "b0", "a1", "b1"):
+            done = arrivals[name, s]
+            done.wait_send()
+            sends[:] = [copy for copy in sends if copy is not done]
+
+    def in_gradient(pair, lhs):
+        for n in range(8):
+            g = nn(lhs, normed[:, n * 512 : (n + 1) * 512]).astype(BF16)
+            for r in range(4):
+                for c in range(2):
+                    slots_w[c * per + 32 * pair + 4 * n + r] = g[
+                        c * BLK : (c + 1) * BLK, r * BLK : (r + 1) * BLK
+                    ]
+            if n % 2 == 1:
+                b = 32 * pair + 8 * (n // 2)
+                cast(
+                    ("swap", pair, n // 2, 0),
+                    slots_w.at[pl.ds((1 - core) * per + b, 8)],
+                    slots_p.at[pl.ds(sb + b, 8)],
+                    sib,
+                )
+
+    for pair in (0, 1):
+        attention_back(1, 2 * pair, 2 * pair + 2, 2)
+        in_gradient(pair, sides[0, 2 * pair * BLK : 2 * (pair + 1) * BLK, :])
     for u in range(2):
         dk = proj[u * BLK : (u + 1) * BLK, tail].astype(BF16).astype(F32).T
         sides[1, 0:BLK, halves[u]] = unrot(dk, halves[u]).astype(BF16).T
         sides[1, BLK : 2 * BLK, halves[u]] = proj[
             half + u * BLK : half + (u + 1) * BLK, tail
         ].astype(BF16)
-    for s in (0, 1):
-        for name in ("a0", "b0", "a1", "b1"):
-            done = arrivals[name, s]
-            done.wait_send()
-            sends[:] = [copy for copy in sends if copy is not done]
-    for n in range(8):
-        cols = slice(n * 512, (n + 1) * 512)
-        for c0, lhs in ((0, sides[0]), (4, sides[1, 0 : 2 * BLK, :])):
-            g = nn(lhs, normed[:, cols]).astype(BF16)
-            for r in range(4):
-                for c in range(lhs.shape[0] // BLK):
-                    slots_w[((c0 + c) % 2) * per + 3 * (4 * n + r) + (c0 + c) // 2] = g[
-                        c * BLK : (c + 1) * BLK, r * BLK : (r + 1) * BLK
-                    ]
-        cast(
-            ("swap", n),
-            slots_w.at[pl.ds((1 - core) * per + 12 * n, 12)],
-            slots_p.at[pl.ds(sb + 12 * n, 12)],
-            sib,
-        )
+    in_gradient(2, sides[1, 0 : 2 * BLK, :])
     for rel in (OWN, NXT, PRV, FAR):
         for i in range(4):
             got("swap", rel, i)
-    for n in range(8):
-        got("swap", n)
+    for pair in range(3):
+        for n in range(4):
+            got("swap", pair, n, 0)
     for copy in sends:
         copy.wait_send()
     sends.clear()
@@ -610,6 +617,7 @@
             base = (starts[d] + 1 - core) // 2
             for i in range(HALF):
                 j = jnp.minimum(base + i, per - 1)
+                j = jnp.where(j < n_in, 32 * lax.rem(j, 3) + lax.div(j, 3), j)
                 slots_p[acc_at(part, rel, i // 3) + 3 * srel + i % 3] = (
                     slots_w[core * per + j].astype(F32) + slots_p[sb + j].astype(F32)
                 ).astype(BF16)
@@ -767,8 +775,8 @@
             v((2, 2, 3) + block, BF16),
             v((2, 2, 3) + block, BF16),
             v((2, HALF) + block, F32),
-            pltpu.SemaphoreType.DMA((241,)),
-            pltpu.SemaphoreType.DMA((241,)),
+            pltpu.SemaphoreType.DMA((245,)),
+            pltpu.SemaphoreType.DMA((245,)),
             pltpu.SemaphoreType.DMA((7,)),
             pltpu.SemaphoreType.REGULAR,
         ],

time: 205 us -> 205 us (level)
  no operation moved by 1% of the time
where the time goes in v8:
time: 205 us
  Pallas kernels  203 us (99%)
  other arithmetic  2.08 us (1%)
    pallas_call x1, Pallas kernels, product(): pl.pallas_call(kernel, out_shape=jax.ShapeDtypeStruct((SLOTS,) + block, F...  203 us

profile of v8, /device:TPU:1, one launch (start us, length us, event | category | flops | bytes accessed | tf_op | source)
XLA Modules:
  0.0 204.7 jit_solution(15430090577653914298)
XLA Ops:
  0.0 202.6 %product.1 = f32[12,128,128]{2,1,0:T(8,128)} custom-call(s32[32]{0:T(128)} %bitcast.13, bf16[12,128,128]{2,1,0:T(8,128)(2,1)} %bitcast.10, bf16[12,128,128]{2,1,0:T(8,128)(2,1)} %bitcast.11, f32[1,4096]{1,0:T(1,128)} %bitcast.12, bf16[512,4096]{1,0:T(8,128)(2,1)} %bitcast.8, f32[512,128]{1,0:T(8,128)} %constant.6.clone.cos_in, ...), custom_call_target="tpu_custom_call" | custom-call | tf_op jit(solution)/shard_map/product/pallas_call | solution.py:748
  202.6 2.1 %multiply_bitcast_fusion = f32[1,12,128,128]{3,2,1,0:T(8,128)} fusion(f32[12,128,128]{2,1,0:T(8,128)} %product.1), kind=kLoop, calls=%fused_computation | loop fusion | flops 196608 | bytes 1572864 | tf_op jit(solution)/shard_map/broadcast_in_dim | solution.py:803

commit v9 on v8

--- a/solution.py
+++ b/solution.py
@@ -366,7 +366,7 @@
             ).astype(BF16)
             return carry
 
-        lax.fori_loop(0, QH, one, 0)
+        lax.fori_loop(0, QH, one, 0, unroll=2 - s)
 
     def term_at(rel, s, part):
         return (0, 32, 64, 160)[rel] + (s * 2 + part) * 8

time: 205 us -> 205 us (level)
  no operation moved by 1% of the time
where the time goes in v9:
time: 205 us; the launch traced here: 204 us
  Pallas kernels  202 us (99%)
  other arithmetic  2.08 us (1%)
    pallas_call x1, Pallas kernels, product(): pl.pallas_call(kernel, out_shape=jax.ShapeDtypeStruct((SLOTS,) + block, F...  202 us

profile of v9, /device:TPU:1, one launch (start us, length us, event | category | flops | bytes accessed | tf_op | source)
XLA Modules:
  0.0 204.3 jit_solution(4774715968780616875)
XLA Ops:
  0.0 202.2 %product.1 = f32[12,128,128]{2,1,0:T(8,128)} custom-call(s32[32]{0:T(128)} %bitcast.13, bf16[12,128,128]{2,1,0:T(8,128)(2,1)} %bitcast.10, bf16[12,128,128]{2,1,0:T(8,128)(2,1)} %bitcast.11, f32[1,4096]{1,0:T(1,128)} %bitcast.12, bf16[512,4096]{1,0:T(8,128)(2,1)} %bitcast.8, f32[512,128]{1,0:T(8,128)} %constant.6.clone.cos_in, ...), custom_call_target="tpu_custom_call" | custom-call | tf_op jit(solution)/shard_map/product/pallas_call | solution.py:748
  202.2 2.1 %multiply_bitcast_fusion = f32[1,12,128,128]{3,2,1,0:T(8,128)} fusion(f32[12,128,128]{2,1,0:T(8,128)} %product.1), kind=kLoop, calls=%fused_computation | loop fusion | flops 196608 | bytes 1572864 | tf_op jit(solution)/shard_map/broadcast_in_dim | solution.py:803
